TPU v7x, 128 devices: a whole 4x4x4 slice. The times are simulated.
128 devices in a mesh: row: 8 (over x, y_hi), col: 16 (over y_lo, z, core).
Axes of the slice: x: 4, y: 4 (y_hi: 2, y_lo: 2; y = y_hi * 2 + y_lo), z: 4, core: 2. Of those that a mesh axis runs over, the one named last changes fastest.
Arguments:
- frame: bfloat16 [256, 512, 256], P('row', 'col'), may hold values from -6 to 6
- gain_attn: float32 [2, 256], replicated, may hold values from 0.1 to 1.9
- w_qkv: bfloat16 [2, 256, 768], replicated, may hold values from -2 to 2
- w_out: bfloat16 [2, 256, 256], replicated, may hold values from -1 to 1
- gain_mlp: float32 [2, 256], replicated, may hold values from 0.1 to 1.9
- w_up: bfloat16 [2, 256, 1024], replicated, may hold values from -0.375 to 0.375
- w_down: bfloat16 [2, 1024, 256], replicated, may hold values from -0.1875 to 0.1875
Outputs:
- result: bfloat16 [256, 512, 256], P('row', 'col')
All inputs are finite; a program needn't handle non-finite values.
Results may differ from a plain program's by a relative error of at most 0.014.
The roundings to bfloat16 on the way count: a program that leaves them out, or rounds other values in their place, can miss the bound.
Values may be sent and summed in bfloat16 or wider, within the bound.
No kernel may reach another device: no remote copies, remote signals or barrier semaphores. Data moves between devices by JAX's collectives and lax.ppermute only.
A program may use at most 128 MiB of HBM per device.

v0:
```python
import jax
import jax.numpy as jnp
from jax import lax
from jax.experimental import pallas as pl
from jax.experimental.pallas import tpu as pltpu
from jax.sharding import PartitionSpec as P

D = 256
HEADS = 8
LAYERS = 2
EPS = 1e-05
HD = 32
SCALE = 32 ** -0.5 * 1.4426950408889634
BF = jnp.bfloat16
F32 = jnp.float32


def attend_item(get, n, put, kx, vx, sbuf, kb, qn):
    nk = n * 256
    ones = jnp.ones((16, 256), BF)
    def prep(s, c):
        kt = get(s, 32, 64)
        kk = jnp.concatenate([kt, kt], axis=0).astype(F32).T.astype(BF)
        kx[pl.ds(s * 256, 256), 0:64] = kk
        vx[:, pl.ds(s * 256, 256)] = jnp.concatenate([get(s, 64, 96), ones], axis=0)
        return c
    for s in range(n): prep(s, 0)
    chunks = nk // kb
    W = 256 * qn
    def qblock(i, c):
        qs = []
        for j in range(qn):
            q = get(i * qn + j, 0, 32).astype(F32) * SCALE
            hi = q.astype(BF)
            lo = (q - hi.astype(F32)).astype(BF)
            qs.append(jnp.concatenate([hi, lo], axis=0))
        qt = jnp.concatenate(qs, axis=1) if qn > 1 else qs[0]
        def scores(j, slot):
            sbuf[slot] = jnp.dot(kx[j * kb:(j + 1) * kb, 0:64], qt, preferred_element_type=F32)
        scores(0, 0)
        m = jnp.full((8, W), -jnp.inf, F32)
        o = jnp.zeros((48, W), F32)
        for j in range(chunks):
            if j + 1 < chunks: scores(j + 1, (j + 1) % 2)
            s = sbuf[j % 2]
            mb = jnp.max(s.reshape(kb // 8, 8, W), axis=0)
            mb = jnp.max(mb, axis=0, keepdims=True)
            mn = jnp.maximum(m, mb)
            alpha = jnp.exp2(m - mn)
            p = jnp.exp2(s.reshape(kb // 8, 8, W) - mn[None]).reshape(kb, W).astype(BF)
            pv = jnp.dot(vx[:, j * kb:(j + 1) * kb], p, preferred_element_type=F32)
            o = (o.reshape(6, 8, W) * alpha[None]).reshape(48, W) + pv if j else pv
            m = mn
        r = o[0:32] / o[32:33]
        for j in range(qn):
            put(i * qn + j, r[:, j * 256:(j + 1) * 256].astype(BF))
        return c
    lax.fori_loop(0, n // qn, qblock, 0)

def h_kernel(a_ref, o_ref, kx, vx, sbuf, *, kb, qn):
    n = a_ref.shape[0]
    def put(s, v): o_ref[s] = v
    attend_item(lambda s, lo, hi: a_ref[s, lo:hi, :], n, put, kx, vx, sbuf, kb, qn)

def v_kernel(a_ref, o_ref, kx, vx, sbuf, *, kb, qn):
    n = a_ref.shape[0]
    for it in range(a_ref.shape[1]):
        def put(s, v): o_ref[s, it] = v
        attend_item(lambda s, lo, hi: a_ref[s, it, lo:hi, :], n, put, kx, vx, sbuf, kb, qn)

def attn_h(a, kb=256, qn=4):
    n = a.shape[0]
    return pl.pallas_call(lambda *r: h_kernel(*r, kb=kb, qn=qn), out_shape=jax.ShapeDtypeStruct((n, 32, 256), BF),
        in_specs=[pl.BlockSpec(memory_space=pltpu.VMEM)], out_specs=pl.BlockSpec(memory_space=pltpu.VMEM),
        scratch_shapes=[pltpu.VMEM((n*256,128),BF), pltpu.VMEM((48,n*256),BF), pltpu.VMEM((2,kb,256*qn),F32)],
        cost_estimate=pl.CostEstimate(flops=4*(n*256)**2*256,transcendentals=(n*256)**2,bytes_accessed=2*n*128*256),
        name="attn_h")(a)
def attn_v(a, kb=256, qn=4):
    n = a.shape[0]
    return pl.pallas_call(lambda *r: v_kernel(*r, kb=kb, qn=qn), out_shape=jax.ShapeDtypeStruct((n, 2, 32, 256), BF),
        in_specs=[pl.BlockSpec(memory_space=pltpu.VMEM)], out_specs=pl.BlockSpec(memory_space=pltpu.VMEM),
        scratch_shapes=[pltpu.VMEM((n*256,128),BF), pltpu.VMEM((48,n*256),BF), pltpu.VMEM((2,kb,256*qn),F32)],
        cost_estimate=pl.CostEstimate(flops=8*(n*256)**2*256,transcendentals=2*(n*256)**2,bytes_accessed=4*n*128*256),
        name="attn_v")(a)


def norm(x, gain):
    center = x - jnp.mean(x, axis=-1, keepdims=True)
    spread = jnp.mean(center * center, axis=-1, keepdims=True)
    return center * lax.rsqrt(spread + EPS) * gain


def project(get, gain, wt_ref, c_ref, r_ref, nrm):
    for b in range(4):
        n = norm(get(b), gain)
        nrm[pl.ds(8 * b, 8)] = n.reshape(8, 4, 8, D)
        out = lax.dot_general(wt_ref[0:384, :], n.astype(BF), (((1,), (1,)), ((), ())), preferred_element_type=F32)
        c_ref[4 * b:4 * b + 4] = out.astype(BF).reshape(4, 96, 256)
    for cb in range(4):
        n = nrm[:, cb].reshape(256, D).astype(BF)
        out = lax.dot_general(wt_ref[384:768, :], n, (((1,), (1,)), ((), ())), preferred_element_type=F32)
        r_ref[2 * cb:2 * cb + 2] = out.astype(BF).reshape(2, 2, 96, 256)


def first_kernel(x_ref, gain_ref, wt_ref, c_ref, r_ref, nrm):
    project(lambda b: x_ref[8 * b:8 * b + 8].reshape(256, D).astype(F32), gain_ref[...], wt_ref, c_ref, r_ref, nrm)


def finish(x_ref, hc_ref, hv_ref, wo_ref, gain_ref, wu_ref, wd_ref, mix, put):
    tdot = lambda a, b: lax.dot_general(a, b, (((0,), (0,)), ((), ())), preferred_element_type=F32)
    for cb in range(4):
        h = hv_ref[4 * cb:4 * cb + 4].reshape(128, 256)
        mix[:, cb] = tdot(h, wo_ref[128:256, :]).reshape(32, 8, D)
    for b in range(4):
        h = hc_ref[4 * b:4 * b + 4].reshape(128, 256)
        mixed = tdot(h, wo_ref[0:128, :]) + mix[pl.ds(8 * b, 8)].reshape(256, D)
        mixed = mixed + x_ref[8 * b:8 * b + 8].reshape(256, D).astype(F32)
        n2 = norm(mixed, gain_ref[...]).astype(BF)
        up = jnp.dot(n2, wu_ref[...], preferred_element_type=F32)
        act = 0.5 * up * (1.0 + jnp.tanh(0.7978845608028654 * (up + 0.044715 * (up * up * up))))
        out = mixed + jnp.dot(act.astype(BF), wd_ref[...], preferred_element_type=F32)
        put(b, out.astype(BF))


def mid_kernel(x_ref, hc_ref, hv_ref, wo_ref, gm_ref, wu_ref, wd_ref, ga_ref, wt_ref, y_ref, c_ref, r_ref, mix, nrm):
    def put(b, v):
        y_ref[8 * b:8 * b + 8] = v.reshape(8, 32, D)

    finish(x_ref, hc_ref, hv_ref, wo_ref, gm_ref, wu_ref, wd_ref, mix, put)
    project(lambda b: y_ref[8 * b:8 * b + 8].reshape(256, D).astype(F32), ga_ref[...], wt_ref, c_ref, r_ref, nrm)


def last_kernel(x_ref, hc_ref, hv_ref, wo_ref, gm_ref, wu_ref, wd_ref, y_ref, mix):
    def put(b, v):
        y_ref[8 * b:8 * b + 8] = v.reshape(8, 32, D)

    finish(x_ref, hc_ref, hv_ref, wo_ref, gm_ref, wu_ref, wd_ref, mix, put)


VM = pl.BlockSpec(memory_space=pltpu.VMEM)
SENDS = (jax.ShapeDtypeStruct((16, 96, 256), BF), jax.ShapeDtypeStruct((8, 2, 96, 256), BF))
STATE = jax.ShapeDtypeStruct((32, 32, D), BF)
GRID4 = pltpu.VMEM((32, 4, 8, D), F32)


def call(kernel, name, outs, scratch, flops, *args):
    return pl.pallas_call(
        kernel, out_shape=outs, in_specs=[VM] * len(args), out_specs=jax.tree.map(lambda _: VM, outs),
        scratch_shapes=scratch, name=name,
        cost_estimate=pl.CostEstimate(flops=flops, transcendentals=0, bytes_accessed=1 << 20),
    )(*args)


def shards(frame, gain_attn, w_qkv, w_out, gain_mlp, w_up, w_down):
    wt = w_qkv.reshape(LAYERS, D, 3, HEADS, HD).transpose(0, 3, 2, 4, 1).reshape(LAYERS, 3 * D, D)
    ga = gain_attn.reshape(LAYERS, 1, D)
    gm = gain_mlp.reshape(LAYERS, 1, D)
    state = frame
    c, r = call(first_kernel, "first", SENDS, [GRID4], 4 << 30, state, ga[0], wt[0])
    for layer in range(LAYERS):
        c = lax.all_to_all(c, "col", 0, 0, tiled=True)
        r = lax.all_to_all(r, "row", 0, 0, tiled=True)
        hc = lax.all_to_all(attn_h(c), "col", 0, 0, tiled=True)
        hv = lax.all_to_all(attn_v(r), "row", 0, 0, tiled=True).reshape(16, 32, 256)
        rest = (state, hc, hv, w_out[layer], gm[layer], w_up[layer], w_down[layer])
        if layer + 1 < LAYERS:
            state, c, r = call(mid_kernel, "mid", (STATE,) + SENDS, [GRID4, GRID4], 8 << 30, *rest, ga[layer + 1], wt[layer + 1])
        else:
            state = call(last_kernel, "last", STATE, [GRID4], 4 << 30, *rest)
    return state


def solution(mesh):
    placed = (P("row", "col", None), P(), P(), P(), P(), P(), P())
    return jax.shard_map(
        shards, mesh=mesh, in_specs=placed, out_specs=P("row", "col", None), check_vma=False
    )
```

profile of v0, /device:TPU:1, one launch (start us, length us, event | category | flops | bytes accessed | tf_op | source)
XLA Modules:
  0.0 170.3 jit_solution(14878843026519391565)
XLA Ops:
  0.0 1.4 fusion.2
  1.4 1.4 copy.9
  2.8 0.1 fusion
  2.8 0.8 copy.10
  3.6 3.1 %first.1 = (bf16[16,96,256]{2,1,0:T(8,128)(2,1)}, bf16[8,2,96,256]{3,2,1,0:T(8,128)(2,1)}) custom-call(bf16[32,32,256]{2,1,0:T(8,128)(2,1)} %x_ref.3, f32[1,256]{1,0:T(1,128)} %get-tuple-element.26.gain_ref, bf16[768,256]{1,0:T(8,128)(2,1)} %bitcast.21), custom_call_target="tpu_custom_call" | custom-call | flops 4294967296 | bytes 1048576 | tf_op jit(solution)/shard_map/first/pallas_call | solution.py:147
  6.7 0.0 copy-start
  6.7 7.6 %all-to-all-start.2 = ((bf16[8,2,96,256]{3,2,1,0:T(8,128)(2,1)}), bf16[8,2,96,256]{3,2,1,0:T(8,128)(2,1)S(1)}, u32[]{:S(2)}, u32[]{:S(2)}) async-start(bf16[8,2,96,256]{3,2,1,0:T(8,128)(2,1)} %get-tuple-element.11), calls=%async_computation.2 | async-start | bytes 1572864 | tf_op jit(solution)/shard_map/all_to_all | solution.py:162
  14.3 0.0 copy-done
  14.3 0.0 copy-start.1
  14.3 1.0 slice_bitcast_fusion.1
  15.4 0.6 copy-done.1
  15.9 1.1 slice_bitcast_fusion
  17.0 10.4 %all-to-all-done.2.r_0_ = bf16[8,2,96,256]{3,2,1,0:T(8,128)(2,1)S(1)} async-done(((bf16[8,2,96,256]{3,2,1,0:T(8,128)(2,1)}), bf16[8,2,96,256]{3,2,1,0:T(8,128)(2,1)S(1)}, u32[]{:S(2)}, u32[]{:S(2)}) %all-to-all-start.2) | async-done | bytes 786464 | tf_op jit(solution)/shard_map/all_to_all | solution.py:162
  27.4 0.0 copy-start.2
  27.4 0.9 copy-done.2
  28.4 6.6 %all-to-all-start = ((bf16[16,96,256]{2,1,0:T(8,128)(2,1)}), bf16[16,96,256]{2,1,0:T(8,128)(2,1)S(1)}, u32[]{:S(2)}, u32[]{:S(2)}) async-start(bf16[16,96,256]{2,1,0:T(8,128)(2,1)} %get-tuple-element.10), calls=%async_computation | async-start | bytes 1572864 | tf_op jit(solution)/shard_map/all_to_all | solution.py:161
  35.0 10.7 %attn_v.2 = bf16[8,2,32,256]{3,2,1,0:T(8,128)(2,1)} custom-call(bf16[8,2,96,256]{3,2,1,0:T(8,128)(2,1)} %copy-done.2), custom_call_target="tpu_custom_call" | custom-call | flops 8589934592 | bytes 1048576 | tf_op jit(solution)/shard_map/attn_v/pallas_call | solution.py:80
  45.7 1.8 %all-to-all-done.r_0_ = bf16[16,96,256]{2,1,0:T(8,128)(2,1)S(1)} async-done(((bf16[16,96,256]{2,1,0:T(8,128)(2,1)}), bf16[16,96,256]{2,1,0:T(8,128)(2,1)S(1)}, u32[]{:S(2)}, u32[]{:S(2)}) %all-to-all-start) | async-done | bytes 786464 | tf_op jit(solution)/shard_map/all_to_all | solution.py:161
  47.5 0.0 copy-start.3
  47.5 4.2 %all-to-all-start.3 = ((bf16[8,2,32,256]{3,2,1,0:T(8,128)(2,1)}), bf16[8,2,32,256]{3,2,1,0:T(8,128)(2,1)S(1)}, u32[]{:S(2)}, u32[]{:S(2)}) async-start(bf16[8,2,32,256]{3,2,1,0:T(8,128)(2,1)} %attn_v.2), calls=%async_computation.3 | async-start | bytes 524288 | tf_op jit(solution)/shard_map/all_to_all | solution.py:164
  51.7 0.0 copy-done.3
  51.7 19.6 %attn_h.2 = bf16[16,32,256]{2,1,0:T(8,128)(2,1)} custom-call(bf16[16,96,256]{2,1,0:T(8,128)(2,1)} %copy-done.3), custom_call_target="tpu_custom_call" | custom-call | flops 17179869184 | bytes 1048576 | tf_op jit(solution)/shard_map/attn_h/pallas_call | solution.py:73
  71.3 0.0 copy-start.9
  71.3 0.0 all-to-all-done.3
  71.3 0.0 copy-start.6
  71.3 0.7 copy-done.6
  72.0 4.9 %all-to-all-start.1 = ((bf16[16,32,256]{2,1,0:T(8,128)(2,1)}), bf16[16,32,256]{2,1,0:T(8,128)(2,1)S(1)}, u32[]{:S(2)}, u32[]{:S(2)}) async-start(bf16[16,32,256]{2,1,0:T(8,128)(2,1)} %attn_h.2), calls=%async_computation.1 | async-start | bytes 524288 | tf_op jit(solution)/shard_map/all_to_all | solution.py:163
  76.9 0.0 copy-done.9
  76.9 0.6 fusion.1
  77.5 0.0 copy-start.5
  77.5 0.8 copy.11
  78.3 0.2 copy-done.5
  78.5 0.7 slice_bitcast_fusion.4
  79.2 4.9 %all-to-all-done.1.hc_ref = bf16[16,32,256]{2,1,0:T(8,128)(2,1)S(1)} async-done(((bf16[16,32,256]{2,1,0:T(8,128)(2,1)}), bf16[16,32,256]{2,1,0:T(8,128)(2,1)S(1)}, u32[]{:S(2)}, u32[]{:S(2)}) %all-to-all-start.1) | async-done | bytes 262176 | tf_op jit(solution)/shard_map/all_to_all | solution.py:163
  84.1 0.0 copy-start.7
  84.1 0.7 copy-done.7
  84.8 6.3 %mid.1 = (bf16[32,32,256]{2,1,0:T(8,128)(2,1)}, bf16[16,96,256]{2,1,0:T(8,128)(2,1)}, bf16[8,2,96,256]{3,2,1,0:T(8,128)(2,1)}) custom-call(bf16[32,32,256]{2,1,0:T(8,128)(2,1)} %x_ref.3, bf16[16,32,256]{2,1,0:T(8,128)(2,1)} %copy-done.7, bf16[16,32,256]{2,1,0:T(8,128)(2,1)} %bitcast.22, bf16[256,256]{1,0:T(8,128)(2,1)} %get-tuple-element.22.wo_ref, ...), custom_call_target="tpu_custom_call" | custom-call | flops 8589934592 | bytes 1048576 | tf_op jit(solution)/shard_map/mid/pallas_call | solution.py:147
  91.1 19.6 %all_to_all.40.r_0_ = bf16[8,2,96,256]{3,2,1,0:T(8,128)(2,1)} all-to-all(bf16[8,2,96,256]{3,2,1,0:T(8,128)(2,1)} %get-tuple-element.14), channel_id=1, replica_groups=mesh['row'=8,'col'=16] {'row'}, dimensions={0} | all-to-all | bytes 1572864 | tf_op jit(solution)/shard_map/all_to_all | solution.py:162
  110.7 5.8 %all-to-all-start.4 = ((bf16[16,96,256]{2,1,0:T(8,128)(2,1)}), bf16[16,96,256]{2,1,0:T(8,128)(2,1)S(1)}, u32[]{:S(2)}, u32[]{:S(2)}) async-start(bf16[16,96,256]{2,1,0:T(8,128)(2,1)} %get-tuple-element.13), calls=%async_computation.4 | async-start | bytes 1572864 | tf_op jit(solution)/shard_map/all_to_all | solution.py:161
  116.5 10.7 %attn_v.3 = bf16[8,2,32,256]{3,2,1,0:T(8,128)(2,1)} custom-call(bf16[8,2,96,256]{3,2,1,0:T(8,128)(2,1)} %all_to_all.40.r_0_), custom_call_target="tpu_custom_call" | custom-call | flops 8589934592 | bytes 1048576 | tf_op jit(solution)/shard_map/attn_v/pallas_call | solution.py:80
  127.3 1.9 %all-to-all-done.4.r_0_ = bf16[16,96,256]{2,1,0:T(8,128)(2,1)S(1)} async-done(((bf16[16,96,256]{2,1,0:T(8,128)(2,1)}), bf16[16,96,256]{2,1,0:T(8,128)(2,1)S(1)}, u32[]{:S(2)}, u32[]{:S(2)}) %all-to-all-start.4) | async-done | bytes 786464 | tf_op jit(solution)/shard_map/all_to_all | solution.py:161
  129.2 3.6 %all-to-all-start.7 = ((bf16[8,2,32,256]{3,2,1,0:T(8,128)(2,1)}), bf16[8,2,32,256]{3,2,1,0:T(8,128)(2,1)S(1)}, u32[]{:S(2)}, u32[]{:S(2)}) async-start(bf16[8,2,32,256]{3,2,1,0:T(8,128)(2,1)} %attn_v.3), calls=%async_computation.7 | async-start | bytes 524288 | tf_op jit(solution)/shard_map/all_to_all | solution.py:164
  132.8 0.0 copy-done.4
  132.8 19.6 %attn_h.3 = bf16[16,32,256]{2,1,0:T(8,128)(2,1)} custom-call(bf16[16,96,256]{2,1,0:T(8,128)(2,1)} %copy-done.4), custom_call_target="tpu_custom_call" | custom-call | flops 17179869184 | bytes 1048576 | tf_op jit(solution)/shard_map/attn_h/pallas_call | solution.py:73
  152.4 0.0 all-to-all-done.7
  152.4 12.5 %all_to_all.41.hc_ref = bf16[16,32,256]{2,1,0:T(8,128)(2,1)} all-to-all(bf16[16,32,256]{2,1,0:T(8,128)(2,1)} %attn_h.3), channel_id=1, replica_groups=mesh['row'=8,'col'=16] {'col'}, dimensions={0} | all-to-all | bytes 524288 | tf_op jit(solution)/shard_map/all_to_all | solution.py:163
  164.9 0.0 copy-done.8
  164.9 5.3 %last.1 = bf16[32,32,256]{2,1,0:T(8,128)(2,1)} custom-call(bf16[32,32,256]{2,1,0:T(8,128)(2,1)} %get-tuple-element.12.x_ref, bf16[16,32,256]{2,1,0:T(8,128)(2,1)} %all_to_all.41.hc_ref, bf16[16,32,256]{2,1,0:T(8,128)(2,1)} %bitcast.23, bf16[256,256]{1,0:T(8,128)(2,1)} %get-tuple-element.21.wo_ref, f32[1,256]{1,0:T(1,128)} %get-tuple-element.23.gm_ref, ...), custom_call_target="tpu_custom_call" | custom-call | flops 4294967296 | bytes 1048576 | tf_op jit(solution)/shard_map/last/pallas_call | solution.py:147
  (2 shorter events, 0.0 us)
Async XLA Ops:
  6.7 7.6 %copy-start = (bf16[2,256,1024]{2,1,0:T(8,128)(2,1)S(1)}, bf16[2,256,1024]{2,1,0:T(8,128)(2,1)}, u32[]{:S(2)}) copy-start(bf16[2,256,1024]{2,1,0:T(8,128)(2,1)} %param.12) | copy-start | bytes 3145732
  6.7 20.7 %all-to-all-start.2 = ((bf16[8,2,96,256]{3,2,1,0:T(8,128)(2,1)}), bf16[8,2,96,256]{3,2,1,0:T(8,128)(2,1)S(1)}, u32[]{:S(2)}, u32[]{:S(2)}) async-start(bf16[8,2,96,256]{3,2,1,0:T(8,128)(2,1)} %get-tuple-element.11), calls=%async_computation.2 | async-start | bytes 1572864 | tf_op jit(solution)/shard_map/all_to_all | solution.py:162
  14.3 1.6 copy-start.1
  27.4 0.9 copy-start.2
  28.4 19.2 %all-to-all-start = ((bf16[16,96,256]{2,1,0:T(8,128)(2,1)}), bf16[16,96,256]{2,1,0:T(8,128)(2,1)S(1)}, u32[]{:S(2)}, u32[]{:S(2)}) async-start(bf16[16,96,256]{2,1,0:T(8,128)(2,1)} %get-tuple-element.10), calls=%async_computation | async-start | bytes 1572864 | tf_op jit(solution)/shard_map/all_to_all | solution.py:161
  47.5 4.2 %copy-start.3 = (bf16[16,96,256]{2,1,0:T(8,128)(2,1)}, bf16[16,96,256]{2,1,0:T(8,128)(2,1)S(1)}, u32[]{:S(2)}) copy-start(bf16[16,96,256]{2,1,0:T(8,128)(2,1)S(1)} %all-to-all-done.r_0_) | copy-start | bytes 2359300
  47.5 23.8 %all-to-all-start.3 = ((bf16[8,2,32,256]{3,2,1,0:T(8,128)(2,1)}), bf16[8,2,32,256]{3,2,1,0:T(8,128)(2,1)S(1)}, u32[]{:S(2)}, u32[]{:S(2)}) async-start(bf16[8,2,32,256]{3,2,1,0:T(8,128)(2,1)} %attn_v.2), calls=%async_computation.3 | async-start | bytes 524288 | tf_op jit(solution)/shard_map/all_to_all | solution.py:164
  71.3 5.6 %copy-start.9 = (f32[2,256]{1,0:T(2,128)S(1)}, f32[2,256]{1,0:T(2,128)}, u32[]{:S(2)}) copy-start(f32[2,256]{1,0:T(2,128)} %param.11) | copy-start | bytes 6148
  71.3 0.7 copy-start.6
  72.0 12.1 %all-to-all-start.1 = ((bf16[16,32,256]{2,1,0:T(8,128)(2,1)}), bf16[16,32,256]{2,1,0:T(8,128)(2,1)S(1)}, u32[]{:S(2)}, u32[]{:S(2)}) async-start(bf16[16,32,256]{2,1,0:T(8,128)(2,1)} %attn_h.2), calls=%async_computation.1 | async-start | bytes 524288 | tf_op jit(solution)/shard_map/all_to_all | solution.py:163
  77.5 1.0 copy-start.5
  84.1 0.7 copy-start.7
  110.7 18.5 %all-to-all-start.4 = ((bf16[16,96,256]{2,1,0:T(8,128)(2,1)}), bf16[16,96,256]{2,1,0:T(8,128)(2,1)S(1)}, u32[]{:S(2)}, u32[]{:S(2)}) async-start(bf16[16,96,256]{2,1,0:T(8,128)(2,1)} %get-tuple-element.13), calls=%async_computation.4 | async-start | bytes 1572864 | tf_op jit(solution)/shard_map/all_to_all | solution.py:161
  129.2 3.6 %copy-start.4 = (bf16[16,96,256]{2,1,0:T(8,128)(2,1)}, bf16[16,96,256]{2,1,0:T(8,128)(2,1)S(1)}, u32[]{:S(2)}) copy-start(bf16[16,96,256]{2,1,0:T(8,128)(2,1)S(1)} %all-to-all-done.4.r_0_) | copy-start | bytes 2359300
  129.2 23.2 %all-to-all-start.7 = ((bf16[8,2,32,256]{3,2,1,0:T(8,128)(2,1)}), bf16[8,2,32,256]{3,2,1,0:T(8,128)(2,1)S(1)}, u32[]{:S(2)}, u32[]{:S(2)}) async-start(bf16[8,2,32,256]{3,2,1,0:T(8,128)(2,1)} %attn_v.3), calls=%async_computation.7 | async-start | bytes 524288 | tf_op jit(solution)/shard_map/all_to_all | solution.py:164
  152.4 12.5 %copy-start.8 = (bf16[8,2,32,256]{3,2,1,0:T(8,128)(2,1)}, bf16[8,2,32,256]{3,2,1,0:T(8,128)(2,1)S(1)}, u32[]{:S(2)}) copy-start(bf16[8,2,32,256]{3,2,1,0:T(8,128)(2,1)S(1)} %all-to-all-done.7) | copy-start | bytes 786436
where the time goes:
time: 172 us; the launch traced here: 170 us
  Pallas kernels  75.3 us (44%)
  starting transfers between devices  32.7 us (19%)
  blocking collectives  32.1 us (19%)
  waiting for transfers between devices  19.1 us (11%)
  local copies, waits for them, and re-layouts  11 us (6%)
    pallas_call x2, Pallas kernels, attn_h(): pl.pallas_call(lambda *r: h_kernel(*r, kb=kb, qn=qn), out_shape=jax.Shape...  39.2 us
    pallas_call x2, Pallas kernels, attn_v(): pl.pallas_call(lambda *r: v_kernel(*r, kb=kb, qn=qn), out_shape=jax.Shape...  21.5 us
    all_to_all x1, blocking collectives, shards(): r = lax.all_to_all(r, 'row', 0, 0, tiled=True)  19.6 us
    pallas_call x3, Pallas kernels, call(): pl.pallas_call(kernel, out_shape=outs, in_specs=[VM] * len(args), out_spe...  14.7 us
    all_to_all x1, blocking collectives, shards(): hc = lax.all_to_all(attn_h(c), 'col', 0, 0, tiled=True)  12.5 us
    all_to_all x2, starting transfers between devices, shards(): c = lax.all_to_all(c, 'col', 0, 0, tiled=True)  12.4 us
    all_to_all x1, waiting for transfers between devices, shards(): r = lax.all_to_all(r, 'row', 0, 0, tiled=True)  10.4 us
    all_to_all x2, starting transfers between devices, shards(): hv = lax.all_to_all(attn_v(r), 'row', 0, 0, tiled=True).reshape(16, 32, 256)  7.81 us
  transfers between devices with their start and end apart: 6, of which 4 were waited for; matrix products, arithmetic and copies ran while one was open for 2% of the time, Pallas kernels for 36%

commit v1 on v0

v1 whole, which is shorter than its diff:
```python
import jax
import jax.numpy as jnp
from jax import lax
from jax.experimental import pallas as pl
from jax.experimental.pallas import tpu as pltpu
from jax.sharding import PartitionSpec as P

D = 256
LAYERS = 2
EPS = 1e-05
SCALE = 32 ** -0.5 * 1.4426950408889634
BF = jnp.bfloat16
F32 = jnp.float32


GAP = 90.0


def prepare(get, n, kx, vx, qx):
    nk = n * 256
    ones = jnp.ones((16, 256), BF)
    ksum = jnp.zeros((32, 256), F32)
    for s in range(n):
        kt = get(s, 32, 64)
        ksum = ksum + kt.astype(F32)
        kx[pl.ds(s * 256, 256), 0:80] = jnp.concatenate([kt, kt, ones], axis=0).T
        vx[0:32, pl.ds(s * 256, 256)] = get(s, 64, 96)
    vx[32:48, :] = jnp.ones((16, nk), BF)
    kmean = jnp.sum(ksum, axis=1, keepdims=True) * (1.0 / nk)
    far = jnp.zeros((1, 256), F32)
    for s in range(n):
        dev = get(s, 32, 64).astype(F32) - kmean
        far = jnp.maximum(far, jnp.sum(dev * dev, axis=0, keepdims=True))
    radius = jnp.sqrt(jnp.max(far, axis=1, keepdims=True))
    reach = jnp.zeros((1, 256), F32)
    low = jnp.zeros((15, 256), F32)
    for s in range(n):
        q = get(s, 0, 32).astype(F32) * SCALE
        hi = q.astype(BF)
        lo = (q - hi.astype(F32)).astype(BF)
        size = jnp.sqrt(jnp.sum(q * q, axis=0, keepdims=True)) * radius
        reach = jnp.maximum(reach, size)
        shift = jnp.sum(q * kmean, axis=0, keepdims=True) + size
        qx[:, pl.ds(s * 256, 256)] = jnp.concatenate([hi, lo, jnp.concatenate([-shift, low], axis=0).astype(BF)], axis=0)
    return jnp.max(reach)


def bounded(jobs, kb, qn, depth):
    W = 256 * qn
    seq = []
    for kx, vx, qt, put in jobs:
        steps = kx.shape[0] // kb
        for j in range(steps):
            seq.append((kx, vx, qt, put, j, j + 1 == steps))

    def dots(t):
        kx, _, qt, _, j, _ = seq[t]
        return jnp.dot(kx[j * kb:(j + 1) * kb, 0:80], qt(), preferred_element_type=F32)

    ahead = {t: dots(t) for t in range(depth)}
    for t, (kx, vx, qt, put, j, last) in enumerate(seq):
        if t + depth < len(seq):
            ahead[t + depth] = dots(t + depth)
        p = jnp.exp2(ahead.pop(t))
        part = jnp.sum(p.reshape(kb // 8, 8, W), axis=0)
        out = jnp.dot(vx[0:32, j * kb:(j + 1) * kb], p.astype(BF), preferred_element_type=F32)
        l, o = (part, out) if j == 0 else (l + part, o + out)
        if last:
            put((o / jnp.sum(l, axis=0, keepdims=True)).astype(BF))


def general(n, put, kx, vx, qx):
    def qblock(i, c):
        qt = qx[0:64, pl.ds(pl.multiple_of(i * 256, 256), 256)]

        def step(j, carry):
            m, o = carry
            k0 = pl.multiple_of(j * 256, 256)
            s = jnp.dot(kx[pl.ds(k0, 256), 0:64], qt, preferred_element_type=F32)
            mn = jnp.maximum(m, jnp.max(s, axis=0, keepdims=True))
            p = jnp.exp2(s - mn).astype(BF)
            return mn, o * jnp.exp2(m - mn) + jnp.dot(vx[:, pl.ds(k0, 256)], p, preferred_element_type=F32)

        _, o = lax.fori_loop(0, n, step, (jnp.full((1, 256), -jnp.inf, F32), jnp.zeros((48, 256), F32)))
        put(i, (o[0:32] / o[32:33]).astype(BF))
        return c

    lax.fori_loop(0, n, qblock, 0)


def attention(a, kb, qn, depth, group):
    items = a.shape[1] if a.ndim == 4 else 1
    n = a.shape[0]

    def kernel(a_ref, o_ref, *sc):
        refs = [sc[3 * i:3 * i + 3] for i in range(items)]

        def put(it, s, v):
            if a.ndim == 4:
                o_ref[s, it] = v
            else:
                o_ref[s] = v

        def getter(it):
            return lambda s, lo, hi: a_ref[s, it, lo:hi, :] if a.ndim == 4 else a_ref[s, lo:hi, :]

        reach = prepare(getter(0), n, *refs[0])
        for it in range(1, items):
            reach = jnp.maximum(reach, prepare(getter(it), n, *refs[it]))
        fits = reach <= GAP
        W = 256 * qn

        @pl.when(fits)
        def _():
            def body(g, c):
                jobs = []
                for it in range(items):
                    kx, vx, qx = refs[it]
                    for u in range(group):
                        i = g * group + u

                        def qt(i=i, qx=qx):
                            start = i * W if isinstance(i, int) else pl.multiple_of(i * W, W)
                            return qx[:, pl.ds(start, W)]

                        def store(r, i=i, it=it):
                            for v in range(qn):
                                put(it, i * qn + v, r[:, v * 256:(v + 1) * 256])

                        jobs.append((kx, vx, qt, store))
                bounded(jobs, kb, qn, depth)
                return c

            trips = n // (qn * group)
            if trips == 1:
                body(0, 0)
            else:
                lax.fori_loop(0, trips, body, 0)

        @pl.when(jnp.logical_not(fits))
        def _():
            for it in range(items):
                general(n, lambda s, v, it=it: put(it, s, v), *refs[it])

    vm = pl.BlockSpec(memory_space=pltpu.VMEM)
    return pl.pallas_call(
        kernel, out_shape=jax.ShapeDtypeStruct(a.shape[:-2] + (32, 256), BF), in_specs=[vm], out_specs=vm,
        scratch_shapes=[pltpu.VMEM((n * 256, 128), BF), pltpu.VMEM((48, n * 256), BF), pltpu.VMEM((80, n * 256), BF)] * items,
        compiler_params=pltpu.CompilerParams(vmem_limit_bytes=16 << 20),
        cost_estimate=pl.CostEstimate(flops=8 * items * (n * 256) ** 2 * 256, transcendentals=0, bytes_accessed=1 << 20),
        name="attn_v" if items > 1 else "attn_h",
    )(a)


def norm(x, gain):
    center = x - jnp.mean(x, axis=-1, keepdims=True)
    spread = jnp.mean(center * center, axis=-1, keepdims=True)
    return center * lax.rsqrt(spread + EPS) * gain


def tdot(a, b):
    return lax.dot_general(a, b, (((0,), (1,)), ((), ())), preferred_element_type=F32)


def project_across(get, gain, w_ref, c_ref):
    for b in range(4):
        n = norm(get(b), gain).astype(BF)
        for t in range(3):
            out = tdot(w_ref[:, t * 256:t * 256 + 128], n).astype(BF)
            c_ref[4 * b:4 * b + 4, t * 32:t * 32 + 32, :] = out.reshape(4, 32, 256)


def down_kernel(layer, x_ref, gain_ref, w_ref, r_ref):
    for cb in range(4):
        x = x_ref[:, 8 * cb:8 * cb + 8, :].astype(F32).reshape(256, D)
        n = norm(x, gain_ref[layer:layer + 1]).astype(BF)
        for t in range(3):
            out = tdot(w_ref[:, t * 256 + 128:t * 256 + 256], n).astype(BF)
            r_ref[2 * cb:2 * cb + 2, :, t * 32:t * 32 + 32, :] = out.reshape(2, 2, 32, 256)


def mix_kernel(x_ref, hc_ref, wo_ref, m_ref):
    for b in range(4):
        h = hc_ref[4 * b:4 * b + 4].reshape(128, 256)
        out = lax.dot_general(h, wo_ref[0:128, :], (((0,), (0,)), ((), ())), preferred_element_type=F32)
        m_ref[8 * b:8 * b + 8] = out.reshape(8, 32, D) + x_ref[8 * b:8 * b + 8].astype(F32)


def finish(layer, m_ref, hv_ref, wo_ref, gain_ref, wu_ref, wd_ref, mix, put):
    for cb in range(4):
        h = hv_ref[4 * cb:4 * cb + 4].reshape(128, 256)
        out = lax.dot_general(h, wo_ref[128:256, :], (((0,), (0,)), ((), ())), preferred_element_type=F32)
        mix[:, 8 * cb:8 * cb + 8, :] = out.reshape(32, 8, D)
    for b in range(4):
        mixed = (m_ref[8 * b:8 * b + 8] + mix[8 * b:8 * b + 8]).reshape(256, D)
        n2 = norm(mixed, gain_ref[layer:layer + 1]).astype(BF)
        up = jnp.dot(n2, wu_ref[...], preferred_element_type=F32)
        act = 0.5 * up * (1.0 + jnp.tanh(0.7978845608028654 * (up + 0.044715 * (up * up * up))))
        out = mixed + jnp.dot(act.astype(BF), wd_ref[...], preferred_element_type=F32)
        put(b, out.astype(BF))


def mid_kernel(layer, m_ref, hv_ref, wo_ref, gm_ref, wu_ref, wd_ref, ga_ref, w_ref, y_ref, c_ref, mix):
    def put(b, v):
        y_ref[8 * b:8 * b + 8] = v.reshape(8, 32, D)

    finish(layer, m_ref, hv_ref, wo_ref, gm_ref, wu_ref, wd_ref, mix, put)
    project_across(lambda b: y_ref[8 * b:8 * b + 8].reshape(256, D).astype(F32), ga_ref[layer + 1:layer + 2], w_ref, c_ref)


def last_kernel(layer, m_ref, hv_ref, wo_ref, gm_ref, wu_ref, wd_ref, y_ref, mix):
    def put(b, v):
        y_ref[8 * b:8 * b + 8] = v.reshape(8, 32, D)

    finish(layer, m_ref, hv_ref, wo_ref, gm_ref, wu_ref, wd_ref, mix, put)


VM = pl.BlockSpec(memory_space=pltpu.VMEM)
ACROSS = jax.ShapeDtypeStruct((16, 96, 256), BF)
DOWN = jax.ShapeDtypeStruct((8, 2, 96, 256), BF)
STATE = jax.ShapeDtypeStruct((32, 32, D), BF)
MIXED = jax.ShapeDtypeStruct((32, 32, D), F32)


def call(kernel, outs, scratch, flops, *args):
    def body(*refs):
        picked = [r.at[a[1]] if isinstance(a, tuple) else r for r, a in zip(refs, args)]
        kernel(*picked, *refs[len(args):])

    return pl.pallas_call(
        body, out_shape=outs, in_specs=[VM] * len(args), out_specs=jax.tree.map(lambda _: VM, outs),
        scratch_shapes=scratch, compiler_params=pltpu.CompilerParams(vmem_limit_bytes=24 << 20),
        cost_estimate=pl.CostEstimate(flops=flops, transcendentals=0, bytes_accessed=1 << 20),
    )(*[a[0] if isinstance(a, tuple) else a for a in args])


def shards(frame, gain_attn, w_qkv, w_out, gain_mlp, w_up, w_down):
    bind = lambda f, layer: (lambda *refs: f(layer, *refs))
    scratch = [pltpu.VMEM((32, 32, D), F32)]
    state = frame
    first = lambda x_ref, g_ref, w_ref, c_ref: project_across(
        lambda b: x_ref[8 * b:8 * b + 8].reshape(256, D).astype(F32), g_ref[0:1], w_ref, c_ref)
    c = call(first, ACROSS, [], 2 << 30, state, gain_attn, (w_qkv, 0))
    for layer in range(LAYERS):
        c = lax.all_to_all(c, "col", 0, 0, tiled=True)
        r = call(bind(down_kernel, layer), DOWN, [], 2 << 30, state, gain_attn, (w_qkv, layer))
        r = lax.all_to_all(r, "row", 0, 0, tiled=True)
        hc = attention(c, 256, 2, 2, 2)
        hc = lax.all_to_all(hc, "col", 0, 0, tiled=True)
        hv = attention(r, 256, 2, 2, 2)
        hv = lax.all_to_all(hv, "row", 0, 0, tiled=True).reshape(16, 32, 256)
        m = call(mix_kernel, MIXED, [], 1 << 30, state, hc, (w_out, layer))
        rest = (m, hv, (w_out, layer), gain_mlp, (w_up, layer), (w_down, layer))
        if layer + 1 < LAYERS:
            state, c = call(bind(mid_kernel, layer), (STATE, ACROSS), scratch, 6 << 30, *rest, gain_attn, (w_qkv, layer + 1))
        else:
            state = call(bind(last_kernel, layer), STATE, scratch, 4 << 30, *rest)
    return state


def solution(mesh):
    placed = (P("row", "col", None), P(), P(), P(), P(), P(), P())
    return jax.shard_map(
        shards, mesh=mesh, in_specs=placed, out_specs=P("row", "col", None), check_vma=False
    )
```

time: 172 us -> 410 us (2.38)
  Pallas kernels: 75.3 us -> 317 us
  blocking collectives: 32.1 us -> 0 us
  starting transfers between devices: 32.7 us -> 48.4 us
  waiting for transfers between devices: 19.1 us -> 33.5 us
    pallas_call x7 -> x11, Pallas kernels: 75.3 us -> 317 us  [the longest x4 304 us: attention(): pl.pallas_call(kernel, out_shape=jax.ShapeDtypeStruct(a.shape[:-2] + (32,...]
    all_to_all x2 -> x0, blocking collectives: 32.1 us -> none  [the longest x1 19.6 us: shards(): r = lax.all_to_all(r, 'row', 0, 0, tiled=True)]
    all_to_all x2, waiting for transfers between devices: 3.76 us -> 21.2 us  [shards(): c = lax.all_to_all(c, 'col', 0, 0, tiled=True)]
    all_to_all x3 -> x4, starting transfers between devices: 12.7 us -> 23.6 us  [the longest x2 14.1 us: shards(): hv = lax.all_to_all(hv, 'row', 0, 0, tiled=True).reshape(16, 32, 256)]
    all_to_all x1 -> x2, waiting for transfers between devices: 10.4 us -> 0.01 us  [shards(): r = lax.all_to_all(r, 'row', 0, 0, tiled=True)]
    all_to_all x3 -> x4, waiting for transfers between devices: 4.92 us -> 12.4 us  [the longest x2 12.4 us: shards(): hv = lax.all_to_all(hv, 'row', 0, 0, tiled=True).reshape(16, 32, 256)]
    unnamed x21 -> x40, local copies, waits for them, and re-layouts: 4.56 us -> 9.31 us
    all_to_all x1 -> x2, starting transfers between devices: 7.6 us -> 9.9 us  [shards(): r = lax.all_to_all(r, 'row', 0, 0, tiled=True)]
  transfers between devices with their start and end apart: 6 -> 8, of which waited for: 4 -> 4; matrix products, arithmetic and copies ran while one was open for 2% -> 0% of each run, Pallas kernels for 36% -> 75%
where the time goes in v1:
time: 410 us; the launch traced here: 409 us
  Pallas kernels  317 us (77%)
  starting transfers between devices  48.4 us (12%)
  waiting for transfers between devices  33.5 us (8%)
  local copies, waits for them, and re-layouts  9.31 us (2%)
    pallas_call x4, Pallas kernels, attention(): pl.pallas_call(kernel, out_shape=jax.ShapeDtypeStruct(a.shape[:-2] + (32,...  304 us
    all_to_all x2, waiting for transfers between devices, shards(): c = lax.all_to_all(c, 'col', 0, 0, tiled=True)  21.2 us
    all_to_all x2, starting transfers between devices, shards(): c = lax.all_to_all(c, 'col', 0, 0, tiled=True)  14.8 us
    all_to_all x2, starting transfers between devices, shards(): hv = lax.all_to_all(hv, 'row', 0, 0, tiled=True).reshape(16, 32, 256)  14.1 us
    pallas_call x7, Pallas kernels, call(): pl.pallas_call(body, out_shape=outs, in_specs=[VM] * len(args), out_specs...  13.7 us
    all_to_all x2, waiting for transfers between devices, shards(): hv = lax.all_to_all(hv, 'row', 0, 0, tiled=True).reshape(16, 32, 256)  12.4 us
    all_to_all x2, starting transfers between devices, shards(): r = lax.all_to_all(r, 'row', 0, 0, tiled=True)  9.9 us
    all_to_all x2, starting transfers between devices, shards(): hc = lax.all_to_all(hc, 'col', 0, 0, tiled=True)  9.52 us
  transfers between devices with their start and end apart: 8, of which 4 were waited for; matrix products, arithmetic and copies ran while one was open for 0% of the time, Pallas kernels for 75%

profile of v1, /device:TPU:1, one launch (start us, length us, event | category | flops | bytes accessed | tf_op | source)
XLA Modules:
  0.0 408.6 jit_solution(8958411468534983665)
XLA Ops:
  0.0 1.1 copy-done.3
  1.1 1.0 copy-done.5
  2.2 0.7 copy-done.10
  2.9 2.0 shard_map.73
  4.8 8.0 %all-to-all-start = ((bf16[16,96,256]{2,1,0:T(8,128)(2,1)}), bf16[16,96,256]{2,1,0:T(8,128)(2,1)S(1)}, u32[]{:S(2)}, u32[]{:S(2)}) async-start(bf16[16,96,256]{2,1,0:T(8,128)(2,1)} %shard_map.73), calls=%async_computation | async-start | bytes 1572864 | tf_op jit(solution)/shard_map/all_to_all | solution.py:245
  12.8 0.0 copy-done.4
  12.8 0.0 copy-done.6
  12.8 0.0 copy-done.11
  12.8 2.0 shard_map.75
  14.8 10.6 %all-to-all-done.a_ref = bf16[16,96,256]{2,1,0:T(8,128)(2,1)S(1)} async-done(((bf16[16,96,256]{2,1,0:T(8,128)(2,1)}), bf16[16,96,256]{2,1,0:T(8,128)(2,1)S(1)}, u32[]{:S(2)}, u32[]{:S(2)}) %all-to-all-start) | async-done | bytes 786464 | tf_op jit(solution)/shard_map/all_to_all | solution.py:245
  25.3 6.4 %all-to-all-start.2 = ((bf16[8,2,96,256]{3,2,1,0:T(8,128)(2,1)}), bf16[8,2,96,256]{3,2,1,0:T(8,128)(2,1)S(1)}, u32[]{:S(2)}, u32[]{:S(2)}) async-start(bf16[8,2,96,256]{3,2,1,0:T(8,128)(2,1)} %shard_map.75), calls=%async_computation.2 | async-start | bytes 1572864 | tf_op jit(solution)/shard_map/all_to_all | solution.py:247
  31.7 100.6 %attn_h.2 = bf16[16,32,256]{2,1,0:T(8,128)(2,1)} custom-call(bf16[16,96,256]{2,1,0:T(8,128)(2,1)S(1)} %all-to-all-done.a_ref), custom_call_target="tpu_custom_call" | custom-call | flops 34359738368 | bytes 1048576 | tf_op jit(solution)/shard_map/attn_h/pallas_call | solution.py:146
  132.3 0.0 all-to-all-done.2.a_ref
  132.3 4.9 %all-to-all-start.1 = ((bf16[16,32,256]{2,1,0:T(8,128)(2,1)}), bf16[16,32,256]{2,1,0:T(8,128)(2,1)S(1)}, u32[]{:S(2)}, u32[]{:S(2)}) async-start(bf16[16,32,256]{2,1,0:T(8,128)(2,1)} %attn_h.2), calls=%async_computation.1 | async-start | bytes 524288 | tf_op jit(solution)/shard_map/all_to_all | solution.py:249
  137.1 51.1 %attn_v.2 = bf16[8,2,32,256]{3,2,1,0:T(8,128)(2,1)} custom-call(bf16[8,2,96,256]{3,2,1,0:T(8,128)(2,1)S(1)} %all-to-all-done.2.a_ref), custom_call_target="tpu_custom_call" | custom-call | flops 17179869184 | bytes 1048576 | tf_op jit(solution)/shard_map/attn_v/pallas_call | solution.py:146
  188.2 0.0 all-to-all-done.1.refs_1_
  188.2 7.1 %all-to-all-start.3 = ((bf16[8,2,32,256]{3,2,1,0:T(8,128)(2,1)}), bf16[8,2,32,256]{3,2,1,0:T(8,128)(2,1)S(1)}, u32[]{:S(2)}, u32[]{:S(2)}) async-start(bf16[8,2,32,256]{3,2,1,0:T(8,128)(2,1)} %attn_v.2), calls=%async_computation.3 | async-start | bytes 524288 | tf_op jit(solution)/shard_map/all_to_all | solution.py:251
  195.3 0.0 copy-done.8
  195.3 0.0 copy-done.7
  195.3 0.0 copy-start
  195.3 0.0 copy-start.12
  195.3 0.3 shard_map.74.refs_0_
  195.7 0.0 copy-start.13
  195.7 1.0 copy-done.13
  196.6 6.2 %all-to-all-done.3 = bf16[8,2,32,256]{3,2,1,0:T(8,128)(2,1)S(1)} async-done(((bf16[8,2,32,256]{3,2,1,0:T(8,128)(2,1)}), bf16[8,2,32,256]{3,2,1,0:T(8,128)(2,1)S(1)}, u32[]{:S(2)}, u32[]{:S(2)}) %all-to-all-start.3) | async-done | bytes 262176 | tf_op jit(solution)/shard_map/all_to_all | solution.py:251
  202.8 0.0 copy-done
  202.8 0.0 copy-done.12
  202.8 1.2 copy-done.1
  204.1 1.2 copy-done.14
  205.3 3.9 shard_map.76
  209.2 0.8 copy-done.17
  210.0 6.9 %all-to-all-start.4 = ((bf16[16,96,256]{2,1,0:T(8,128)(2,1)}), bf16[16,96,256]{2,1,0:T(8,128)(2,1)S(1)}, u32[]{:S(2)}, u32[]{:S(2)}) async-start(bf16[16,96,256]{2,1,0:T(8,128)(2,1)} %get-tuple-element.8), calls=%async_computation.4 | async-start | bytes 1572864 | tf_op jit(solution)/shard_map/all_to_all | solution.py:245
  216.9 2.0 shard_map.78
  218.8 10.6 %all-to-all-done.4.a_ref = bf16[16,96,256]{2,1,0:T(8,128)(2,1)S(1)} async-done(((bf16[16,96,256]{2,1,0:T(8,128)(2,1)}), bf16[16,96,256]{2,1,0:T(8,128)(2,1)S(1)}, u32[]{:S(2)}, u32[]{:S(2)}) %all-to-all-start.4) | async-done | bytes 786464 | tf_op jit(solution)/shard_map/all_to_all | solution.py:245
  229.4 3.5 all-to-all-start.6
  233.0 100.6 %attn_h.3 = bf16[16,32,256]{2,1,0:T(8,128)(2,1)} custom-call(bf16[16,96,256]{2,1,0:T(8,128)(2,1)S(1)} %all-to-all-done.4.a_ref), custom_call_target="tpu_custom_call" | custom-call | flops 34359738368 | bytes 1048576 | tf_op jit(solution)/shard_map/attn_h/pallas_call | solution.py:146
  333.5 0.0 all-to-all-done.6.a_ref
  333.5 4.7 %all-to-all-start.5 = ((bf16[16,32,256]{2,1,0:T(8,128)(2,1)}), bf16[16,32,256]{2,1,0:T(8,128)(2,1)S(1)}, u32[]{:S(2)}, u32[]{:S(2)}) async-start(bf16[16,32,256]{2,1,0:T(8,128)(2,1)} %attn_h.3), calls=%async_computation.5 | async-start | bytes 524288 | tf_op jit(solution)/shard_map/all_to_all | solution.py:249
  338.2 51.3 %attn_v.3 = bf16[8,2,32,256]{3,2,1,0:T(8,128)(2,1)} custom-call(bf16[8,2,96,256]{3,2,1,0:T(8,128)(2,1)S(1)} %all-to-all-done.6.a_ref), custom_call_target="tpu_custom_call" | custom-call | flops 17179869184 | bytes 1048576 | tf_op jit(solution)/shard_map/attn_v/pallas_call | solution.py:146
  389.5 0.0 all-to-all-done.5.refs_1_
  389.5 7.1 %all-to-all-start.7 = ((bf16[8,2,32,256]{3,2,1,0:T(8,128)(2,1)}), bf16[8,2,32,256]{3,2,1,0:T(8,128)(2,1)S(1)}, u32[]{:S(2)}, u32[]{:S(2)}) async-start(bf16[8,2,32,256]{3,2,1,0:T(8,128)(2,1)} %attn_v.3), calls=%async_computation.7 | async-start | bytes 524288 | tf_op jit(solution)/shard_map/all_to_all | solution.py:251
  396.6 0.0 copy-done.19
  396.6 0.0 copy-start.2
  396.6 0.3 shard_map.77.refs_0_
  397.0 1.0 copy-done.15
  397.9 6.2 %all-to-all-done.7 = bf16[8,2,32,256]{3,2,1,0:T(8,128)(2,1)S(1)} async-done(((bf16[8,2,32,256]{3,2,1,0:T(8,128)(2,1)}), bf16[8,2,32,256]{3,2,1,0:T(8,128)(2,1)S(1)}, u32[]{:S(2)}, u32[]{:S(2)}) %all-to-all-start.7) | async-done | bytes 262176 | tf_op jit(solution)/shard_map/all_to_all | solution.py:251
  404.1 1.2 copy-done.16
  405.3 3.3 shard_map.79
  (19 shorter events, 0.0 us)
Async XLA Ops:
  0.0 1.1 copy-start.3
  1.1 1.0 copy-start.5
  2.2 0.7 copy-start.10
  4.8 8.0 %copy-start.4 = (bf16[2,256,768]{2,1,0:T(8,128)(2,1)S(1)}, bf16[2,256,768]{2,1,0:T(8,128)(2,1)}, u32[]{:S(2)}) copy-start(bf16[2,256,768]{2,1,0:T(8,128)(2,1)} %refs_2_.12) | copy-start | bytes 2359300
  4.8 8.0 %copy-start.6 = (bf16[32,32,256]{2,1,0:T(8,128)(2,1)S(1)}, bf16[32,32,256]{2,1,0:T(8,128)(2,1)}, u32[]{:S(2)}) copy-start(bf16[32,32,256]{2,1,0:T(8,128)(2,1)} %refs_0_.5) | copy-start | bytes 1572868
  4.8 8.0 %copy-start.11 = (f32[2,256]{1,0:T(2,128)S(1)}, f32[2,256]{1,0:T(2,128)}, u32[]{:S(2)}) copy-start(f32[2,256]{1,0:T(2,128)} %refs_1_.5) | copy-start | bytes 6148
  4.8 20.5 %all-to-all-start = ((bf16[16,96,256]{2,1,0:T(8,128)(2,1)}), bf16[16,96,256]{2,1,0:T(8,128)(2,1)S(1)}, u32[]{:S(2)}, u32[]{:S(2)}) async-start(bf16[16,96,256]{2,1,0:T(8,128)(2,1)} %shard_map.73), calls=%async_computation | async-start | bytes 1572864 | tf_op jit(solution)/shard_map/all_to_all | solution.py:245
  25.3 106.9 %all-to-all-start.2 = ((bf16[8,2,96,256]{3,2,1,0:T(8,128)(2,1)}), bf16[8,2,96,256]{3,2,1,0:T(8,128)(2,1)S(1)}, u32[]{:S(2)}, u32[]{:S(2)}) async-start(bf16[8,2,96,256]{3,2,1,0:T(8,128)(2,1)} %shard_map.75), calls=%async_computation.2 | async-start | bytes 1572864 | tf_op jit(solution)/shard_map/all_to_all | solution.py:247
  132.3 56.0 %all-to-all-start.1 = ((bf16[16,32,256]{2,1,0:T(8,128)(2,1)}), bf16[16,32,256]{2,1,0:T(8,128)(2,1)S(1)}, u32[]{:S(2)}, u32[]{:S(2)}) async-start(bf16[16,32,256]{2,1,0:T(8,128)(2,1)} %attn_h.2), calls=%async_computation.1 | async-start | bytes 524288 | tf_op jit(solution)/shard_map/all_to_all | solution.py:249
  137.1 58.2 %copy-start.8 = (bf16[2,256,256]{2,1,0:T(8,128)(2,1)S(1)}, bf16[2,256,256]{2,1,0:T(8,128)(2,1)}, u32[]{:S(2)}) copy-start(bf16[2,256,256]{2,1,0:T(8,128)(2,1)} %refs_2_.13) | copy-start | bytes 786436
  188.2 7.1 %copy-start.7 = (bf16[32,32,256]{2,1,0:T(8,128)(2,1)S(1)}, bf16[32,32,256]{2,1,0:T(8,128)(2,1)}, u32[]{:S(2)}) copy-start(bf16[32,32,256]{2,1,0:T(8,128)(2,1)} %refs_0_.5) | copy-start | bytes 1572868
  188.2 14.6 %all-to-all-start.3 = ((bf16[8,2,32,256]{3,2,1,0:T(8,128)(2,1)}), bf16[8,2,32,256]{3,2,1,0:T(8,128)(2,1)S(1)}, u32[]{:S(2)}, u32[]{:S(2)}) async-start(bf16[8,2,32,256]{3,2,1,0:T(8,128)(2,1)} %attn_v.2), calls=%async_computation.3 | async-start | bytes 524288 | tf_op jit(solution)/shard_map/all_to_all | solution.py:251
  195.3 7.5 %copy-start = (bf16[2,256,1024]{2,1,0:T(8,128)(2,1)S(1)}, bf16[2,256,1024]{2,1,0:T(8,128)(2,1)}, u32[]{:S(2)}) copy-start(bf16[2,256,1024]{2,1,0:T(8,128)(2,1)} %refs_4_.3) | copy-start | bytes 3145732
  195.3 7.5 %copy-start.12 = (f32[2,256]{1,0:T(2,128)S(1)}, f32[2,256]{1,0:T(2,128)}, u32[]{:S(2)}) copy-start(f32[2,256]{1,0:T(2,128)} %refs_3_.3) | copy-start | bytes 6148
  195.7 1.0 copy-start.13
  202.8 1.2 copy-start.1
  204.1 1.2 copy-start.14
  209.2 0.8 copy-start.17
  210.0 6.9 %copy-start.18 = (bf16[32,32,256]{2,1,0:T(8,128)(2,1)S(1)}, bf16[32,32,256]{2,1,0:T(8,128)(2,1)}, u32[]{:S(2)}) copy-start(bf16[32,32,256]{2,1,0:T(8,128)(2,1)} %copy-done.17) | copy-start | bytes 1572868
  210.0 19.4 %all-to-all-start.4 = ((bf16[16,96,256]{2,1,0:T(8,128)(2,1)}), bf16[16,96,256]{2,1,0:T(8,128)(2,1)S(1)}, u32[]{:S(2)}, u32[]{:S(2)}) async-start(bf16[16,96,256]{2,1,0:T(8,128)(2,1)} %get-tuple-element.8), calls=%async_computation.4 | async-start | bytes 1572864 | tf_op jit(solution)/shard_map/all_to_all | solution.py:245
  229.4 104.1 %all-to-all-start.6 = ((bf16[8,2,96,256]{3,2,1,0:T(8,128)(2,1)}), bf16[8,2,96,256]{3,2,1,0:T(8,128)(2,1)S(1)}, u32[]{:S(2)}, u32[]{:S(2)}) async-start(bf16[8,2,96,256]{3,2,1,0:T(8,128)(2,1)} %shard_map.78), calls=%async_computation.6 | async-start | bytes 1572864 | tf_op jit(solution)/shard_map/all_to_all | solution.py:247
  333.5 56.0 %all-to-all-start.5 = ((bf16[16,32,256]{2,1,0:T(8,128)(2,1)}), bf16[16,32,256]{2,1,0:T(8,128)(2,1)S(1)}, u32[]{:S(2)}, u32[]{:S(2)}) async-start(bf16[16,32,256]{2,1,0:T(8,128)(2,1)} %attn_h.3), calls=%async_computation.5 | async-start | bytes 524288 | tf_op jit(solution)/shard_map/all_to_all | solution.py:249
  338.2 58.4 %copy-start.19 = (bf16[32,32,256]{2,1,0:T(8,128)(2,1)S(1)}, bf16[32,32,256]{2,1,0:T(8,128)(2,1)}, u32[]{:S(2)}) copy-start(bf16[32,32,256]{2,1,0:T(8,128)(2,1)} %copy-done.17) | copy-start | bytes 1572868
  389.5 7.1 %copy-start.9 = (bf16[2,256,256]{2,1,0:T(8,128)(2,1)S(1)}, bf16[2,256,256]{2,1,0:T(8,128)(2,1)}, u32[]{:S(2)}) copy-start(bf16[2,256,256]{2,1,0:T(8,128)(2,1)} %refs_2_.13) | copy-start | bytes 786436
  389.5 14.6 %all-to-all-start.7 = ((bf16[8,2,32,256]{3,2,1,0:T(8,128)(2,1)}), bf16[8,2,32,256]{3,2,1,0:T(8,128)(2,1)S(1)}, u32[]{:S(2)}, u32[]{:S(2)}) async-start(bf16[8,2,32,256]{3,2,1,0:T(8,128)(2,1)} %attn_v.3), calls=%async_computation.7 | async-start | bytes 524288 | tf_op jit(solution)/shard_map/all_to_all | solution.py:251
  396.6 7.5 %copy-start.2 = (bf16[2,1024,256]{2,1,0:T(8,128)(2,1)S(1)}, bf16[2,1024,256]{2,1,0:T(8,128)(2,1)}, u32[]{:S(2)}) copy-start(bf16[2,1024,256]{2,1,0:T(8,128)(2,1)} %refs_5_.3) | copy-start | bytes 3145732
  396.9 1.0 copy-start.15
  404.1 1.2 copy-start.16

commit v2 on v1

v2 whole, which is shorter than its diff:
```python
import jax
import jax.numpy as jnp
from jax import lax
from jax.experimental import pallas as pl
from jax.experimental.pallas import tpu as pltpu
from jax.sharding import Mesh
from jax.sharding import PartitionSpec as P

D = 256
LAYERS = 2
EPS = 1e-05
SCALE = 32 ** -0.5 * 1.4426950408889634
BF = jnp.bfloat16
F32 = jnp.float32
ROW = ("x", "yh")
COL = "col"


GAP = 90.0


def prepare(get, n, kx, vx, qx):
    nk = n * 256
    ones = jnp.ones((16, 256), BF)
    ksum = jnp.zeros((32, 256), F32)
    for s in range(n):
        kt = get(s, 32, 64)
        ksum = ksum + kt.astype(F32)
        kx[pl.ds(s * 256, 256), 0:80] = jnp.concatenate([kt, kt, ones], axis=0).T
        vx[0:32, pl.ds(s * 256, 256)] = get(s, 64, 96)
    vx[32:48, :] = jnp.ones((16, nk), BF)
    kmean = jnp.sum(ksum, axis=1, keepdims=True) * (1.0 / nk)
    far = jnp.zeros((1, 256), F32)
    for s in range(n):
        dev = get(s, 32, 64).astype(F32) - kmean
        far = jnp.maximum(far, jnp.sum(dev * dev, axis=0, keepdims=True))
    radius = jnp.sqrt(jnp.max(far, axis=1, keepdims=True))
    reach = jnp.zeros((1, 256), F32)
    low = jnp.zeros((15, 256), F32)
    for s in range(n):
        q = get(s, 0, 32).astype(F32) * SCALE
        hi = q.astype(BF)
        lo = (q - hi.astype(F32)).astype(BF)
        size = jnp.sqrt(jnp.sum(q * q, axis=0, keepdims=True)) * radius
        reach = jnp.maximum(reach, size)
        shift = jnp.sum(q * kmean, axis=0, keepdims=True) + size
        qx[:, pl.ds(s * 256, 256)] = jnp.concatenate([hi, lo, jnp.concatenate([-shift, low], axis=0).astype(BF)], axis=0)
    return jnp.max(reach)


def bounded(jobs, kb, qn, depth):
    W = 256 * qn
    seq = []
    for kx, vx, qt, put in jobs:
        steps = kx.shape[0] // kb
        for j in range(steps):
            seq.append((kx, vx, qt, put, j, j + 1 == steps))

    def dots(t):
        kx, _, qt, _, j, _ = seq[t]
        return jnp.dot(kx[j * kb:(j + 1) * kb, 0:80], qt(), preferred_element_type=F32)

    ahead = {t: dots(t) for t in range(depth)}
    for t, (kx, vx, qt, put, j, last) in enumerate(seq):
        if t + depth < len(seq):
            ahead[t + depth] = dots(t + depth)
        p = jnp.exp2(ahead.pop(t))
        part = jnp.sum(p.reshape(kb // 8, 8, W), axis=0)
        out = jnp.dot(vx[0:32, j * kb:(j + 1) * kb], p.astype(BF), preferred_element_type=F32)
        l, o = (part, out) if j == 0 else (l + part, o + out)
        if last:
            put((o / jnp.sum(l, axis=0, keepdims=True)).astype(BF))


def general(n, put, kx, vx, qx):
    def qblock(i, c):
        qt = qx[0:64, pl.ds(pl.multiple_of(i * 256, 256), 256)]

        def step(j, carry):
            m, o = carry
            k0 = pl.multiple_of(j * 256, 256)
            s = jnp.dot(kx[pl.ds(k0, 256), 0:64], qt, preferred_element_type=F32)
            mn = jnp.maximum(m, jnp.max(s, axis=0, keepdims=True))
            p = jnp.exp2(s - mn).astype(BF)
            return mn, o * jnp.exp2(m - mn) + jnp.dot(vx[:, pl.ds(k0, 256)], p, preferred_element_type=F32)

        _, o = lax.fori_loop(0, n, step, (jnp.full((1, 256), -jnp.inf, F32), jnp.zeros((48, 256), F32)))
        put(i, (o[0:32] / o[32:33]).astype(BF))
        return c

    lax.fori_loop(0, n, qblock, 0)


def attend(items, n, get, put, refs, group):
    kb, qn, depth = 256, 2, 2
    reach = prepare(lambda *k: get(0, *k), n, *refs[0])
    for it in range(1, items):
        reach = jnp.maximum(reach, prepare(lambda *k, it=it: get(it, *k), n, *refs[it]))
    fits = reach <= GAP
    W = 256 * qn
    trips = n // (qn * group)

    @pl.when(fits)
    def _():
        def body(g, c):
            jobs = []
            for it in range(items):
                kx, vx, qx = refs[it]
                for u in range(group):
                    i = g * group + u

                    def qt(i=i, qx=qx):
                        return qx[:, pl.ds(pl.multiple_of(i * W, W), W)]

                    def store(r, i=i, it=it):
                        for v in range(qn):
                            put(it, i * qn + v, r[:, v * 256:(v + 1) * 256])

                    jobs.append((kx, vx, qt, store))
            bounded(jobs, kb, qn, depth)
            return c

        lax.fori_loop(0, trips, body, 0)

    @pl.when(jnp.logical_not(fits))
    def _():
        for it in range(items):
            general(n, lambda s, v, it=it: put(it, s, v), *refs[it])


def across_kernel(a_ref, o_ref, *sc):
    def put(it, s, v):
        o_ref[s] = v

    attend(1, 16, lambda it, s, lo, hi: a_ref[s, lo:hi, :], put, [sc], 2)


def split_kernel(*refs):
    for k in range(4):
        for e in range(2):
            refs[4 + e][k] = refs[k][e]


def down_attend_kernel(pos, near, far, o_ref, *sc):
    def get(it, s, lo, hi):
        return (far if s % 2 else near)[s // 2, it, lo:hi, :]

    def put(it, s, v):
        k, e = s // 2, s % 2
        o_ref[2 * ((pos[0] - k + 4) % 4) + (pos[1] + e) % 2, it] = v

    attend(2, 8, get, put, [sc[0:3], sc[3:6]], 2)


def norm(x, gain):
    center = x - jnp.mean(x, axis=-1, keepdims=True)
    spread = jnp.mean(center * center, axis=-1, keepdims=True)
    return center * lax.rsqrt(spread + EPS) * gain


def tdot(a, b):
    return lax.dot_general(a, b, (((0,), (1,)), ((), ())), preferred_element_type=F32)


def project(get, pos, gain, w_ref, c_ref, outs, nrm, all_ref):
    for b in range(4):
        n = norm(get(b), gain)
        nrm[8 * b:8 * b + 8] = n.reshape(8, 32, D)
        n = n.astype(BF)
        for t in range(3):
            out = tdot(w_ref[:, t * 256:t * 256 + 128], n).astype(BF)
            c_ref[4 * b:4 * b + 4, t * 32:t * 32 + 32, :] = out.reshape(4, 32, 256)
    for cb in range(4):
        n = nrm[:, 8 * cb:8 * cb + 8, :].reshape(256, D).astype(BF)
        k = (cb - pos[0] + 4) % 4
        for t in range(3):
            out = tdot(w_ref[:, t * 256 + 128:t * 256 + 256], n).astype(BF).reshape(2, 2, 32, 256)
            for hp in range(2):
                all_ref[k, (hp + pos[1]) % 2, :, t * 32:t * 32 + 32, :] = out[hp]
    for k in range(4):
        outs[k][...] = all_ref[k]


def first_kernel(pos, x_hbm, g_hbm, w_hbm, c_ref, s0, s1, s2, s3, nrm, all_ref, x, g, w, sems):
    copies = [pltpu.make_async_copy(g_hbm, g, sems.at[0]), pltpu.make_async_copy(w_hbm.at[0], w, sems.at[1]), pltpu.make_async_copy(x_hbm, x, sems.at[2])]
    for copy in copies:
        copy.start()
    for copy in copies:
        copy.wait()
    project(lambda b: x[8 * b:8 * b + 8].reshape(256, D).astype(F32), pos, g[0:1], w, c_ref, (s0, s1, s2, s3), nrm, all_ref)


def finish(layer, x_ref, hc_ref, hv_ref, wo_ref, gain_ref, wu_ref, wd, ready, mix, put):
    cdot = lambda h, w: lax.dot_general(h, w, (((0,), (0,)), ((), ())), preferred_element_type=F32)
    for cb in range(4):
        h = hv_ref[4 * cb:4 * cb + 4].reshape(128, 256)
        mix[:, 8 * cb:8 * cb + 8, :] = cdot(h, wo_ref[layer, 128:256, :]).reshape(32, 8, D)
    ready()
    for b in range(4):
        h = hc_ref[4 * b:4 * b + 4].reshape(128, 256)
        mixed = cdot(h, wo_ref[layer, 0:128, :]) + x_ref[8 * b:8 * b + 8].reshape(256, D).astype(F32)
        mixed = mixed + mix[8 * b:8 * b + 8].reshape(256, D)
        n2 = norm(mixed, gain_ref[layer:layer + 1]).astype(BF)
        up = jnp.dot(n2, wu_ref[layer], preferred_element_type=F32)
        act = 0.5 * up * (1.0 + jnp.tanh(0.7978845608028654 * (up + 0.044715 * (up * up * up))))
        out = mixed + jnp.dot(act.astype(BF), wd[...], preferred_element_type=F32)
        put(b, out.astype(BF))


def mid_kernel(layer, pos, x_ref, hc_ref, hv_ref, wo_ref, gm_ref, wu_ref, wd_hbm, ga_ref, w_hbm, y_hbm, c_ref, s0, s1, s2, s3, mix, all_ref, wd, y, sems, w):
    loads = [pltpu.make_async_copy(wd_hbm.at[layer], wd, sems.at[0]), pltpu.make_async_copy(w_hbm.at[layer + 1], w, sems.at[1])]
    save = pltpu.make_async_copy(y, y_hbm, sems.at[2])
    for copy in loads:
        copy.start()

    def ready():
        for copy in loads:
            copy.wait()

    def put(b, v):
        y[8 * b:8 * b + 8] = v.reshape(8, 32, D)

    finish(layer, x_ref, hc_ref, hv_ref, wo_ref, gm_ref, wu_ref, wd, ready, mix, put)
    save.start()
    project(lambda b: y[8 * b:8 * b + 8].reshape(256, D).astype(F32), pos, ga_ref[layer + 1:layer + 2], w, c_ref, (s0, s1, s2, s3), mix, all_ref)
    save.wait()


def last_kernel(layer, x_ref, hc_ref, hv_ref, wo_ref, gm_ref, wu_ref, wd_hbm, y_ref, mix, wd, sems):
    load = pltpu.make_async_copy(wd_hbm.at[layer], wd, sems.at[0])
    load.start()

    def put(b, v):
        y_ref[8 * b:8 * b + 8] = v.reshape(8, 32, D)

    finish(layer, x_ref, hc_ref, hv_ref, wo_ref, gm_ref, wu_ref, wd, load.wait, mix, put)


VM = pl.BlockSpec(memory_space=pltpu.VMEM)
HB = pl.BlockSpec(memory_space=pltpu.HBM)
SM = pl.BlockSpec(memory_space=pltpu.SMEM)
ACROSS = jax.ShapeDtypeStruct((16, 96, 256), BF)
HALF = jax.ShapeDtypeStruct((4, 2, 96, 256), BF)
BLOCK = jax.ShapeDtypeStruct((2, 2, 96, 256), BF)
STATE = jax.ShapeDtypeStruct((32, 32, D), BF)
HBM_STATE = pltpu.HBM((32, 32, D), BF)
SEMS = pltpu.SemaphoreType.DMA((3,))


def call(kernel, specs, outs, out_specs, scratch, flops, limit, *args):
    return pl.pallas_call(
        kernel, out_shape=outs, in_specs=specs, out_specs=out_specs,
        scratch_shapes=scratch, compiler_params=pltpu.CompilerParams(vmem_limit_bytes=limit << 20),
        cost_estimate=pl.CostEstimate(flops=flops, transcendentals=0, bytes_accessed=1 << 20),
    )(*args)


def far_memory(x):
    return pltpu.with_memory_space_constraint(x, pltpu.HBM)


def attention_scratch(n):
    return [pltpu.VMEM((n * 256, 128), BF), pltpu.VMEM((48, n * 256), BF), pltpu.VMEM((80, n * 256), BF)]


def shards(frame, gain_attn, w_qkv, w_out, gain_mlp, w_up, w_down):
    bind = lambda f, layer: (lambda *refs: f(layer, *refs))
    vm = lambda *shape, dtype=BF: pltpu.VMEM(shape, dtype)
    pos = jnp.stack([lax.axis_index("x"), lax.axis_index("yh")]).astype(jnp.int32)
    shift = lambda value, axis, k, size: lax.ppermute(value, axis, [(i, (i + k) % size) for i in range(size)])
    state = frame
    work = [vm(32, 32, D, dtype=F32), vm(4, 2, 2, 96, 256)]
    c, *s = call(first_kernel, [SM] + [HB] * 3, (ACROSS,) + (BLOCK,) * 4, (VM,) * 5, work + [vm(32, 32, D), vm(LAYERS, D, dtype=F32), vm(D, 3 * D), SEMS], 2 << 30, 12, pos, *map(far_memory, (state, gain_attn, w_qkv)))
    for layer in range(LAYERS):
        c = lax.all_to_all(c, COL, 0, 0, tiled=True)
        r = [s[0]] + [shift(s[k], "x", k, 4) for k in (1, 2, 3)]
        near, far = call(split_kernel, [VM] * 4, (HALF,) * 2, (VM,) * 2, [], 1 << 28, 4, *r)
        far = shift(far, "yh", 1, 2)
        hc = call(across_kernel, [VM], jax.ShapeDtypeStruct((16, 32, 256), BF), VM, attention_scratch(16), 32 << 30, 16, c)
        hc = lax.all_to_all(hc, COL, 0, 0, tiled=True)
        hv = call(down_attend_kernel, [SM] + [VM] * 2, jax.ShapeDtypeStruct((8, 2, 32, 256), BF), VM, attention_scratch(8) * 2, 16 << 30, 16, pos, near, far)
        hv = lax.all_to_all(hv, ROW, 0, 0, tiled=True).reshape(16, 32, 256)
        rest = (state, hc, hv, w_out, gain_mlp, w_up, far_memory(w_down))
        specs = [VM] * 6 + [HB]
        if layer + 1 < LAYERS:
            state, c, *s = call(bind(mid_kernel, layer), [SM] + specs + [VM, HB], (HBM_STATE, ACROSS) + (BLOCK,) * 4, (HB,) + (VM,) * 5, work + [vm(4 * D, D), vm(32, 32, D), SEMS, vm(D, 3 * D)], 6 << 30, 24, pos, *rest, gain_attn, far_memory(w_qkv))
        else:
            state = call(bind(last_kernel, layer), specs, STATE, VM, work[:1] + [vm(4 * D, D), SEMS], 4 << 30, 24, *rest)
    return state


def solution(mesh):
    torus = Mesh(mesh.devices.reshape(4, 2, mesh.shape["col"]), ("x", "yh", "col"))
    placed = (P(ROW, COL, None), P(), P(), P(), P(), P(), P())
    return jax.shard_map(
        shards, mesh=torus, in_specs=placed, out_specs=P(ROW, COL, None), check_vma=False
    )
```

time: 410 us -> 411 us (level)
  blocking collectives: 0 us -> 29.7 us
  waiting for transfers between devices: 33.5 us -> 17.2 us
  local copies, waits for them, and re-layouts: 9.31 us -> 0.04 us
    all_to_all x8 -> x4, waiting for transfers between devices: 33.5 us -> 0.01 us  [the longest x2 0.01 us: shards(): c = lax.all_to_all(c, COL, 0, 0, tiled=True)]
    all_to_all x0 -> x2, blocking collectives: none -> 29.7 us  [shards(): hc = lax.all_to_all(hc, COL, 0, 0, tiled=True)]
    all_to_all x8 -> x4, starting transfers between devices: 48.4 us -> 27.5 us  [the longest x2 14.7 us: shards(): hv = lax.all_to_all(hv, ROW, 0, 0, tiled=True).reshape(16, 32, 256)]
    ppermute x0 -> x8, starting transfers between devices: none -> 17.4 us  [shards(): lax.ppermute(value, axis, [(i, (i + k) % size) for i in range(size)])]
    ppermute x0 -> x8, waiting for transfers between devices: none -> 17.2 us  [shards(): lax.ppermute(value, axis, [(i, (i + k) % size) for i in range(size)])]
    unnamed x40 -> x12, local copies, waits for them, and re-layouts: 9.31 us -> 0.04 us
    pallas_call x11 -> x9, Pallas kernels: 317 us -> 318 us  [call(): pl.pallas_call(kernel, out_shape=outs, in_specs=specs, out_specs=out_spec...]
  transfers between devices with their start and end apart: 8 -> 12, of which waited for: 4 -> 6; matrix products, arithmetic and copies ran while one was open for 0% -> 0% of each run, Pallas kernels for 75% -> 74%
where the time goes in v2:
time: 411 us
  Pallas kernels  318 us (77%)
  starting transfers between devices  44.9 us (11%)
  blocking collectives  29.7 us (7%)
  waiting for transfers between devices  17.2 us (4%)
    pallas_call x9, Pallas kernels, call(): pl.pallas_call(kernel, out_shape=outs, in_specs=specs, out_specs=out_spec...  318 us
    all_to_all x2, blocking collectives, shards(): hc = lax.all_to_all(hc, COL, 0, 0, tiled=True)  29.7 us
    ppermute x8, starting transfers between devices, shards(): lax.ppermute(value, axis, [(i, (i + k) % size) for i in range(size)])  17.4 us
    ppermute x8, waiting for transfers between devices, shards(): lax.ppermute(value, axis, [(i, (i + k) % size) for i in range(size)])  17.2 us
    all_to_all x2, starting transfers between devices, shards(): hv = lax.all_to_all(hv, ROW, 0, 0, tiled=True).reshape(16, 32, 256)  14.7 us
    all_to_all x2, starting transfers between devices, shards(): c = lax.all_to_all(c, COL, 0, 0, tiled=True)  12.7 us
  transfers between devices with their start and end apart: 12, of which 6 were waited for; matrix products, arithmetic and copies ran while one was open for 0% of the time, Pallas kernels for 74%

profile of v2, /device:TPU:1, one launch (start us, length us, event | category | flops | bytes accessed | tf_op | source)
XLA Modules:
  0.0 410.6 jit_solution(8985781255874784192)
XLA Ops:
  0.0 0.1 pad_add_fusion.pos.refs_0_
  0.1 3.8 shard_map.73
  3.9 2.1 collective-permute-start
  6.0 2.5 collective-permute-start.1
  8.4 1.1 collective-permute-start.2
  9.6 1.9 collective-permute-done.refs_1_
  11.5 5.5 %collective-permute-done.1.refs_2_ = bf16[2,2,96,256]{3,2,1,0:T(8,128)(2,1)S(1)} collective-permute-done((bf16[2,2,96,256]{3,2,1,0:T(8,128)(2,1)S(1)}, bf16[2,2,96,256]{3,2,1,0:T(8,128)(2,1)S(1)}, u32[]{:S(2)}, u32[]{:S(2)}) %collective-permute-start.1) | collective-permute-done | bytes 196640 | tf_op jit(solution)/shard_map/ppermute | solution.py:270
  16.9 0.0 collective-permute-done.2.refs_3_
  16.9 0.1 shard_map.75
  17.0 3.0 collective-permute-start.3
  20.0 7.2 %all-to-all-start = ((bf16[16,96,256]{2,1,0:T(8,128)(2,1)}), bf16[16,96,256]{2,1,0:T(8,128)(2,1)S(1)}, u32[]{:S(2)}, u32[]{:S(2)}) async-start(bf16[16,96,256]{2,1,0:T(8,128)(2,1)} %get-tuple-element.20), calls=%async_computation | async-start | bytes 1572864 | tf_op jit(solution)/shard_map/all_to_all | solution.py:275
  27.2 0.5 collective-permute-done.3.far
  27.7 51.6 %shard_map.76 = bf16[8,2,32,256]{3,2,1,0:T(8,128)(2,1)} custom-call(s32[2]{0:T(128)S(1)} %pad_add_fusion.pos.refs_0_, bf16[4,2,96,256]{3,2,1,0:T(8,128)(2,1)S(1)} %get-tuple-element.25.near, bf16[4,2,96,256]{3,2,1,0:T(8,128)(2,1)S(1)} %collective-permute-done.3.far), custom_call_target="tpu_custom_call" | custom-call | flops 17179869184 | bytes 1048576 | tf_op jit(solution)/shard_map/pallas_call | solution.py:251
  79.4 0.0 all-to-all-done.a_ref
  79.4 7.4 %all-to-all-start.2 = ((bf16[8,2,32,256]{3,2,1,0:T(8,128)(2,1)}), bf16[8,2,32,256]{3,2,1,0:T(8,128)(2,1)S(1)}, u32[]{:S(2)}, u32[]{:S(2)}) async-start(bf16[8,2,32,256]{3,2,1,0:T(8,128)(2,1)} %shard_map.76), calls=%async_computation.2 | async-start | bytes 524288 | tf_op jit(solution)/shard_map/all_to_all | solution.py:282
  86.8 0.0 copy-start
  86.8 0.0 copy-start.2
  86.8 0.0 copy-start.3
  86.8 0.0 copy-start.4
  86.8 99.9 %shard_map.74 = bf16[16,32,256]{2,1,0:T(8,128)(2,1)S(1)} custom-call(bf16[16,96,256]{2,1,0:T(8,128)(2,1)S(1)} %all-to-all-done.a_ref), custom_call_target="tpu_custom_call" | custom-call | flops 34359738368 | bytes 1048576 | tf_op jit(solution)/shard_map/pallas_call | solution.py:251
  186.7 0.0 copy-start.1
  186.7 0.0 all-to-all-done.2
  186.7 15.7 %all_to_all.30.refs_2_ = bf16[16,32,256]{2,1,0:T(8,128)(2,1)S(1)} all-to-all(bf16[16,32,256]{2,1,0:T(8,128)(2,1)S(1)} %shard_map.74), channel_id=1, replica_groups=mesh['x'=4,'yh'=2,'col'=16] {'col'}, dimensions={0} | all-to-all | bytes 524288 | tf_op jit(solution)/shard_map/all_to_all | solution.py:280
  202.4 0.0 copy-done
  202.4 0.0 copy-done.2
  202.4 0.0 copy-done.3
  202.4 0.0 copy-done.4
  202.4 0.0 copy-done.1
  202.4 6.6 %shard_map.77 = (bf16[32,32,256]{2,1,0:T(8,128)(2,1)}, bf16[16,96,256]{2,1,0:T(8,128)(2,1)}, bf16[2,2,96,256]{3,2,1,0:T(8,128)(2,1)S(1)}, bf16[2,2,96,256]{3,2,1...) custom-call(s32[2]{0:T(128)S(1)} %pad_add_fusion.pos.refs_0_, ...), custom_call_target="tpu_custom_call" | custom-call | flops 6442450944 | bytes 1048576 | tf_op jit(solution)/shard_map/pallas_call | solution.py:251
  209.0 1.8 collective-permute-start.4
  210.8 2.4 collective-permute-start.5
  213.2 1.2 collective-permute-start.6
  214.4 2.0 collective-permute-done.4.refs_1_
  216.3 5.1 %collective-permute-done.5.refs_2_ = bf16[2,2,96,256]{3,2,1,0:T(8,128)(2,1)S(1)} collective-permute-done((bf16[2,2,96,256]{3,2,1,0:T(8,128)(2,1)S(1)}, bf16[2,2,96,256]{3,2,1,0:T(8,128)(2,1)S(1)}, u32[]{:S(2)}, u32[]{:S(2)}) %collective-permute-start.5) | collective-permute-done | bytes 196640 | tf_op jit(solution)/shard_map/ppermute | solution.py:270
  221.4 0.0 collective-permute-done.6.refs_3_
  221.5 0.1 shard_map.79
  221.5 3.4 collective-permute-start.7
  224.9 5.5 %all-to-all-start.3 = ((bf16[16,96,256]{2,1,0:T(8,128)(2,1)}), bf16[16,96,256]{2,1,0:T(8,128)(2,1)S(1)}, u32[]{:S(2)}, u32[]{:S(2)}) async-start(bf16[16,96,256]{2,1,0:T(8,128)(2,1)} %get-tuple-element.28), calls=%async_computation.3 | async-start | bytes 1572864 | tf_op jit(solution)/shard_map/all_to_all | solution.py:275
  230.3 2.2 collective-permute-done.7.far
  232.6 51.6 %shard_map.80 = bf16[8,2,32,256]{3,2,1,0:T(8,128)(2,1)} custom-call(s32[2]{0:T(128)S(1)} %pad_add_fusion.pos.refs_0_, bf16[4,2,96,256]{3,2,1,0:T(8,128)(2,1)S(1)} %get-tuple-element.33.near, bf16[4,2,96,256]{3,2,1,0:T(8,128)(2,1)S(1)} %collective-permute-done.7.far), custom_call_target="tpu_custom_call" | custom-call | flops 17179869184 | bytes 1048576 | tf_op jit(solution)/shard_map/pallas_call | solution.py:251
  284.2 0.0 all-to-all-done.3.a_ref
  284.2 7.3 %all-to-all-start.5 = ((bf16[8,2,32,256]{3,2,1,0:T(8,128)(2,1)}), bf16[8,2,32,256]{3,2,1,0:T(8,128)(2,1)S(1)}, u32[]{:S(2)}, u32[]{:S(2)}) async-start(bf16[8,2,32,256]{3,2,1,0:T(8,128)(2,1)} %shard_map.80), calls=%async_computation.5 | async-start | bytes 524288 | tf_op jit(solution)/shard_map/all_to_all | solution.py:282
  291.6 100.1 %shard_map.78 = bf16[16,32,256]{2,1,0:T(8,128)(2,1)S(1)} custom-call(bf16[16,96,256]{2,1,0:T(8,128)(2,1)S(1)} %all-to-all-done.3.a_ref), custom_call_target="tpu_custom_call" | custom-call | flops 34359738368 | bytes 1048576 | tf_op jit(solution)/shard_map/pallas_call | solution.py:251
  391.7 0.0 copy-start.5
  391.7 0.0 all-to-all-done.5
  391.7 14.0 %all_to_all.31.refs_1_ = bf16[16,32,256]{2,1,0:T(8,128)(2,1)S(1)} all-to-all(bf16[16,32,256]{2,1,0:T(8,128)(2,1)S(1)} %shard_map.78), channel_id=1, replica_groups=mesh['x'=4,'yh'=2,'col'=16] {'col'}, dimensions={0} | all-to-all | bytes 524288 | tf_op jit(solution)/shard_map/all_to_all | solution.py:280
  405.7 0.0 copy-done.5
  405.7 4.7 %shard_map.81 = bf16[32,32,256]{2,1,0:T(8,128)(2,1)} custom-call(bf16[32,32,256]{2,1,0:T(8,128)(2,1)S(1)} %copy-done.5, bf16[16,32,256]{2,1,0:T(8,128)(2,1)S(1)} %all_to_all.31.refs_1_, bf16[16,32,256]{2,1,0:T(8,128)(2,1)S(1)} %bitcast.5, bf16[2,256,256]{2,1,0:T(8,128)(2,1)S(1)} %copy-done.2, f32[2,256]{1,0:T(2,128)S(1)} %copy-done.4, ...), custom_call_target="tpu_custom_call" | custom-call | flops 4294967296 | bytes 1048576 | tf_op jit(solution)/shard_map/pallas_call | solution.py:251
Async XLA Ops:
  3.9 7.6 %collective-permute-start = (bf16[2,2,96,256]{3,2,1,0:T(8,128)(2,1)S(1)}, bf16[2,2,96,256]{3,2,1,0:T(8,128)(2,1)S(1)}, u32[]{:S(2)}, u32[]{:S(2)}) collective-permute-start(bf16[2,2,96,256]{3,2,1,0:T(8,128)(2,1)S(1)} %get-tuple-element.22), channel_id=1, source_target_pairs={{0,32},{32,64},{64,96},{96,0},{1,33},{33,65},{65,97},{97,1},{2,34}... | collective-permute-start | bytes 589832 | tf_op jit(solution)/shard_map/ppermute | solution.py:270
  6.0 11.0 %collective-permute-start.1 = (bf16[2,2,96,256]{3,2,1,0:T(8,128)(2,1)S(1)}, bf16[2,2,96,256]{3,2,1,0:T(8,128)(2,1)S(1)}, u32[]{:S(2)}, u32[]{:S(2)}) collective-permute-start(bf16[2,2,96,256]{3,2,1,0:T(8,128)(2,1)S(1)} %get-tuple-element.23), channel_id=1, source_target_pairs={{0,64},{32,96},{64,0},{96,32},{1,65},{33,97},{65,1},{97,33},{2,66}... | collective-permute-start | bytes 589832 | tf_op jit(solution)/shard_map/ppermute | solution.py:270
  8.4 8.5 %collective-permute-start.2 = (bf16[2,2,96,256]{3,2,1,0:T(8,128)(2,1)S(1)}, bf16[2,2,96,256]{3,2,1,0:T(8,128)(2,1)S(1)}, u32[]{:S(2)}, u32[]{:S(2)}) collective-permute-start(bf16[2,2,96,256]{3,2,1,0:T(8,128)(2,1)S(1)} %get-tuple-element.24), channel_id=1, source_target_pairs={{0,96},{32,0},{64,32},{96,64},{1,97},{33,1},{65,33},{97,65},{2,98}... | collective-permute-start | bytes 589832 | tf_op jit(solution)/shard_map/ppermute | solution.py:270
  17.0 10.7 %collective-permute-start.3 = (bf16[4,2,96,256]{3,2,1,0:T(8,128)(2,1)S(1)}, bf16[4,2,96,256]{3,2,1,0:T(8,128)(2,1)S(1)}, u32[]{:S(2)}, u32[]{:S(2)}) collective-permute-start(bf16[4,2,96,256]{3,2,1,0:T(8,128)(2,1)S(1)} %get-tuple-element.26), channel_id=1, source_target_pairs={{0,16},{16,0},{1,17},{17,1},{2,18},{18,2},{3,19},{19,3},{4,20},{20... | collective-permute-start | bytes 1179656 | tf_op jit(solution)/shard_map/ppermute | solution.py:270
  20.0 59.4 %all-to-all-start = ((bf16[16,96,256]{2,1,0:T(8,128)(2,1)}), bf16[16,96,256]{2,1,0:T(8,128)(2,1)S(1)}, u32[]{:S(2)}, u32[]{:S(2)}) async-start(bf16[16,96,256]{2,1,0:T(8,128)(2,1)} %get-tuple-element.20), calls=%async_computation | async-start | bytes 1572864 | tf_op jit(solution)/shard_map/all_to_all | solution.py:275
  79.4 107.3 %all-to-all-start.2 = ((bf16[8,2,32,256]{3,2,1,0:T(8,128)(2,1)}), bf16[8,2,32,256]{3,2,1,0:T(8,128)(2,1)S(1)}, u32[]{:S(2)}, u32[]{:S(2)}) async-start(bf16[8,2,32,256]{3,2,1,0:T(8,128)(2,1)} %shard_map.76), calls=%async_computation.2 | async-start | bytes 524288 | tf_op jit(solution)/shard_map/all_to_all | solution.py:282
  86.8 115.6 %copy-start = (bf16[2,256,1024]{2,1,0:T(8,128)(2,1)S(1)}, bf16[2,256,1024]{2,1,0:T(8,128)(2,1)}, u32[]{:S(2)}) copy-start(bf16[2,256,1024]{2,1,0:T(8,128)(2,1)} %refs_5_.3) | copy-start | bytes 3145732
  86.8 115.6 %copy-start.2 = (bf16[2,256,256]{2,1,0:T(8,128)(2,1)S(1)}, bf16[2,256,256]{2,1,0:T(8,128)(2,1)}, u32[]{:S(2)}) copy-start(bf16[2,256,256]{2,1,0:T(8,128)(2,1)} %refs_3_.1) | copy-start | bytes 786436
  86.8 115.6 %copy-start.3 = (f32[2,256]{1,0:T(2,128)S(1)}, f32[2,256]{1,0:T(2,128)}, u32[]{:S(2)}) copy-start(f32[2,256]{1,0:T(2,128)} %refs_8_.1) | copy-start | bytes 6148
  86.8 115.6 %copy-start.4 = (f32[2,256]{1,0:T(2,128)S(1)}, f32[2,256]{1,0:T(2,128)}, u32[]{:S(2)}) copy-start(f32[2,256]{1,0:T(2,128)} %refs_4_.3) | copy-start | bytes 6148
  186.7 15.7 %copy-start.1 = (bf16[32,32,256]{2,1,0:T(8,128)(2,1)S(1)}, bf16[32,32,256]{2,1,0:T(8,128)(2,1)}, u32[]{:S(2)}) copy-start(bf16[32,32,256]{2,1,0:T(8,128)(2,1)} %refs_1_.1) | copy-start | bytes 1572868
  209.0 7.3 %collective-permute-start.4 = (bf16[2,2,96,256]{3,2,1,0:T(8,128)(2,1)S(1)}, bf16[2,2,96,256]{3,2,1,0:T(8,128)(2,1)S(1)}, u32[]{:S(2)}, u32[]{:S(2)}) collective-permute-start(bf16[2,2,96,256]{3,2,1,0:T(8,128)(2,1)S(1)} %get-tuple-element.30), channel_id=1, source_target_pairs={{0,32},{32,64},{64,96},{96,0},{1,33},{33,65},{65,97},{97,1},{2,34}... | collective-permute-start | bytes 589832 | tf_op jit(solution)/shard_map/ppermute | solution.py:270
  210.8 10.7 %collective-permute-start.5 = (bf16[2,2,96,256]{3,2,1,0:T(8,128)(2,1)S(1)}, bf16[2,2,96,256]{3,2,1,0:T(8,128)(2,1)S(1)}, u32[]{:S(2)}, u32[]{:S(2)}) collective-permute-start(bf16[2,2,96,256]{3,2,1,0:T(8,128)(2,1)S(1)} %get-tuple-element.31), channel_id=1, source_target_pairs={{0,64},{32,96},{64,0},{96,32},{1,65},{33,97},{65,1},{97,33},{2,66}... | collective-permute-start | bytes 589832 | tf_op jit(solution)/shard_map/ppermute | solution.py:270
  213.2 8.3 %collective-permute-start.6 = (bf16[2,2,96,256]{3,2,1,0:T(8,128)(2,1)S(1)}, bf16[2,2,96,256]{3,2,1,0:T(8,128)(2,1)S(1)}, u32[]{:S(2)}, u32[]{:S(2)}) collective-permute-start(bf16[2,2,96,256]{3,2,1,0:T(8,128)(2,1)S(1)} %get-tuple-element.32), channel_id=1, source_target_pairs={{0,96},{32,0},{64,32},{96,64},{1,97},{33,1},{65,33},{97,65},{2,98}... | collective-permute-start | bytes 589832 | tf_op jit(solution)/shard_map/ppermute | solution.py:270
  221.5 11.1 %collective-permute-start.7 = (bf16[4,2,96,256]{3,2,1,0:T(8,128)(2,1)S(1)}, bf16[4,2,96,256]{3,2,1,0:T(8,128)(2,1)S(1)}, u32[]{:S(2)}, u32[]{:S(2)}) collective-permute-start(bf16[4,2,96,256]{3,2,1,0:T(8,128)(2,1)S(1)} %get-tuple-element.34), channel_id=1, source_target_pairs={{0,16},{16,0},{1,17},{17,1},{2,18},{18,2},{3,19},{19,3},{4,20},{20... | collective-permute-start | bytes 1179656 | tf_op jit(solution)/shard_map/ppermute | solution.py:270
  224.9 59.4 %all-to-all-start.3 = ((bf16[16,96,256]{2,1,0:T(8,128)(2,1)}), bf16[16,96,256]{2,1,0:T(8,128)(2,1)S(1)}, u32[]{:S(2)}, u32[]{:S(2)}) async-start(bf16[16,96,256]{2,1,0:T(8,128)(2,1)} %get-tuple-element.28), calls=%async_computation.3 | async-start | bytes 1572864 | tf_op jit(solution)/shard_map/all_to_all | solution.py:275
  284.2 107.4 %all-to-all-start.5 = ((bf16[8,2,32,256]{3,2,1,0:T(8,128)(2,1)}), bf16[8,2,32,256]{3,2,1,0:T(8,128)(2,1)S(1)}, u32[]{:S(2)}, u32[]{:S(2)}) async-start(bf16[8,2,32,256]{3,2,1,0:T(8,128)(2,1)} %shard_map.80), calls=%async_computation.5 | async-start | bytes 524288 | tf_op jit(solution)/shard_map/all_to_all | solution.py:282
  391.7 14.0 %copy-start.5 = (bf16[32,32,256]{2,1,0:T(8,128)(2,1)S(1)}, bf16[32,32,256]{2,1,0:T(8,128)(2,1)}, u32[]{:S(2)}) copy-start(bf16[32,32,256]{2,1,0:T(8,128)(2,1)} %get-tuple-element.27.refs_0_) | copy-start | bytes 1572868

commit v3 on v2

--- a/solution.py
+++ b/solution.py
@@ -135,21 +135,22 @@
     attend(1, 16, lambda it, s, lo, hi: a_ref[s, lo:hi, :], put, [sc], 2)
 
 
-def split_kernel(*refs):
+def pair_kernel(near, far, *outs):
     for k in range(4):
-        for e in range(2):
-            refs[4 + e][k] = refs[k][e]
-
-
-def down_attend_kernel(pos, near, far, o_ref, *sc):
-    def get(it, s, lo, hi):
-        return (far if s % 2 else near)[s // 2, it, lo:hi, :]
+        outs[k][0] = near[k]
+        outs[k][1] = far[k]
+
+
+def down_attend_kernel(p0, p1, p2, p3, near, far, all_ref, *sc):
+    blocks = (p0, p1, p2, p3)
 
     def put(it, s, v):
-        k, e = s // 2, s % 2
-        o_ref[2 * ((pos[0] - k + 4) % 4) + (pos[1] + e) % 2, it] = v
-
-    attend(2, 8, get, put, [sc[0:3], sc[3:6]], 2)
+        all_ref[s, it] = v
+
+    attend(2, 8, lambda it, s, lo, hi: blocks[s // 2][s % 2, it, lo:hi, :], put, [sc[0:3], sc[3:6]], 2)
+    for k in range(4):
+        near[k] = all_ref[2 * k]
+        far[k] = all_ref[2 * k + 1]
 
 
 def norm(x, gain):
@@ -162,7 +163,7 @@
     return lax.dot_general(a, b, (((0,), (1,)), ((), ())), preferred_element_type=F32)
 
 
-def project(get, pos, gain, w_ref, c_ref, outs, nrm, all_ref):
+def project(get, pos, gain, w_ref, c_ref, sends, nrm, sent):
     for b in range(4):
         n = norm(get(b), gain)
         nrm[8 * b:8 * b + 8] = n.reshape(8, 32, D)
@@ -170,46 +171,56 @@
         for t in range(3):
             out = tdot(w_ref[:, t * 256:t * 256 + 128], n).astype(BF)
             c_ref[4 * b:4 * b + 4, t * 32:t * 32 + 32, :] = out.reshape(4, 32, 256)
+    sent()
     for cb in range(4):
         n = nrm[:, 8 * cb:8 * cb + 8, :].reshape(256, D).astype(BF)
         k = (cb - pos[0] + 4) % 4
         for t in range(3):
             out = tdot(w_ref[:, t * 256 + 128:t * 256 + 256], n).astype(BF).reshape(2, 2, 32, 256)
             for hp in range(2):
-                all_ref[k, (hp + pos[1]) % 2, :, t * 32:t * 32 + 32, :] = out[hp]
-    for k in range(4):
-        outs[k][...] = all_ref[k]
-
-
-def first_kernel(pos, x_hbm, g_hbm, w_hbm, c_ref, s0, s1, s2, s3, nrm, all_ref, x, g, w, sems):
+                sends[(hp + pos[1]) % 2, k, :, t * 32:t * 32 + 32, :] = out[hp]
+
+
+def first_kernel(pos, x_hbm, g_hbm, w_hbm, c_hbm, near, far, nrm, sends, x, g, w, sems, c):
     copies = [pltpu.make_async_copy(g_hbm, g, sems.at[0]), pltpu.make_async_copy(w_hbm.at[0], w, sems.at[1]), pltpu.make_async_copy(x_hbm, x, sems.at[2])]
+    save = pltpu.make_async_copy(c, c_hbm, sems.at[3])
     for copy in copies:
         copy.start()
     for copy in copies:
         copy.wait()
-    project(lambda b: x[8 * b:8 * b + 8].reshape(256, D).astype(F32), pos, g[0:1], w, c_ref, (s0, s1, s2, s3), nrm, all_ref)
-
-
-def finish(layer, x_ref, hc_ref, hv_ref, wo_ref, gain_ref, wu_ref, wd, ready, mix, put):
+    project(lambda b: x[8 * b:8 * b + 8].reshape(256, D).astype(F32), pos, g[0:1], w, c, sends, nrm, save.start)
+    near[...] = sends[0]
+    far[...] = sends[1]
+    save.wait()
+
+
+def finish(layer, pos, x_ref, hc_ref, heads, wo_ref, gain_ref, wu_ref, wd, ready, mix, hv, n2, put):
     cdot = lambda h, w: lax.dot_general(h, w, (((0,), (0,)), ((), ())), preferred_element_type=F32)
+    for k in range(4):
+        at = 2 * ((pos[0] + k) % 4)
+        hv[at + pos[1]] = heads[k][0]
+        hv[at + 1 - pos[1]] = heads[k][1]
     for cb in range(4):
-        h = hv_ref[4 * cb:4 * cb + 4].reshape(128, 256)
+        h = hv[2 * cb:2 * cb + 2].reshape(128, 256)
         mix[:, 8 * cb:8 * cb + 8, :] = cdot(h, wo_ref[layer, 128:256, :]).reshape(32, 8, D)
+    for b in range(4):
+        rows = slice(8 * b, 8 * b + 8)
+        h = hc_ref[4 * b:4 * b + 4].reshape(128, 256)
+        mixed = cdot(h, wo_ref[layer, 0:128, :]) + x_ref[rows].reshape(256, D).astype(F32)
+        mixed = mixed + mix[rows].reshape(256, D)
+        mix[rows] = mixed.reshape(8, 32, D)
+        n2[256 * b:256 * b + 256, :] = norm(mixed, gain_ref[layer:layer + 1]).astype(BF)
     ready()
     for b in range(4):
-        h = hc_ref[4 * b:4 * b + 4].reshape(128, 256)
-        mixed = cdot(h, wo_ref[layer, 0:128, :]) + x_ref[8 * b:8 * b + 8].reshape(256, D).astype(F32)
-        mixed = mixed + mix[8 * b:8 * b + 8].reshape(256, D)
-        n2 = norm(mixed, gain_ref[layer:layer + 1]).astype(BF)
-        up = jnp.dot(n2, wu_ref[layer], preferred_element_type=F32)
+        up = jnp.dot(n2[256 * b:256 * b + 256, :], wu_ref[layer], preferred_element_type=F32)
         act = 0.5 * up * (1.0 + jnp.tanh(0.7978845608028654 * (up + 0.044715 * (up * up * up))))
-        out = mixed + jnp.dot(act.astype(BF), wd[...], preferred_element_type=F32)
-        put(b, out.astype(BF))
-
-
-def mid_kernel(layer, pos, x_ref, hc_ref, hv_ref, wo_ref, gm_ref, wu_ref, wd_hbm, ga_ref, w_hbm, y_hbm, c_ref, s0, s1, s2, s3, mix, all_ref, wd, y, sems, w):
+        out = jnp.dot(act.astype(BF), wd[...], preferred_element_type=F32)
+        put(b, (mix[8 * b:8 * b + 8].reshape(256, D) + out).astype(BF))
+
+
+def mid_kernel(layer, pos, x_ref, hc_ref, h0, h1, h2, h3, wo_ref, gm_ref, wu_ref, wd_hbm, ga_ref, w_hbm, y_hbm, c_hbm, near, far, mix, sends, wd, hv, n2, sems, y, w, c):
     loads = [pltpu.make_async_copy(wd_hbm.at[layer], wd, sems.at[0]), pltpu.make_async_copy(w_hbm.at[layer + 1], w, sems.at[1])]
-    save = pltpu.make_async_copy(y, y_hbm, sems.at[2])
+    saves = [pltpu.make_async_copy(y, y_hbm, sems.at[2]), pltpu.make_async_copy(c, c_hbm, sems.at[3])]
     for copy in loads:
         copy.start()
 
@@ -220,31 +231,39 @@
     def put(b, v):
         y[8 * b:8 * b + 8] = v.reshape(8, 32, D)
 
-    finish(layer, x_ref, hc_ref, hv_ref, wo_ref, gm_ref, wu_ref, wd, ready, mix, put)
-    save.start()
-    project(lambda b: y[8 * b:8 * b + 8].reshape(256, D).astype(F32), pos, ga_ref[layer + 1:layer + 2], w, c_ref, (s0, s1, s2, s3), mix, all_ref)
-    save.wait()
-
-
-def last_kernel(layer, x_ref, hc_ref, hv_ref, wo_ref, gm_ref, wu_ref, wd_hbm, y_ref, mix, wd, sems):
+    def sent():
+        for copy in saves:
+            copy.start()
+
+    finish(layer, pos, x_ref, hc_ref, (h0, h1, h2, h3), wo_ref, gm_ref, wu_ref, wd, ready, mix, hv, n2, put)
+    project(lambda b: y[8 * b:8 * b + 8].reshape(256, D).astype(F32), pos, ga_ref[layer + 1:layer + 2], w, c, sends, mix, sent)
+    near[...] = sends[0]
+    far[...] = sends[1]
+    for copy in saves:
+        copy.wait()
+
+
+def last_kernel(layer, pos, x_ref, hc_ref, h0, h1, h2, h3, wo_ref, gm_ref, wu_ref, wd_hbm, y_ref, mix, wd, hv, n2, sems):
     load = pltpu.make_async_copy(wd_hbm.at[layer], wd, sems.at[0])
     load.start()
 
     def put(b, v):
         y_ref[8 * b:8 * b + 8] = v.reshape(8, 32, D)
 
-    finish(layer, x_ref, hc_ref, hv_ref, wo_ref, gm_ref, wu_ref, wd, load.wait, mix, put)
+    finish(layer, pos, x_ref, hc_ref, (h0, h1, h2, h3), wo_ref, gm_ref, wu_ref, wd, load.wait, mix, hv, n2, put)
 
 
 VM = pl.BlockSpec(memory_space=pltpu.VMEM)
 HB = pl.BlockSpec(memory_space=pltpu.HBM)
 SM = pl.BlockSpec(memory_space=pltpu.SMEM)
-ACROSS = jax.ShapeDtypeStruct((16, 96, 256), BF)
+REPLY = jax.ShapeDtypeStruct((2, 2, 32, 256), BF)
+HALF_REPLY = jax.ShapeDtypeStruct((4, 2, 32, 256), BF)
 HALF = jax.ShapeDtypeStruct((4, 2, 96, 256), BF)
 BLOCK = jax.ShapeDtypeStruct((2, 2, 96, 256), BF)
 STATE = jax.ShapeDtypeStruct((32, 32, D), BF)
+HBM_ACROSS = pltpu.HBM((16, 96, 256), BF)
 HBM_STATE = pltpu.HBM((32, 32, D), BF)
-SEMS = pltpu.SemaphoreType.DMA((3,))
+SEMS = pltpu.SemaphoreType.DMA((4,))
 
 
 def call(kernel, specs, outs, out_specs, scratch, flops, limit, *args):
@@ -269,23 +288,28 @@
     pos = jnp.stack([lax.axis_index("x"), lax.axis_index("yh")]).astype(jnp.int32)
     shift = lambda value, axis, k, size: lax.ppermute(value, axis, [(i, (i + k) % size) for i in range(size)])
     state = frame
-    work = [vm(32, 32, D, dtype=F32), vm(4, 2, 2, 96, 256)]
-    c, *s = call(first_kernel, [SM] + [HB] * 3, (ACROSS,) + (BLOCK,) * 4, (VM,) * 5, work + [vm(32, 32, D), vm(LAYERS, D, dtype=F32), vm(D, 3 * D), SEMS], 2 << 30, 12, pos, *map(far_memory, (state, gain_attn, w_qkv)))
+    sends = vm(2, 4, 2, 96, 256)
+    mix = vm(32, 32, D, dtype=F32)
+    mlp = [vm(4 * D, D), vm(8, 2, 32, 256), vm(4 * D, D), SEMS]
+    buffers = [vm(D, 3 * D), vm(16, 96, 256)]
+    c, near, far = call(first_kernel, [SM] + [HB] * 3, (HBM_ACROSS, HALF, HALF), (HB, VM, VM), [mix, sends, vm(32, 32, D), vm(LAYERS, D, dtype=F32), buffers[0], SEMS, buffers[1]], 2 << 30, 12, pos, *map(far_memory, (state, gain_attn, w_qkv)))
     for layer in range(LAYERS):
+        far = shift(far, "yh", 1, 2)
         c = lax.all_to_all(c, COL, 0, 0, tiled=True)
-        r = [s[0]] + [shift(s[k], "x", k, 4) for k in (1, 2, 3)]
-        near, far = call(split_kernel, [VM] * 4, (HALF,) * 2, (VM,) * 2, [], 1 << 28, 4, *r)
+        r = call(pair_kernel, [VM] * 2, (BLOCK,) * 4, (VM,) * 4, [], 1 << 28, 4, near, far)
+        r = [r[0]] + [shift(r[k], "x", k, 4) for k in (1, 2, 3)]
+        hc = call(across_kernel, [VM], jax.ShapeDtypeStruct((16, 32, 256), BF), VM, attention_scratch(16), 32 << 30, 16, c)
+        near, far = call(down_attend_kernel, [VM] * 4, (HALF_REPLY,) * 2, (VM,) * 2, [vm(8, 2, 32, 256)] + attention_scratch(8) * 2, 16 << 30, 16, *r)
         far = shift(far, "yh", 1, 2)
-        hc = call(across_kernel, [VM], jax.ShapeDtypeStruct((16, 32, 256), BF), VM, attention_scratch(16), 32 << 30, 16, c)
         hc = lax.all_to_all(hc, COL, 0, 0, tiled=True)
-        hv = call(down_attend_kernel, [SM] + [VM] * 2, jax.ShapeDtypeStruct((8, 2, 32, 256), BF), VM, attention_scratch(8) * 2, 16 << 30, 16, pos, near, far)
-        hv = lax.all_to_all(hv, ROW, 0, 0, tiled=True).reshape(16, 32, 256)
-        rest = (state, hc, hv, w_out, gain_mlp, w_up, far_memory(w_down))
-        specs = [VM] * 6 + [HB]
+        o = call(pair_kernel, [VM] * 2, (REPLY,) * 4, (VM,) * 4, [], 1 << 28, 4, near, far)
+        o = [o[0]] + [shift(o[k], "x", 4 - k, 4) for k in (1, 2, 3)]
+        rest = (pos, state, hc, *o, w_out, gain_mlp, w_up, far_memory(w_down))
+        specs = [SM] + [VM] * 9 + [HB]
         if layer + 1 < LAYERS:
-            state, c, *s = call(bind(mid_kernel, layer), [SM] + specs + [VM, HB], (HBM_STATE, ACROSS) + (BLOCK,) * 4, (HB,) + (VM,) * 5, work + [vm(4 * D, D), vm(32, 32, D), SEMS, vm(D, 3 * D)], 6 << 30, 24, pos, *rest, gain_attn, far_memory(w_qkv))
+            state, c, near, far = call(bind(mid_kernel, layer), specs + [VM, HB], (HBM_STATE, HBM_ACROSS, HALF, HALF), (HB, HB, VM, VM), [mix, sends] + mlp + [vm(32, 32, D)] + buffers, 6 << 30, 24, *rest, gain_attn, far_memory(w_qkv))
         else:
-            state = call(bind(last_kernel, layer), specs, STATE, VM, work[:1] + [vm(4 * D, D), SEMS], 4 << 30, 24, *rest)
+            state = call(bind(last_kernel, layer), specs, STATE, VM, [mix] + mlp, 4 << 30, 24, *rest)
     return state
 
 

time: 411 us -> 423 us (1.029)
  waiting for transfers between devices: 17.2 us -> 54.2 us
  blocking collectives: 29.7 us -> 0 us
    ppermute x8 -> x16, waiting for transfers between devices: 17.2 us -> 54.1 us  [shards(): lax.ppermute(value, axis, [(i, (i + k) % size) for i in range(size)])]
    all_to_all x2 -> x0, blocking collectives: 29.7 us -> none  [shards(): hc = lax.all_to_all(hc, COL, 0, 0, tiled=True)]
    ppermute x8 -> x16, starting transfers between devices: 17.4 us -> 21.1 us  [shards(): lax.ppermute(value, axis, [(i, (i + k) % size) for i in range(size)])]
    pallas_call x9 -> x11, Pallas kernels: 318 us -> 316 us  [call(): pl.pallas_call(kernel, out_shape=outs, in_specs=specs, out_specs=out_spec...]
  transfers between devices with their start and end apart: 12 -> 20, of which waited for: 6 -> 10; matrix products, arithmetic and copies ran while one was open for 0% -> 0% of each run, Pallas kernels for 74% -> 72%
where the time goes in v3:
time: 423 us; the launch traced here: 421 us
  Pallas kernels  316 us (75%)
  waiting for transfers between devices  54.2 us (13%)
  starting transfers between devices  48.6 us (11%)
    pallas_call x11, Pallas kernels, call(): pl.pallas_call(kernel, out_shape=outs, in_specs=specs, out_specs=out_spec...  316 us
    ppermute x16, waiting for transfers between devices, shards(): lax.ppermute(value, axis, [(i, (i + k) % size) for i in range(size)])  54.1 us
    ppermute x16, starting transfers between devices, shards(): lax.ppermute(value, axis, [(i, (i + k) % size) for i in range(size)])  21.1 us
    all_to_all x2, starting transfers between devices, shards(): c = lax.all_to_all(c, COL, 0, 0, tiled=True)  15.4 us
    all_to_all x2, starting transfers between devices, shards(): hc = lax.all_to_all(hc, COL, 0, 0, tiled=True)  12.1 us
  transfers between devices with their start and end apart: 20, of which 10 were waited for; matrix products, arithmetic and copies ran while one was open for 0% of the time, Pallas kernels for 72%

profile of v3, /device:TPU:1, one launch (start us, length us, event | category | flops | bytes accessed | tf_op | source)
XLA Modules:
  0.0 420.9 jit_solution(7731097003637416622)
XLA Ops:
  0.0 0.1 pad_add_fusion.pos.refs_0_
  0.1 3.9 shard_map.73
  4.0 7.8 %all-to-all-start = ((bf16[16,96,256]{2,1,0:T(8,128)(2,1)}), bf16[16,96,256]{2,1,0:T(8,128)(2,1)S(1)}, u32[]{:S(2)}, u32[]{:S(2)}) async-start(bf16[16,96,256]{2,1,0:T(8,128)(2,1)} %get-tuple-element.32), calls=%async_computation | async-start | bytes 1572864 | tf_op jit(solution)/shard_map/all_to_all | solution.py:298
  11.8 2.6 collective-permute-start
  14.5 18.2 %collective-permute-done.far = bf16[4,2,96,256]{3,2,1,0:T(8,128)(2,1)S(1)} collective-permute-done((bf16[4,2,96,256]{3,2,1,0:T(8,128)(2,1)S(1)}, bf16[4,2,96,256]{3,2,1,0:T(8,128)(2,1)S(1)}, u32[]{:S(2)}, u32[]{:S(2)}) %collective-permute-start) | collective-permute-done | bytes 393248 | tf_op jit(solution)/shard_map/ppermute | solution.py:289
  32.6 0.1 shard_map.75
  32.7 1.3 collective-permute-start.1
  34.0 2.5 collective-permute-start.2
  36.4 1.2 collective-permute-start.3
  37.6 0.0 all-to-all-done.a_ref
  37.6 100.6 %shard_map.74 = bf16[16,32,256]{2,1,0:T(8,128)(2,1)} custom-call(bf16[16,96,256]{2,1,0:T(8,128)(2,1)S(1)} %all-to-all-done.a_ref), custom_call_target="tpu_custom_call" | custom-call | flops 34359738368 | bytes 1048576 | tf_op jit(solution)/shard_map/pallas_call | solution.py:270
  138.2 6.1 %all-to-all-start.1 = ((bf16[16,32,256]{2,1,0:T(8,128)(2,1)}), bf16[16,32,256]{2,1,0:T(8,128)(2,1)S(1)}, u32[]{:S(2)}, u32[]{:S(2)}) async-start(bf16[16,32,256]{2,1,0:T(8,128)(2,1)} %shard_map.74), calls=%async_computation.1 | async-start | bytes 524288 | tf_op jit(solution)/shard_map/all_to_all | solution.py:304
  144.3 0.0 collective-permute-done.1.p1
  144.3 0.0 copy-start
  144.3 50.4 %shard_map.76 = (bf16[4,2,32,256]{3,2,1,0:T(8,128)(2,1)S(1)}, bf16[4,2,32,256]{3,2,1,0:T(8,128)(2,1)S(1)}) custom-call(bf16[2,2,96,256]{3,2,1,0:T(8,128)(2,1)S(1)} %get-tuple-element.35.p0, bf16[2,2,96,256]{3,2,1,0:T(8,128)(2,1)S(1)} %collective-permute-done.1.p1, bf16[2,2,96,256]{3,2,1,0:T(8,128)(2,1)S(1)} %collective-permute-done.2.p2, ...), custom_call_target="tpu_custom_call" | custom-call | flops 17179869184 | bytes 1048576 | tf_op jit(solution)/shard_map/pallas_call | solution.py:270
  194.7 0.0 copy-start.1
  194.7 1.6 collective-permute-start.4
  196.4 4.9 %collective-permute-done.4.far = bf16[4,2,32,256]{3,2,1,0:T(8,128)(2,1)S(1)} collective-permute-done((bf16[4,2,32,256]{3,2,1,0:T(8,128)(2,1)S(1)}, bf16[4,2,32,256]{3,2,1,0:T(8,128)(2,1)S(1)}, u32[]{:S(2)}, u32[]{:S(2)}) %collective-permute-start.4) | collective-permute-done | bytes 131104 | tf_op jit(solution)/shard_map/ppermute | solution.py:289
  201.3 0.1 collective-permute-start.5
  201.4 0.0 copy-start.4
  201.4 0.0 copy-start.3
  201.4 2.1 collective-permute-start.6
  203.4 0.0 collective-permute-start.7
  203.4 1.0 collective-permute-done.5.refs_4_
  204.5 1.6 collective-permute-done.6.refs_5_
  206.1 2.1 collective-permute-done.7.refs_6_
  208.3 5.5 %shard_map.78 = (bf16[32,32,256]{2,1,0:T(8,128)(2,1)}, bf16[16,96,256]{2,1,0:T(8,128)(2,1)}, bf16[4,2,96,256]{3,2,1,0:T(8,128)(2,1)S(1)}, bf16[4,2,96,256]{3,2,1,0:T(8,128)(2,1)S(1)}) custom-call(s32[2]{0:T(128)S(1)} %pad_add_fusion.pos.refs_0_, bf16[32,32,256]{2,1,0:T(8,128)(2,1)S(1)} %copy-done.1, bf16[16,32,256]{2,1,0:T(8,128)(2,1)S(1)} %all-to-all-done.1.refs_2_, ...), custom_call_target="tpu_custom_call" | custom-call | flops 6442450944 | bytes 1048576 | tf_op jit(solution)/shard_map/pallas_call | solution.py:270
  213.8 0.8 copy-done.5
  214.5 7.6 %all-to-all-start.2 = ((bf16[16,96,256]{2,1,0:T(8,128)(2,1)}), bf16[16,96,256]{2,1,0:T(8,128)(2,1)S(1)}, u32[]{:S(2)}, u32[]{:S(2)}) async-start(bf16[16,96,256]{2,1,0:T(8,128)(2,1)} %get-tuple-element.46), calls=%async_computation.2 | async-start | bytes 1572864 | tf_op jit(solution)/shard_map/all_to_all | solution.py:298
  222.1 1.6 collective-permute-start.8
  223.6 18.2 %collective-permute-done.8.far = bf16[4,2,96,256]{3,2,1,0:T(8,128)(2,1)S(1)} collective-permute-done((bf16[4,2,96,256]{3,2,1,0:T(8,128)(2,1)S(1)}, bf16[4,2,96,256]{3,2,1,0:T(8,128)(2,1)S(1)}, u32[]{:S(2)}, u32[]{:S(2)}) %collective-permute-start.8) | collective-permute-done | bytes 393248 | tf_op jit(solution)/shard_map/ppermute | solution.py:289
  241.8 1.0 copy-done.6
  242.8 0.1 shard_map.80
  242.9 0.3 collective-permute-start.10
  243.2 1.6 collective-permute-start.11
  244.8 100.6 %shard_map.79 = bf16[16,32,256]{2,1,0:T(8,128)(2,1)} custom-call(bf16[16,96,256]{2,1,0:T(8,128)(2,1)S(1)} %all-to-all-done.2.a_ref), custom_call_target="tpu_custom_call" | custom-call | flops 34359738368 | bytes 1048576 | tf_op jit(solution)/shard_map/pallas_call | solution.py:270
  345.3 6.0 %all-to-all-start.3 = ((bf16[16,32,256]{2,1,0:T(8,128)(2,1)}), bf16[16,32,256]{2,1,0:T(8,128)(2,1)S(1)}, u32[]{:S(2)}, u32[]{:S(2)}) async-start(bf16[16,32,256]{2,1,0:T(8,128)(2,1)} %shard_map.79), calls=%async_computation.3 | async-start | bytes 524288 | tf_op jit(solution)/shard_map/all_to_all | solution.py:304
  351.3 50.6 %shard_map.81 = (bf16[4,2,32,256]{3,2,1,0:T(8,128)(2,1)S(1)}, bf16[4,2,32,256]{3,2,1,0:T(8,128)(2,1)S(1)}) custom-call(bf16[2,2,96,256]{3,2,1,0:T(8,128)(2,1)S(1)} %get-tuple-element.49.p0, bf16[2,2,96,256]{3,2,1,0:T(8,128)(2,1)S(1)} %collective-permute-done.9.p1, bf16[2,2,96,256]{3,2,1,0:T(8,128)(2,1)S(1)} %collective-permute-done.10.p2, ...), custom_call_target="tpu_custom_call" | custom-call | flops 17179869184 | bytes 1048576 | tf_op jit(solution)/shard_map/pallas_call | solution.py:270
  402.0 0.0 copy-start.7
  402.0 2.7 collective-permute-start.12
  404.7 3.8 collective-permute-done.12.far
  408.5 2.9 collective-permute-start.13
  411.4 0.1 collective-permute-start.14
  411.5 0.8 collective-permute-start.15
  412.2 0.5 collective-permute-done.13.refs_4_
  412.7 3.4 collective-permute-done.14.refs_5_
  416.1 0.4 collective-permute-done.15.refs_6_
  416.5 4.2 %shard_map.83 = bf16[32,32,256]{2,1,0:T(8,128)(2,1)} custom-call(s32[2]{0:T(128)S(1)} %pad_add_fusion.pos.refs_0_, bf16[32,32,256]{2,1,0:T(8,128)(2,1)S(1)} %copy-done.7, bf16[16,32,256]{2,1,0:T(8,128)(2,1)S(1)} %all-to-all-done.3.refs_2_, bf16[2,2,32,256]{3,2,1,0:T(8,128)(2,1)S(1)} %get-tuple-element.55.refs_3_, ...), custom_call_target="tpu_custom_call" | custom-call | flops 4294967296 | bytes 1048576 | tf_op jit(solution)/shard_map/pallas_call | solution.py:270
  (20 shorter events, 0.1 us)
Async XLA Ops:
  4.0 33.6 %all-to-all-start = ((bf16[16,96,256]{2,1,0:T(8,128)(2,1)}), bf16[16,96,256]{2,1,0:T(8,128)(2,1)S(1)}, u32[]{:S(2)}, u32[]{:S(2)}) async-start(bf16[16,96,256]{2,1,0:T(8,128)(2,1)} %get-tuple-element.32), calls=%async_computation | async-start | bytes 1572864 | tf_op jit(solution)/shard_map/all_to_all | solution.py:298
  11.8 20.8 %collective-permute-start = (bf16[4,2,96,256]{3,2,1,0:T(8,128)(2,1)S(1)}, bf16[4,2,96,256]{3,2,1,0:T(8,128)(2,1)S(1)}, u32[]{:S(2)}, u32[]{:S(2)}) collective-permute-start(bf16[4,2,96,256]{3,2,1,0:T(8,128)(2,1)S(1)} %get-tuple-element.34), channel_id=1, source_target_pairs={{0,16},{16,0},{1,17},{17,1},{2,18},{18,2},{3,19},{19,3},{4,20},{20... | collective-permute-start | bytes 1179656 | tf_op jit(solution)/shard_map/ppermute | solution.py:289
  32.7 111.6 %collective-permute-start.1 = (bf16[2,2,96,256]{3,2,1,0:T(8,128)(2,1)S(1)}, bf16[2,2,96,256]{3,2,1,0:T(8,128)(2,1)S(1)}, u32[]{:S(2)}, u32[]{:S(2)}) collective-permute-start(bf16[2,2,96,256]{3,2,1,0:T(8,128)(2,1)S(1)} %get-tuple-element.36), channel_id=1, source_target_pairs={{0,32},{32,64},{64,96},{96,0},{1,33},{33,65},{65,97},{97,1},{2,34}... | collective-permute-start | bytes 589832 | tf_op jit(solution)/shard_map/ppermute | solution.py:289
  34.0 110.3 %collective-permute-start.2 = (bf16[2,2,96,256]{3,2,1,0:T(8,128)(2,1)S(1)}, bf16[2,2,96,256]{3,2,1,0:T(8,128)(2,1)S(1)}, u32[]{:S(2)}, u32[]{:S(2)}) collective-permute-start(bf16[2,2,96,256]{3,2,1,0:T(8,128)(2,1)S(1)} %get-tuple-element.37), channel_id=1, source_target_pairs={{0,64},{32,96},{64,0},{96,32},{1,65},{33,97},{65,1},{97,33},{2,66}... | collective-permute-start | bytes 589832 | tf_op jit(solution)/shard_map/ppermute | solution.py:289
  36.4 107.8 %collective-permute-start.3 = (bf16[2,2,96,256]{3,2,1,0:T(8,128)(2,1)S(1)}, bf16[2,2,96,256]{3,2,1,0:T(8,128)(2,1)S(1)}, u32[]{:S(2)}, u32[]{:S(2)}) collective-permute-start(bf16[2,2,96,256]{3,2,1,0:T(8,128)(2,1)S(1)} %get-tuple-element.38), channel_id=1, source_target_pairs={{0,96},{32,0},{64,32},{96,64},{1,97},{33,1},{65,33},{97,65},{2,98}... | collective-permute-start | bytes 589832 | tf_op jit(solution)/shard_map/ppermute | solution.py:289
  138.2 70.1 %all-to-all-start.1 = ((bf16[16,32,256]{2,1,0:T(8,128)(2,1)}), bf16[16,32,256]{2,1,0:T(8,128)(2,1)S(1)}, u32[]{:S(2)}, u32[]{:S(2)}) async-start(bf16[16,32,256]{2,1,0:T(8,128)(2,1)} %shard_map.74), calls=%async_computation.1 | async-start | bytes 524288 | tf_op jit(solution)/shard_map/all_to_all | solution.py:304
  144.3 63.9 %copy-start = (bf16[2,256,1024]{2,1,0:T(8,128)(2,1)S(1)}, bf16[2,256,1024]{2,1,0:T(8,128)(2,1)}, u32[]{:S(2)}) copy-start(bf16[2,256,1024]{2,1,0:T(8,128)(2,1)} %refs_9_.3) | copy-start | bytes 3145732
  194.7 13.5 %copy-start.1 = (bf16[32,32,256]{2,1,0:T(8,128)(2,1)S(1)}, bf16[32,32,256]{2,1,0:T(8,128)(2,1)}, u32[]{:S(2)}) copy-start(bf16[32,32,256]{2,1,0:T(8,128)(2,1)} %refs_1_.1) | copy-start | bytes 1572868
  194.7 6.5 %collective-permute-start.4 = (bf16[4,2,32,256]{3,2,1,0:T(8,128)(2,1)S(1)}, bf16[4,2,32,256]{3,2,1,0:T(8,128)(2,1)S(1)}, u32[]{:S(2)}, u32[]{:S(2)}) collective-permute-start(bf16[4,2,32,256]{3,2,1,0:T(8,128)(2,1)S(1)} %get-tuple-element.40), channel_id=1, source_target_pairs={{0,16},{16,0},{1,17},{17,1},{2,18},{18,2},{3,19},{19,3},{4,20},{20... | collective-permute-start | bytes 393224 | tf_op jit(solution)/shard_map/ppermute | solution.py:289
  201.3 7.0 %copy-start.2 = (bf16[2,256,256]{2,1,0:T(8,128)(2,1)S(1)}, bf16[2,256,256]{2,1,0:T(8,128)(2,1)}, u32[]{:S(2)}) copy-start(bf16[2,256,256]{2,1,0:T(8,128)(2,1)} %refs_7_.3) | copy-start | bytes 786436
  201.3 3.2 collective-permute-start.5
  201.4 6.9 %copy-start.4 = (f32[2,256]{1,0:T(2,128)S(1)}, f32[2,256]{1,0:T(2,128)}, u32[]{:S(2)}) copy-start(f32[2,256]{1,0:T(2,128)} %refs_8_.3) | copy-start | bytes 6148
  201.4 6.9 %copy-start.3 = (f32[2,256]{1,0:T(2,128)S(1)}, f32[2,256]{1,0:T(2,128)}, u32[]{:S(2)}) copy-start(f32[2,256]{1,0:T(2,128)} %refs_11_.1) | copy-start | bytes 6148
  201.4 4.7 %collective-permute-start.6 = (bf16[2,2,32,256]{3,2,1,0:T(8,128)(2,1)S(1)}, bf16[2,2,32,256]{3,2,1,0:T(8,128)(2,1)S(1)}, u32[]{:S(2)}, u32[]{:S(2)}) collective-permute-start(bf16[2,2,32,256]{3,2,1,0:T(8,128)(2,1)S(1)} %get-tuple-element.43), channel_id=1, source_target_pairs={{0,64},{32,96},{64,0},{96,32},{1,65},{33,97},{65,1},{97,33},{2,66}... | collective-permute-start | bytes 196616 | tf_op jit(solution)/shard_map/ppermute | solution.py:289
  203.4 4.8 %collective-permute-start.7 = (bf16[2,2,32,256]{3,2,1,0:T(8,128)(2,1)S(1)}, bf16[2,2,32,256]{3,2,1,0:T(8,128)(2,1)S(1)}, u32[]{:S(2)}, u32[]{:S(2)}) collective-permute-start(bf16[2,2,32,256]{3,2,1,0:T(8,128)(2,1)S(1)} %get-tuple-element.44), channel_id=1, source_target_pairs={{0,32},{32,64},{64,96},{96,0},{1,33},{33,65},{65,97},{97,1},{2,34}... | collective-permute-start | bytes 196616 | tf_op jit(solution)/shard_map/ppermute | solution.py:289
  213.7 0.8 copy-start.5
  214.5 30.2 %all-to-all-start.2 = ((bf16[16,96,256]{2,1,0:T(8,128)(2,1)}), bf16[16,96,256]{2,1,0:T(8,128)(2,1)S(1)}, u32[]{:S(2)}, u32[]{:S(2)}) async-start(bf16[16,96,256]{2,1,0:T(8,128)(2,1)} %get-tuple-element.46), calls=%async_computation.2 | async-start | bytes 1572864 | tf_op jit(solution)/shard_map/all_to_all | solution.py:298
  222.1 19.8 %collective-permute-start.8 = (bf16[4,2,96,256]{3,2,1,0:T(8,128)(2,1)S(1)}, bf16[4,2,96,256]{3,2,1,0:T(8,128)(2,1)S(1)}, u32[]{:S(2)}, u32[]{:S(2)}) collective-permute-start(bf16[4,2,96,256]{3,2,1,0:T(8,128)(2,1)S(1)} %get-tuple-element.48), channel_id=1, source_target_pairs={{0,16},{16,0},{1,17},{17,1},{2,18},{18,2},{3,19},{19,3},{4,20},{20... | collective-permute-start | bytes 1179656 | tf_op jit(solution)/shard_map/ppermute | solution.py:289
  241.8 1.0 copy-start.6
  242.9 108.4 %collective-permute-start.10 = (bf16[2,2,96,256]{3,2,1,0:T(8,128)(2,1)S(1)}, bf16[2,2,96,256]{3,2,1,0:T(8,128)(2,1)S(1)}, u32[]{:S(2)}, u32[]{:S(2)}) collective-permute-start(bf16[2,2,96,256]{3,2,1,0:T(8,128)(2,1)S(1)} %get-tuple-element.51), channel_id=1, source_target_pairs={{0,64},{32,96},{64,0},{96,32},{1,65},{33,97},{65,1},{97,33},{2,66}... | collective-permute-start | bytes 589832 | tf_op jit(solution)/shard_map/ppermute | solution.py:289
  243.2 108.1 %collective-permute-start.11 = (bf16[2,2,96,256]{3,2,1,0:T(8,128)(2,1)S(1)}, bf16[2,2,96,256]{3,2,1,0:T(8,128)(2,1)S(1)}, u32[]{:S(2)}, u32[]{:S(2)}) collective-permute-start(bf16[2,2,96,256]{3,2,1,0:T(8,128)(2,1)S(1)} %get-tuple-element.52), channel_id=1, source_target_pairs={{0,96},{32,0},{64,32},{96,64},{1,97},{33,1},{65,33},{97,65},{2,98}... | collective-permute-start | bytes 589832 | tf_op jit(solution)/shard_map/ppermute | solution.py:289
  244.8 106.6 %collective-permute-start.9 = (bf16[2,2,96,256]{3,2,1,0:T(8,128)(2,1)S(1)}, bf16[2,2,96,256]{3,2,1,0:T(8,128)(2,1)S(1)}, u32[]{:S(2)}, u32[]{:S(2)}) collective-permute-start(bf16[2,2,96,256]{3,2,1,0:T(8,128)(2,1)S(1)} %get-tuple-element.50), channel_id=1, source_target_pairs={{0,32},{32,64},{64,96},{96,0},{1,33},{33,65},{65,97},{97,1},{2,34}... | collective-permute-start | bytes 589832 | tf_op jit(solution)/shard_map/ppermute | solution.py:289
  345.3 71.2 %all-to-all-start.3 = ((bf16[16,32,256]{2,1,0:T(8,128)(2,1)}), bf16[16,32,256]{2,1,0:T(8,128)(2,1)S(1)}, u32[]{:S(2)}, u32[]{:S(2)}) async-start(bf16[16,32,256]{2,1,0:T(8,128)(2,1)} %shard_map.79), calls=%async_computation.3 | async-start | bytes 524288 | tf_op jit(solution)/shard_map/all_to_all | solution.py:304
  402.0 14.5 %copy-start.7 = (bf16[32,32,256]{2,1,0:T(8,128)(2,1)S(1)}, bf16[32,32,256]{2,1,0:T(8,128)(2,1)}, u32[]{:S(2)}) copy-start(bf16[32,32,256]{2,1,0:T(8,128)(2,1)} %get-tuple-element.45.refs_1_) | copy-start | bytes 1572868
  402.0 6.5 %collective-permute-start.12 = (bf16[4,2,32,256]{3,2,1,0:T(8,128)(2,1)S(1)}, bf16[4,2,32,256]{3,2,1,0:T(8,128)(2,1)S(1)}, u32[]{:S(2)}, u32[]{:S(2)}) collective-permute-start(bf16[4,2,32,256]{3,2,1,0:T(8,128)(2,1)S(1)} %get-tuple-element.54), channel_id=1, source_target_pairs={{0,16},{16,0},{1,17},{17,1},{2,18},{18,2},{3,19},{19,3},{4,20},{20... | collective-permute-start | bytes 393224 | tf_op jit(solution)/shard_map/ppermute | solution.py:289
  408.5 4.2 collective-permute-start.13
  411.4 4.7 %collective-permute-start.14 = (bf16[2,2,32,256]{3,2,1,0:T(8,128)(2,1)S(1)}, bf16[2,2,32,256]{3,2,1,0:T(8,128)(2,1)S(1)}, u32[]{:S(2)}, u32[]{:S(2)}) collective-permute-start(bf16[2,2,32,256]{3,2,1,0:T(8,128)(2,1)S(1)} %get-tuple-element.57), channel_id=1, source_target_pairs={{0,64},{32,96},{64,0},{96,32},{1,65},{33,97},{65,1},{97,33},{2,66}... | collective-permute-start | bytes 196616 | tf_op jit(solution)/shard_map/ppermute | solution.py:289
  411.5 5.0 %collective-permute-start.15 = (bf16[2,2,32,256]{3,2,1,0:T(8,128)(2,1)S(1)}, bf16[2,2,32,256]{3,2,1,0:T(8,128)(2,1)S(1)}, u32[]{:S(2)}, u32[]{:S(2)}) collective-permute-start(bf16[2,2,32,256]{3,2,1,0:T(8,128)(2,1)S(1)} %get-tuple-element.58), channel_id=1, source_target_pairs={{0,32},{32,64},{64,96},{96,0},{1,33},{33,65},{65,97},{97,1},{2,34}... | collective-permute-start | bytes 196616 | tf_op jit(solution)/shard_map/ppermute | solution.py:289

commit v4 on v3

--- a/solution.py
+++ b/solution.py
@@ -135,19 +135,23 @@
     attend(1, 16, lambda it, s, lo, hi: a_ref[s, lo:hi, :], put, [sc], 2)
 
 
+def split_kernel(*refs):
+    for k in range(4):
+        for e in range(2):
+            refs[4 + e][k] = refs[k][e]
+
+
 def pair_kernel(near, far, *outs):
     for k in range(4):
         outs[k][0] = near[k]
         outs[k][1] = far[k]
 
 
-def down_attend_kernel(p0, p1, p2, p3, near, far, all_ref, *sc):
-    blocks = (p0, p1, p2, p3)
-
+def down_attend_kernel(got_near, got_far, near, far, all_ref, *sc):
     def put(it, s, v):
         all_ref[s, it] = v
 
-    attend(2, 8, lambda it, s, lo, hi: blocks[s // 2][s % 2, it, lo:hi, :], put, [sc[0:3], sc[3:6]], 2)
+    attend(2, 8, lambda it, s, lo, hi: (got_far if s % 2 else got_near)[s // 2, it, lo:hi, :], put, [sc[0:3], sc[3:6]], 2)
     for k in range(4):
         near[k] = all_ref[2 * k]
         far[k] = all_ref[2 * k + 1]
@@ -178,10 +182,11 @@
         for t in range(3):
             out = tdot(w_ref[:, t * 256 + 128:t * 256 + 256], n).astype(BF).reshape(2, 2, 32, 256)
             for hp in range(2):
-                sends[(hp + pos[1]) % 2, k, :, t * 32:t * 32 + 32, :] = out[hp]
-
-
-def first_kernel(pos, x_hbm, g_hbm, w_hbm, c_hbm, near, far, nrm, sends, x, g, w, sems, c):
+                sends[k, (hp + pos[1]) % 2, :, t * 32:t * 32 + 32, :] = out[hp]
+
+
+def first_kernel(pos, x_hbm, g_hbm, w_hbm, c_hbm, s0, s1, s2, s3, nrm, sends, x, g, w, sems, c):
+    outs = (s0, s1, s2, s3)
     copies = [pltpu.make_async_copy(g_hbm, g, sems.at[0]), pltpu.make_async_copy(w_hbm.at[0], w, sems.at[1]), pltpu.make_async_copy(x_hbm, x, sems.at[2])]
     save = pltpu.make_async_copy(c, c_hbm, sems.at[3])
     for copy in copies:
@@ -189,8 +194,8 @@
     for copy in copies:
         copy.wait()
     project(lambda b: x[8 * b:8 * b + 8].reshape(256, D).astype(F32), pos, g[0:1], w, c, sends, nrm, save.start)
-    near[...] = sends[0]
-    far[...] = sends[1]
+    for k in range(4):
+        outs[k][...] = sends[k]
     save.wait()
 
 
@@ -218,7 +223,8 @@
         put(b, (mix[8 * b:8 * b + 8].reshape(256, D) + out).astype(BF))
 
 
-def mid_kernel(layer, pos, x_ref, hc_ref, h0, h1, h2, h3, wo_ref, gm_ref, wu_ref, wd_hbm, ga_ref, w_hbm, y_hbm, c_hbm, near, far, mix, sends, wd, hv, n2, sems, y, w, c):
+def mid_kernel(layer, pos, x_ref, hc_ref, h0, h1, h2, h3, wo_ref, gm_ref, wu_ref, wd_hbm, ga_ref, w_hbm, y_hbm, c_hbm, s0, s1, s2, s3, mix, sends, wd, hv, n2, sems, y, w, c):
+    outs = (s0, s1, s2, s3)
     loads = [pltpu.make_async_copy(wd_hbm.at[layer], wd, sems.at[0]), pltpu.make_async_copy(w_hbm.at[layer + 1], w, sems.at[1])]
     saves = [pltpu.make_async_copy(y, y_hbm, sems.at[2]), pltpu.make_async_copy(c, c_hbm, sems.at[3])]
     for copy in loads:
@@ -237,8 +243,8 @@
 
     finish(layer, pos, x_ref, hc_ref, (h0, h1, h2, h3), wo_ref, gm_ref, wu_ref, wd, ready, mix, hv, n2, put)
     project(lambda b: y[8 * b:8 * b + 8].reshape(256, D).astype(F32), pos, ga_ref[layer + 1:layer + 2], w, c, sends, mix, sent)
-    near[...] = sends[0]
-    far[...] = sends[1]
+    for k in range(4):
+        outs[k][...] = sends[k]
     for copy in saves:
         copy.wait()
 
@@ -288,18 +294,18 @@
     pos = jnp.stack([lax.axis_index("x"), lax.axis_index("yh")]).astype(jnp.int32)
     shift = lambda value, axis, k, size: lax.ppermute(value, axis, [(i, (i + k) % size) for i in range(size)])
     state = frame
-    sends = vm(2, 4, 2, 96, 256)
+    sends = vm(4, 2, 2, 96, 256)
     mix = vm(32, 32, D, dtype=F32)
     mlp = [vm(4 * D, D), vm(8, 2, 32, 256), vm(4 * D, D), SEMS]
     buffers = [vm(D, 3 * D), vm(16, 96, 256)]
-    c, near, far = call(first_kernel, [SM] + [HB] * 3, (HBM_ACROSS, HALF, HALF), (HB, VM, VM), [mix, sends, vm(32, 32, D), vm(LAYERS, D, dtype=F32), buffers[0], SEMS, buffers[1]], 2 << 30, 12, pos, *map(far_memory, (state, gain_attn, w_qkv)))
+    c, *r = call(first_kernel, [SM] + [HB] * 3, (HBM_ACROSS,) + (BLOCK,) * 4, (HB,) + (VM,) * 4, [mix, sends, vm(32, 32, D), vm(LAYERS, D, dtype=F32), buffers[0], SEMS, buffers[1]], 2 << 30, 12, pos, *map(far_memory, (state, gain_attn, w_qkv)))
     for layer in range(LAYERS):
+        c = lax.all_to_all(c, COL, 0, 0, tiled=True)
+        r = [r[0]] + [shift(r[k], "x", k, 4) for k in (1, 2, 3)]
+        near, far = call(split_kernel, [VM] * 4, (HALF,) * 2, (VM,) * 2, [], 1 << 28, 4, *r)
         far = shift(far, "yh", 1, 2)
-        c = lax.all_to_all(c, COL, 0, 0, tiled=True)
-        r = call(pair_kernel, [VM] * 2, (BLOCK,) * 4, (VM,) * 4, [], 1 << 28, 4, near, far)
-        r = [r[0]] + [shift(r[k], "x", k, 4) for k in (1, 2, 3)]
         hc = call(across_kernel, [VM], jax.ShapeDtypeStruct((16, 32, 256), BF), VM, attention_scratch(16), 32 << 30, 16, c)
-        near, far = call(down_attend_kernel, [VM] * 4, (HALF_REPLY,) * 2, (VM,) * 2, [vm(8, 2, 32, 256)] + attention_scratch(8) * 2, 16 << 30, 16, *r)
+        near, far = call(down_attend_kernel, [VM] * 2, (HALF_REPLY,) * 2, (VM,) * 2, [vm(8, 2, 32, 256)] + attention_scratch(8) * 2, 16 << 30, 16, near, far)
         far = shift(far, "yh", 1, 2)
         hc = lax.all_to_all(hc, COL, 0, 0, tiled=True)
         o = call(pair_kernel, [VM] * 2, (REPLY,) * 4, (VM,) * 4, [], 1 << 28, 4, near, far)
@@ -307,7 +313,7 @@
         rest = (pos, state, hc, *o, w_out, gain_mlp, w_up, far_memory(w_down))
         specs = [SM] + [VM] * 9 + [HB]
         if layer + 1 < LAYERS:
-            state, c, near, far = call(bind(mid_kernel, layer), specs + [VM, HB], (HBM_STATE, HBM_ACROSS, HALF, HALF), (HB, HB, VM, VM), [mix, sends] + mlp + [vm(32, 32, D)] + buffers, 6 << 30, 24, *rest, gain_attn, far_memory(w_qkv))
+            state, c, *r = call(bind(mid_kernel, layer), specs + [VM, HB], (HBM_STATE, HBM_ACROSS) + (BLOCK,) * 4, (HB, HB) + (VM,) * 4, [mix, sends] + mlp + [vm(32, 32, D)] + buffers, 6 << 30, 24, *rest, gain_attn, far_memory(w_qkv))
         else:
             state = call(bind(last_kernel, layer), specs, STATE, VM, [mix] + mlp, 4 << 30, 24, *rest)
     return state

time: 423 us -> 401 us (0.948)
  waiting for transfers between devices: 54.2 us -> 33.4 us
    ppermute x16, waiting for transfers between devices: 54.1 us -> 33.4 us  [shards(): lax.ppermute(value, axis, [(i, (i + k) % size) for i in range(size)])]
  transfers between devices with their start and end apart: 20 -> 20, of which waited for: 10 -> 13; matrix products, arithmetic and copies ran while one was open for 0% -> 0% of each run, Pallas kernels for 72% -> 76%
where the time goes in v4:
time: 401 us; the launch traced here: 400 us
  Pallas kernels  316 us (79%)
  starting transfers between devices  50.2 us (13%)
  waiting for transfers between devices  33.4 us (8%)
    pallas_call x11, Pallas kernels, call(): pl.pallas_call(kernel, out_shape=outs, in_specs=specs, out_specs=out_spec...  316 us
    ppermute x16, waiting for transfers between devices, shards(): lax.ppermute(value, axis, [(i, (i + k) % size) for i in range(size)])  33.4 us
    ppermute x16, starting transfers between devices, shards(): lax.ppermute(value, axis, [(i, (i + k) % size) for i in range(size)])  21.7 us
    all_to_all x2, starting transfers between devices, shards(): c = lax.all_to_all(c, COL, 0, 0, tiled=True)  15.7 us
    all_to_all x2, starting transfers between devices, shards(): hc = lax.all_to_all(hc, COL, 0, 0, tiled=True)  12.7 us
  transfers between devices with their start and end apart: 20, of which 13 were waited for; matrix products, arithmetic and copies ran while one was open for 0% of the time, Pallas kernels for 76%

profile of v4, /device:TPU:1, one launch (start us, length us, event | category | flops | bytes accessed | tf_op | source)
XLA Modules:
  0.0 399.7 jit_solution(11003276272390142615)
XLA Ops:
  0.0 0.1 pad_add_fusion.pos.refs_0_
  0.1 3.8 shard_map.73
  3.9 7.8 %all-to-all-start = ((bf16[16,96,256]{2,1,0:T(8,128)(2,1)}), bf16[16,96,256]{2,1,0:T(8,128)(2,1)S(1)}, u32[]{:S(2)}, u32[]{:S(2)}) async-start(bf16[16,96,256]{2,1,0:T(8,128)(2,1)} %get-tuple-element.32), calls=%async_computation | async-start | bytes 1572864 | tf_op jit(solution)/shard_map/all_to_all | solution.py:303
  11.7 1.2 collective-permute-start
  12.9 2.5 collective-permute-start.1
  15.4 1.2 collective-permute-start.2
  16.5 2.7 collective-permute-done.refs_1_
  19.2 5.2 %collective-permute-done.1.refs_2_ = bf16[2,2,96,256]{3,2,1,0:T(8,128)(2,1)S(1)} collective-permute-done((bf16[2,2,96,256]{3,2,1,0:T(8,128)(2,1)S(1)}, bf16[2,2,96,256]{3,2,1,0:T(8,128)(2,1)S(1)}, u32[]{:S(2)}, u32[]{:S(2)}) %collective-permute-start.1) | collective-permute-done | bytes 196640 | tf_op jit(solution)/shard_map/ppermute | solution.py:295
  24.4 0.1 shard_map.75
  24.5 2.7 collective-permute-start.3
  27.2 0.0 all-to-all-done.a_ref
  27.2 100.6 %shard_map.74 = bf16[16,32,256]{2,1,0:T(8,128)(2,1)} custom-call(bf16[16,96,256]{2,1,0:T(8,128)(2,1)S(1)} %all-to-all-done.a_ref), custom_call_target="tpu_custom_call" | custom-call | flops 34359738368 | bytes 1048576 | tf_op jit(solution)/shard_map/pallas_call | solution.py:276
  127.7 6.0 %all-to-all-start.1 = ((bf16[16,32,256]{2,1,0:T(8,128)(2,1)}), bf16[16,32,256]{2,1,0:T(8,128)(2,1)S(1)}, u32[]{:S(2)}, u32[]{:S(2)}) async-start(bf16[16,32,256]{2,1,0:T(8,128)(2,1)} %shard_map.74), calls=%async_computation.1 | async-start | bytes 524288 | tf_op jit(solution)/shard_map/all_to_all | solution.py:310
  133.8 0.0 collective-permute-done.3.got_far
  133.8 0.0 copy-start
  133.8 50.4 %shard_map.76 = (bf16[4,2,32,256]{3,2,1,0:T(8,128)(2,1)S(1)}, bf16[4,2,32,256]{3,2,1,0:T(8,128)(2,1)S(1)}) custom-call(bf16[4,2,96,256]{3,2,1,0:T(8,128)(2,1)S(1)} %get-tuple-element.37.got_near, bf16[4,2,96,256]{3,2,1,0:T(8,128)(2,1)S(1)} %collective-permute-done.3.got_far), custom_call_target="tpu_custom_call" | custom-call | flops 17179869184 | bytes 1048576 | tf_op jit(solution)/shard_map/pallas_call | solution.py:276
  184.2 0.0 copy-start.1
  184.2 1.6 collective-permute-start.4
  185.9 4.9 %collective-permute-done.4.far = bf16[4,2,32,256]{3,2,1,0:T(8,128)(2,1)S(1)} collective-permute-done((bf16[4,2,32,256]{3,2,1,0:T(8,128)(2,1)S(1)}, bf16[4,2,32,256]{3,2,1,0:T(8,128)(2,1)S(1)}, u32[]{:S(2)}, u32[]{:S(2)}) %collective-permute-start.4) | collective-permute-done | bytes 131104 | tf_op jit(solution)/shard_map/ppermute | solution.py:295
  190.8 2.1 collective-permute-start.5
  192.8 0.9 collective-permute-start.6
  193.7 0.4 collective-permute-start.7
  194.1 0.1 collective-permute-done.5.refs_4_
  194.2 3.3 collective-permute-done.6.refs_5_
  197.5 0.7 collective-permute-done.7.refs_6_
  198.2 5.3 %shard_map.78 = (bf16[32,32,256]{2,1,0:T(8,128)(2,1)}, bf16[16,96,256]{2,1,0:T(8,128)(2,1)}, bf16[2,2,96,256]{3,2,1,0:T(8,128)(2,1)S(1)}, bf16[2,2,96,256]{3,2,1...) custom-call(s32[2]{0:T(128)S(1)} %pad_add_fusion.pos.refs_0_, ...), custom_call_target="tpu_custom_call" | custom-call | flops 6442450944 | bytes 1048576 | tf_op jit(solution)/shard_map/pallas_call | solution.py:276
  203.5 7.9 %all-to-all-start.2 = ((bf16[16,96,256]{2,1,0:T(8,128)(2,1)}), bf16[16,96,256]{2,1,0:T(8,128)(2,1)S(1)}, u32[]{:S(2)}, u32[]{:S(2)}) async-start(bf16[16,96,256]{2,1,0:T(8,128)(2,1)} %get-tuple-element.46), calls=%async_computation.2 | async-start | bytes 1572864 | tf_op jit(solution)/shard_map/all_to_all | solution.py:303
  211.4 0.1 collective-permute-start.10
  211.5 1.3 collective-permute-start.8
  212.9 0.9 collective-permute-start.9
  213.8 3.9 collective-permute-done.10.refs_3_
  217.7 1.5 collective-permute-done.8.refs_1_
  219.2 3.4 collective-permute-done.9.refs_2_
  222.6 0.1 shard_map.80
  222.6 1.6 collective-permute-start.11
  224.3 100.5 %shard_map.79 = bf16[16,32,256]{2,1,0:T(8,128)(2,1)} custom-call(bf16[16,96,256]{2,1,0:T(8,128)(2,1)S(1)} %all-to-all-done.2.a_ref), custom_call_target="tpu_custom_call" | custom-call | flops 34359738368 | bytes 1048576 | tf_op jit(solution)/shard_map/pallas_call | solution.py:276
  324.8 6.7 %all-to-all-start.3 = ((bf16[16,32,256]{2,1,0:T(8,128)(2,1)}), bf16[16,32,256]{2,1,0:T(8,128)(2,1)S(1)}, u32[]{:S(2)}, u32[]{:S(2)}) async-start(bf16[16,32,256]{2,1,0:T(8,128)(2,1)} %shard_map.79), calls=%async_computation.3 | async-start | bytes 524288 | tf_op jit(solution)/shard_map/all_to_all | solution.py:310
  331.6 50.6 %shard_map.81 = (bf16[4,2,32,256]{3,2,1,0:T(8,128)(2,1)S(1)}, bf16[4,2,32,256]{3,2,1,0:T(8,128)(2,1)S(1)}) custom-call(bf16[4,2,96,256]{3,2,1,0:T(8,128)(2,1)S(1)} %get-tuple-element.51.got_near, bf16[4,2,96,256]{3,2,1,0:T(8,128)(2,1)S(1)} %collective-permute-done.11.got_far), custom_call_target="tpu_custom_call" | custom-call | flops 17179869184 | bytes 1048576 | tf_op jit(solution)/shard_map/pallas_call | solution.py:276
  382.2 0.0 copy-start.5
  382.2 2.7 collective-permute-start.12
  384.9 3.8 collective-permute-done.12.far
  388.8 1.1 collective-permute-start.13
  389.9 0.7 collective-permute-start.14
  390.5 0.8 collective-permute-start.15
  391.3 0.6 collective-permute-done.13.refs_4_
  391.9 2.6 collective-permute-done.14.refs_5_
  394.5 0.7 collective-permute-done.15.refs_6_
  395.2 4.3 %shard_map.83 = bf16[32,32,256]{2,1,0:T(8,128)(2,1)} custom-call(s32[2]{0:T(128)S(1)} %pad_add_fusion.pos.refs_0_, bf16[32,32,256]{2,1,0:T(8,128)(2,1)S(1)} %copy-done.5, bf16[16,32,256]{2,1,0:T(8,128)(2,1)S(1)} %all-to-all-done.3.refs_2_, bf16[2,2,32,256]{3,2,1,0:T(8,128)(2,1)S(1)} %get-tuple-element.55.refs_3_, ...), custom_call_target="tpu_custom_call" | custom-call | flops 4294967296 | bytes 1048576 | tf_op jit(solution)/shard_map/pallas_call | solution.py:276
  (16 shorter events, 0.1 us)
Async XLA Ops:
  3.9 23.3 %all-to-all-start = ((bf16[16,96,256]{2,1,0:T(8,128)(2,1)}), bf16[16,96,256]{2,1,0:T(8,128)(2,1)S(1)}, u32[]{:S(2)}, u32[]{:S(2)}) async-start(bf16[16,96,256]{2,1,0:T(8,128)(2,1)} %get-tuple-element.32), calls=%async_computation | async-start | bytes 1572864 | tf_op jit(solution)/shard_map/all_to_all | solution.py:303
  11.7 7.5 %collective-permute-start = (bf16[2,2,96,256]{3,2,1,0:T(8,128)(2,1)S(1)}, bf16[2,2,96,256]{3,2,1,0:T(8,128)(2,1)S(1)}, u32[]{:S(2)}, u32[]{:S(2)}) collective-permute-start(bf16[2,2,96,256]{3,2,1,0:T(8,128)(2,1)S(1)} %get-tuple-element.34), channel_id=1, source_target_pairs={{0,32},{32,64},{64,96},{96,0},{1,33},{33,65},{65,97},{97,1},{2,34}... | collective-permute-start | bytes 589832 | tf_op jit(solution)/shard_map/ppermute | solution.py:295
  12.9 11.5 %collective-permute-start.1 = (bf16[2,2,96,256]{3,2,1,0:T(8,128)(2,1)S(1)}, bf16[2,2,96,256]{3,2,1,0:T(8,128)(2,1)S(1)}, u32[]{:S(2)}, u32[]{:S(2)}) collective-permute-start(bf16[2,2,96,256]{3,2,1,0:T(8,128)(2,1)S(1)} %get-tuple-element.35), channel_id=1, source_target_pairs={{0,64},{32,96},{64,0},{96,32},{1,65},{33,97},{65,1},{97,33},{2,66}... | collective-permute-start | bytes 589832 | tf_op jit(solution)/shard_map/ppermute | solution.py:295
  15.4 9.0 %collective-permute-start.2 = (bf16[2,2,96,256]{3,2,1,0:T(8,128)(2,1)S(1)}, bf16[2,2,96,256]{3,2,1,0:T(8,128)(2,1)S(1)}, u32[]{:S(2)}, u32[]{:S(2)}) collective-permute-start(bf16[2,2,96,256]{3,2,1,0:T(8,128)(2,1)S(1)} %get-tuple-element.36), channel_id=1, source_target_pairs={{0,96},{32,0},{64,32},{96,64},{1,97},{33,1},{65,33},{97,65},{2,98}... | collective-permute-start | bytes 589832 | tf_op jit(solution)/shard_map/ppermute | solution.py:295
  24.5 109.3 %collective-permute-start.3 = (bf16[4,2,96,256]{3,2,1,0:T(8,128)(2,1)S(1)}, bf16[4,2,96,256]{3,2,1,0:T(8,128)(2,1)S(1)}, u32[]{:S(2)}, u32[]{:S(2)}) collective-permute-start(bf16[4,2,96,256]{3,2,1,0:T(8,128)(2,1)S(1)} %get-tuple-element.38), channel_id=1, source_target_pairs={{0,16},{16,0},{1,17},{17,1},{2,18},{18,2},{3,19},{19,3},{4,20},{20... | collective-permute-start | bytes 1179656 | tf_op jit(solution)/shard_map/ppermute | solution.py:295
  127.7 70.4 %all-to-all-start.1 = ((bf16[16,32,256]{2,1,0:T(8,128)(2,1)}), bf16[16,32,256]{2,1,0:T(8,128)(2,1)S(1)}, u32[]{:S(2)}, u32[]{:S(2)}) async-start(bf16[16,32,256]{2,1,0:T(8,128)(2,1)} %shard_map.74), calls=%async_computation.1 | async-start | bytes 524288 | tf_op jit(solution)/shard_map/all_to_all | solution.py:310
  133.8 64.4 %copy-start = (bf16[2,256,1024]{2,1,0:T(8,128)(2,1)S(1)}, bf16[2,256,1024]{2,1,0:T(8,128)(2,1)}, u32[]{:S(2)}) copy-start(bf16[2,256,1024]{2,1,0:T(8,128)(2,1)} %refs_9_.3) | copy-start | bytes 3145732
  184.2 14.0 %copy-start.1 = (bf16[32,32,256]{2,1,0:T(8,128)(2,1)S(1)}, bf16[32,32,256]{2,1,0:T(8,128)(2,1)}, u32[]{:S(2)}) copy-start(bf16[32,32,256]{2,1,0:T(8,128)(2,1)} %refs_1_.1) | copy-start | bytes 1572868
  184.2 6.5 %collective-permute-start.4 = (bf16[4,2,32,256]{3,2,1,0:T(8,128)(2,1)S(1)}, bf16[4,2,32,256]{3,2,1,0:T(8,128)(2,1)S(1)}, u32[]{:S(2)}, u32[]{:S(2)}) collective-permute-start(bf16[4,2,32,256]{3,2,1,0:T(8,128)(2,1)S(1)} %get-tuple-element.40), channel_id=1, source_target_pairs={{0,16},{16,0},{1,17},{17,1},{2,18},{18,2},{3,19},{19,3},{4,20},{20... | collective-permute-start | bytes 393224 | tf_op jit(solution)/shard_map/ppermute | solution.py:295
  190.7 7.4 %copy-start.2 = (bf16[2,256,256]{2,1,0:T(8,128)(2,1)S(1)}, bf16[2,256,256]{2,1,0:T(8,128)(2,1)}, u32[]{:S(2)}) copy-start(bf16[2,256,256]{2,1,0:T(8,128)(2,1)} %refs_7_.3) | copy-start | bytes 786436
  190.8 3.4 collective-permute-start.5
  192.8 5.4 %copy-start.4 = (f32[2,256]{1,0:T(2,128)S(1)}, f32[2,256]{1,0:T(2,128)}, u32[]{:S(2)}) copy-start(f32[2,256]{1,0:T(2,128)} %refs_8_.3) | copy-start | bytes 6148
  192.8 5.4 %copy-start.3 = (f32[2,256]{1,0:T(2,128)S(1)}, f32[2,256]{1,0:T(2,128)}, u32[]{:S(2)}) copy-start(f32[2,256]{1,0:T(2,128)} %refs_11_.1) | copy-start | bytes 6148
  192.8 4.6 %collective-permute-start.6 = (bf16[2,2,32,256]{3,2,1,0:T(8,128)(2,1)S(1)}, bf16[2,2,32,256]{3,2,1,0:T(8,128)(2,1)S(1)}, u32[]{:S(2)}, u32[]{:S(2)}) collective-permute-start(bf16[2,2,32,256]{3,2,1,0:T(8,128)(2,1)S(1)} %get-tuple-element.43), channel_id=1, source_target_pairs={{0,64},{32,96},{64,0},{96,32},{1,65},{33,97},{65,1},{97,33},{2,66}... | collective-permute-start | bytes 196616 | tf_op jit(solution)/shard_map/ppermute | solution.py:295
  193.7 4.5 %collective-permute-start.7 = (bf16[2,2,32,256]{3,2,1,0:T(8,128)(2,1)S(1)}, bf16[2,2,32,256]{3,2,1,0:T(8,128)(2,1)S(1)}, u32[]{:S(2)}, u32[]{:S(2)}) collective-permute-start(bf16[2,2,32,256]{3,2,1,0:T(8,128)(2,1)S(1)} %get-tuple-element.44), channel_id=1, source_target_pairs={{0,32},{32,64},{64,96},{96,0},{1,33},{33,65},{65,97},{97,1},{2,34}... | collective-permute-start | bytes 196616 | tf_op jit(solution)/shard_map/ppermute | solution.py:295
  203.5 20.8 %all-to-all-start.2 = ((bf16[16,96,256]{2,1,0:T(8,128)(2,1)}), bf16[16,96,256]{2,1,0:T(8,128)(2,1)S(1)}, u32[]{:S(2)}, u32[]{:S(2)}) async-start(bf16[16,96,256]{2,1,0:T(8,128)(2,1)} %get-tuple-element.46), calls=%async_computation.2 | async-start | bytes 1572864 | tf_op jit(solution)/shard_map/all_to_all | solution.py:303
  211.4 6.3 %collective-permute-start.10 = (bf16[2,2,96,256]{3,2,1,0:T(8,128)(2,1)S(1)}, bf16[2,2,96,256]{3,2,1,0:T(8,128)(2,1)S(1)}, u32[]{:S(2)}, u32[]{:S(2)}) collective-permute-start(bf16[2,2,96,256]{3,2,1,0:T(8,128)(2,1)S(1)} %get-tuple-element.50), channel_id=1, source_target_pairs={{0,96},{32,0},{64,32},{96,64},{1,97},{33,1},{65,33},{97,65},{2,98}... | collective-permute-start | bytes 589832 | tf_op jit(solution)/shard_map/ppermute | solution.py:295
  211.5 7.7 %collective-permute-start.8 = (bf16[2,2,96,256]{3,2,1,0:T(8,128)(2,1)S(1)}, bf16[2,2,96,256]{3,2,1,0:T(8,128)(2,1)S(1)}, u32[]{:S(2)}, u32[]{:S(2)}) collective-permute-start(bf16[2,2,96,256]{3,2,1,0:T(8,128)(2,1)S(1)} %get-tuple-element.48), channel_id=1, source_target_pairs={{0,32},{32,64},{64,96},{96,0},{1,33},{33,65},{65,97},{97,1},{2,34}... | collective-permute-start | bytes 589832 | tf_op jit(solution)/shard_map/ppermute | solution.py:295
  212.9 9.7 %collective-permute-start.9 = (bf16[2,2,96,256]{3,2,1,0:T(8,128)(2,1)S(1)}, bf16[2,2,96,256]{3,2,1,0:T(8,128)(2,1)S(1)}, u32[]{:S(2)}, u32[]{:S(2)}) collective-permute-start(bf16[2,2,96,256]{3,2,1,0:T(8,128)(2,1)S(1)} %get-tuple-element.49), channel_id=1, source_target_pairs={{0,64},{32,96},{64,0},{96,32},{1,65},{33,97},{65,1},{97,33},{2,66}... | collective-permute-start | bytes 589832 | tf_op jit(solution)/shard_map/ppermute | solution.py:295
  222.6 108.9 %collective-permute-start.11 = (bf16[4,2,96,256]{3,2,1,0:T(8,128)(2,1)S(1)}, bf16[4,2,96,256]{3,2,1,0:T(8,128)(2,1)S(1)}, u32[]{:S(2)}, u32[]{:S(2)}) collective-permute-start(bf16[4,2,96,256]{3,2,1,0:T(8,128)(2,1)S(1)} %get-tuple-element.52), channel_id=1, source_target_pairs={{0,16},{16,0},{1,17},{17,1},{2,18},{18,2},{3,19},{19,3},{4,20},{20... | collective-permute-start | bytes 1179656 | tf_op jit(solution)/shard_map/ppermute | solution.py:295
  324.8 70.4 %all-to-all-start.3 = ((bf16[16,32,256]{2,1,0:T(8,128)(2,1)}), bf16[16,32,256]{2,1,0:T(8,128)(2,1)S(1)}, u32[]{:S(2)}, u32[]{:S(2)}) async-start(bf16[16,32,256]{2,1,0:T(8,128)(2,1)} %shard_map.79), calls=%async_computation.3 | async-start | bytes 524288 | tf_op jit(solution)/shard_map/all_to_all | solution.py:310
  382.2 13.0 %copy-start.5 = (bf16[32,32,256]{2,1,0:T(8,128)(2,1)S(1)}, bf16[32,32,256]{2,1,0:T(8,128)(2,1)}, u32[]{:S(2)}) copy-start(bf16[32,32,256]{2,1,0:T(8,128)(2,1)} %get-tuple-element.45.refs_1_) | copy-start | bytes 1572868
  382.2 6.5 %collective-permute-start.12 = (bf16[4,2,32,256]{3,2,1,0:T(8,128)(2,1)S(1)}, bf16[4,2,32,256]{3,2,1,0:T(8,128)(2,1)S(1)}, u32[]{:S(2)}, u32[]{:S(2)}) collective-permute-start(bf16[4,2,32,256]{3,2,1,0:T(8,128)(2,1)S(1)} %get-tuple-element.54), channel_id=1, source_target_pairs={{0,16},{16,0},{1,17},{17,1},{2,18},{18,2},{3,19},{19,3},{4,20},{20... | collective-permute-start | bytes 393224 | tf_op jit(solution)/shard_map/ppermute | solution.py:295
  388.8 3.2 collective-permute-start.13
  389.9 4.7 %collective-permute-start.14 = (bf16[2,2,32,256]{3,2,1,0:T(8,128)(2,1)S(1)}, bf16[2,2,32,256]{3,2,1,0:T(8,128)(2,1)S(1)}, u32[]{:S(2)}, u32[]{:S(2)}) collective-permute-start(bf16[2,2,32,256]{3,2,1,0:T(8,128)(2,1)S(1)} %get-tuple-element.57), channel_id=1, source_target_pairs={{0,64},{32,96},{64,0},{96,32},{1,65},{33,97},{65,1},{97,33},{2,66}... | collective-permute-start | bytes 196616 | tf_op jit(solution)/shard_map/ppermute | solution.py:295
  390.5 4.6 %collective-permute-start.15 = (bf16[2,2,32,256]{3,2,1,0:T(8,128)(2,1)S(1)}, bf16[2,2,32,256]{3,2,1,0:T(8,128)(2,1)S(1)}, u32[]{:S(2)}, u32[]{:S(2)}) collective-permute-start(bf16[2,2,32,256]{3,2,1,0:T(8,128)(2,1)S(1)} %get-tuple-element.58), channel_id=1, source_target_pairs={{0,32},{32,64},{64,96},{96,0},{1,33},{33,65},{65,97},{97,1},{2,34}... | collective-permute-start | bytes 196616 | tf_op jit(solution)/shard_map/ppermute | solution.py:295

commit v5 on v4

--- a/solution.py
+++ b/solution.py
@@ -135,10 +135,9 @@
     attend(1, 16, lambda it, s, lo, hi: a_ref[s, lo:hi, :], put, [sc], 2)
 
 
-def split_kernel(*refs):
-    for k in range(4):
-        for e in range(2):
-            refs[4 + e][k] = refs[k][e]
+def stack_kernel(*refs):
+    for k in range(4):
+        refs[4][k] = refs[k][...]
 
 
 def pair_kernel(near, far, *outs):
@@ -147,11 +146,16 @@
         outs[k][1] = far[k]
 
 
-def down_attend_kernel(got_near, got_far, near, far, all_ref, *sc):
+def down_attend_kernel(n0, n1, n2, n3, got_far, near, far, all_ref, *sc):
+    got_near = (n0, n1, n2, n3)
+
+    def get(it, s, lo, hi):
+        return got_far[s // 2, it, lo:hi, :] if s % 2 else got_near[s // 2][it, lo:hi, :]
+
     def put(it, s, v):
         all_ref[s, it] = v
 
-    attend(2, 8, lambda it, s, lo, hi: (got_far if s % 2 else got_near)[s // 2, it, lo:hi, :], put, [sc[0:3], sc[3:6]], 2)
+    attend(2, 8, get, put, [sc[0:3], sc[3:6]], 2)
     for k in range(4):
         near[k] = all_ref[2 * k]
         far[k] = all_ref[2 * k + 1]
@@ -185,8 +189,8 @@
                 sends[k, (hp + pos[1]) % 2, :, t * 32:t * 32 + 32, :] = out[hp]
 
 
-def first_kernel(pos, x_hbm, g_hbm, w_hbm, c_hbm, s0, s1, s2, s3, nrm, sends, x, g, w, sems, c):
-    outs = (s0, s1, s2, s3)
+def first_kernel(pos, x_hbm, g_hbm, w_hbm, c_hbm, *rest):
+    outs, (nrm, sends, x, g, w, sems, c) = rest[:8], rest[8:]
     copies = [pltpu.make_async_copy(g_hbm, g, sems.at[0]), pltpu.make_async_copy(w_hbm.at[0], w, sems.at[1]), pltpu.make_async_copy(x_hbm, x, sems.at[2])]
     save = pltpu.make_async_copy(c, c_hbm, sems.at[3])
     for copy in copies:
@@ -195,7 +199,8 @@
         copy.wait()
     project(lambda b: x[8 * b:8 * b + 8].reshape(256, D).astype(F32), pos, g[0:1], w, c, sends, nrm, save.start)
     for k in range(4):
-        outs[k][...] = sends[k]
+        for e in range(2):
+            outs[4 * e + k][...] = sends[k, e]
     save.wait()
 
 
@@ -223,8 +228,8 @@
         put(b, (mix[8 * b:8 * b + 8].reshape(256, D) + out).astype(BF))
 
 
-def mid_kernel(layer, pos, x_ref, hc_ref, h0, h1, h2, h3, wo_ref, gm_ref, wu_ref, wd_hbm, ga_ref, w_hbm, y_hbm, c_hbm, s0, s1, s2, s3, mix, sends, wd, hv, n2, sems, y, w, c):
-    outs = (s0, s1, s2, s3)
+def mid_kernel(layer, pos, x_ref, hc_ref, h0, h1, h2, h3, wo_ref, gm_ref, wu_ref, wd_hbm, ga_ref, w_hbm, y_hbm, c_hbm, *rest):
+    outs, (mix, sends, wd, hv, n2, sems, y, w, c) = rest[:8], rest[8:]
     loads = [pltpu.make_async_copy(wd_hbm.at[layer], wd, sems.at[0]), pltpu.make_async_copy(w_hbm.at[layer + 1], w, sems.at[1])]
     saves = [pltpu.make_async_copy(y, y_hbm, sems.at[2]), pltpu.make_async_copy(c, c_hbm, sems.at[3])]
     for copy in loads:
@@ -244,7 +249,8 @@
     finish(layer, pos, x_ref, hc_ref, (h0, h1, h2, h3), wo_ref, gm_ref, wu_ref, wd, ready, mix, hv, n2, put)
     project(lambda b: y[8 * b:8 * b + 8].reshape(256, D).astype(F32), pos, ga_ref[layer + 1:layer + 2], w, c, sends, mix, sent)
     for k in range(4):
-        outs[k][...] = sends[k]
+        for e in range(2):
+            outs[4 * e + k][...] = sends[k, e]
     for copy in saves:
         copy.wait()
 
@@ -265,7 +271,7 @@
 REPLY = jax.ShapeDtypeStruct((2, 2, 32, 256), BF)
 HALF_REPLY = jax.ShapeDtypeStruct((4, 2, 32, 256), BF)
 HALF = jax.ShapeDtypeStruct((4, 2, 96, 256), BF)
-BLOCK = jax.ShapeDtypeStruct((2, 2, 96, 256), BF)
+BLOCK = jax.ShapeDtypeStruct((2, 96, 256), BF)
 STATE = jax.ShapeDtypeStruct((32, 32, D), BF)
 HBM_ACROSS = pltpu.HBM((16, 96, 256), BF)
 HBM_STATE = pltpu.HBM((32, 32, D), BF)
@@ -298,14 +304,15 @@
     mix = vm(32, 32, D, dtype=F32)
     mlp = [vm(4 * D, D), vm(8, 2, 32, 256), vm(4 * D, D), SEMS]
     buffers = [vm(D, 3 * D), vm(16, 96, 256)]
-    c, *r = call(first_kernel, [SM] + [HB] * 3, (HBM_ACROSS,) + (BLOCK,) * 4, (HB,) + (VM,) * 4, [mix, sends, vm(32, 32, D), vm(LAYERS, D, dtype=F32), buffers[0], SEMS, buffers[1]], 2 << 30, 12, pos, *map(far_memory, (state, gain_attn, w_qkv)))
+    c, *r = call(first_kernel, [SM] + [HB] * 3, (HBM_ACROSS,) + (BLOCK,) * 8, (HB,) + (VM,) * 8, [mix, sends, vm(32, 32, D), vm(LAYERS, D, dtype=F32), buffers[0], SEMS, buffers[1]], 2 << 30, 12, pos, *map(far_memory, (state, gain_attn, w_qkv)))
     for layer in range(LAYERS):
         c = lax.all_to_all(c, COL, 0, 0, tiled=True)
-        r = [r[0]] + [shift(r[k], "x", k, 4) for k in (1, 2, 3)]
-        near, far = call(split_kernel, [VM] * 4, (HALF,) * 2, (VM,) * 2, [], 1 << 28, 4, *r)
+        far = [r[4]] + [shift(r[4 + k], "x", k, 4) for k in (1, 2, 3)]
+        near = [r[0]] + [shift(r[k], "x", k, 4) for k in (1, 2, 3)]
+        far = call(stack_kernel, [VM] * 4, HALF, VM, [], 1 << 28, 4, *far)
         far = shift(far, "yh", 1, 2)
         hc = call(across_kernel, [VM], jax.ShapeDtypeStruct((16, 32, 256), BF), VM, attention_scratch(16), 32 << 30, 16, c)
-        near, far = call(down_attend_kernel, [VM] * 2, (HALF_REPLY,) * 2, (VM,) * 2, [vm(8, 2, 32, 256)] + attention_scratch(8) * 2, 16 << 30, 16, near, far)
+        near, far = call(down_attend_kernel, [VM] * 5, (HALF_REPLY,) * 2, (VM,) * 2, [vm(8, 2, 32, 256)] + attention_scratch(8) * 2, 16 << 30, 16, *near, far)
         far = shift(far, "yh", 1, 2)
         hc = lax.all_to_all(hc, COL, 0, 0, tiled=True)
         o = call(pair_kernel, [VM] * 2, (REPLY,) * 4, (VM,) * 4, [], 1 << 28, 4, near, far)
@@ -313,7 +320,7 @@
         rest = (pos, state, hc, *o, w_out, gain_mlp, w_up, far_memory(w_down))
         specs = [SM] + [VM] * 9 + [HB]
         if layer + 1 < LAYERS:
-            state, c, *r = call(bind(mid_kernel, layer), specs + [VM, HB], (HBM_STATE, HBM_ACROSS) + (BLOCK,) * 4, (HB, HB) + (VM,) * 4, [mix, sends] + mlp + [vm(32, 32, D)] + buffers, 6 << 30, 24, *rest, gain_attn, far_memory(w_qkv))
+            state, c, *r = call(bind(mid_kernel, layer), specs + [VM, HB], (HBM_STATE, HBM_ACROSS) + (BLOCK,) * 8, (HB, HB) + (VM,) * 8, [mix, sends] + mlp + [vm(32, 32, D)] + buffers, 6 << 30, 24, *rest, gain_attn, far_memory(w_qkv))
         else:
             state = call(bind(last_kernel, layer), specs, STATE, VM, [mix] + mlp, 4 << 30, 24, *rest)
     return state

time: 401 us -> 399 us (level)
  waiting for transfers between devices: 33.4 us -> 23.9 us
  starting transfers between devices: 50.2 us -> 55.8 us
    ppermute x16 -> x22, waiting for transfers between devices: 33.4 us -> 20.3 us  [shards(): lax.ppermute(value, axis, [(i, (i + k) % size) for i in range(size)])]
    ppermute x16 -> x22, starting transfers between devices: 21.7 us -> 29.7 us  [shards(): lax.ppermute(value, axis, [(i, (i + k) % size) for i in range(size)])]
  transfers between devices with their start and end apart: 20 -> 26, of which waited for: 13 -> 12; matrix products, arithmetic and copies ran while one was open for 0% -> 0% of each run, Pallas kernels for 76% -> 76%
where the time goes in v5:
time: 399 us; the launch traced here: 397 us
  Pallas kernels  316 us (79%)
  starting transfers between devices  55.8 us (14%)
  waiting for transfers between devices  23.9 us (6%)
    pallas_call x11, Pallas kernels, call(): pl.pallas_call(kernel, out_shape=outs, in_specs=specs, out_specs=out_spec...  316 us
    ppermute x22, starting transfers between devices, shards(): lax.ppermute(value, axis, [(i, (i + k) % size) for i in range(size)])  29.7 us
    ppermute x22, waiting for transfers between devices, shards(): lax.ppermute(value, axis, [(i, (i + k) % size) for i in range(size)])  20.3 us
    all_to_all x2, starting transfers between devices, shards(): c = lax.all_to_all(c, COL, 0, 0, tiled=True)  15.8 us
    all_to_all x2, starting transfers between devices, shards(): hc = lax.all_to_all(hc, COL, 0, 0, tiled=True)  10.3 us
  transfers between devices with their start and end apart: 26, of which 12 were waited for; matrix products, arithmetic and copies ran while one was open for 0% of the time, Pallas kernels for 76%

profile of v5, /device:TPU:1, one launch (start us, length us, event | category | flops | bytes accessed | tf_op | source)
XLA Modules:
  0.0 397.5 jit_solution(12273829991954124714)
XLA Ops:
  0.0 0.1 pad_add_fusion.pos.refs_0_
  0.1 3.9 shard_map.73
  4.0 7.8 %all-to-all-start = ((bf16[16,96,256]{2,1,0:T(8,128)(2,1)}), bf16[16,96,256]{2,1,0:T(8,128)(2,1)S(1)}, u32[]{:S(2)}, u32[]{:S(2)}) async-start(bf16[16,96,256]{2,1,0:T(8,128)(2,1)} %get-tuple-element.36), calls=%async_computation | async-start | bytes 1572864 | tf_op jit(solution)/shard_map/all_to_all | solution.py:309
  11.8 1.2 collective-permute-start.3
  13.1 2.5 collective-permute-start.4
  15.5 1.2 collective-permute-start.5
  16.7 0.3 collective-permute-start
  17.0 0.9 collective-permute-start.1
  17.8 1.5 collective-permute-start.2
  19.4 1.0 collective-permute-done.4.refs_2_
  20.4 2.7 collective-permute-start.6
  23.1 1.6 all-to-all-done.a_ref
  24.7 100.6 %shard_map.74 = bf16[16,32,256]{2,1,0:T(8,128)(2,1)} custom-call(bf16[16,96,256]{2,1,0:T(8,128)(2,1)S(1)} %all-to-all-done.a_ref), custom_call_target="tpu_custom_call" | custom-call | flops 34359738368 | bytes 1048576 | tf_op jit(solution)/shard_map/pallas_call | solution.py:282
  125.3 5.3 %all-to-all-start.1 = ((bf16[16,32,256]{2,1,0:T(8,128)(2,1)}), bf16[16,32,256]{2,1,0:T(8,128)(2,1)S(1)}, u32[]{:S(2)}, u32[]{:S(2)}) async-start(bf16[16,32,256]{2,1,0:T(8,128)(2,1)} %shard_map.74), calls=%async_computation.1 | async-start | bytes 524288 | tf_op jit(solution)/shard_map/all_to_all | solution.py:317
  130.5 0.0 copy-start
  130.6 50.4 %shard_map.76 = (bf16[4,2,32,256]{3,2,1,0:T(8,128)(2,1)S(1)}, bf16[4,2,32,256]{3,2,1,0:T(8,128)(2,1)S(1)}) custom-call(bf16[2,96,256]{2,1,0:T(8,128)(2,1)S(1)} %get-tuple-element.37.n0, bf16[2,96,256]{2,1,0:T(8,128)(2,1)S(1)} %collective-permute-done.n1, bf16[2,96,256]{2,1,0:T(8,128)(2,1)S(1)} %collective-permute-done.1.n2, ...), custom_call_target="tpu_custom_call" | custom-call | flops 17179869184 | bytes 1048576 | tf_op jit(solution)/shard_map/pallas_call | solution.py:282
  181.0 0.0 copy-start.1
  181.0 1.9 collective-permute-start.7
  182.9 4.8 %collective-permute-done.7.far = bf16[4,2,32,256]{3,2,1,0:T(8,128)(2,1)S(1)} collective-permute-done((bf16[4,2,32,256]{3,2,1,0:T(8,128)(2,1)S(1)}, bf16[4,2,32,256]{3,2,1,0:T(8,128)(2,1)S(1)}, u32[]{:S(2)}, u32[]{:S(2)}) %collective-permute-start.7) | collective-permute-done | bytes 131104 | tf_op jit(solution)/shard_map/ppermute | solution.py:301
  187.7 0.6 collective-permute-start.10
  188.4 2.1 collective-permute-start.8
  190.5 1.4 collective-permute-start.9
  191.9 0.2 collective-permute-done.10.refs_6_
  192.1 3.0 collective-permute-done.9.refs_5_
  195.1 5.3 %shard_map.78 = (bf16[32,32,256]{2,1,0:T(8,128)(2,1)}, bf16[16,96,256]{2,1,0:T(8,128)(2,1)}, bf16[2,96,256]{2,1,0:T(8,128)(2,1)S(1)}, bf16[2,96,256]{2,1,0:T(8,1...) custom-call(s32[2]{0:T(128)S(1)} %pad_add_fusion.pos.refs_0_, ...), custom_call_target="tpu_custom_call" | custom-call | flops 6442450944 | bytes 1048576 | tf_op jit(solution)/shard_map/pallas_call | solution.py:282
  200.4 0.6 copy-done.5
  201.1 0.0 copy-done.8
  201.1 8.0 %all-to-all-start.2 = ((bf16[16,96,256]{2,1,0:T(8,128)(2,1)}), bf16[16,96,256]{2,1,0:T(8,128)(2,1)S(1)}, u32[]{:S(2)}, u32[]{:S(2)}) async-start(bf16[16,96,256]{2,1,0:T(8,128)(2,1)} %get-tuple-element.52), calls=%async_computation.2 | async-start | bytes 1572864 | tf_op jit(solution)/shard_map/all_to_all | solution.py:309
  209.1 1.6 collective-permute-start.15
  210.7 1.9 collective-permute-start.16
  212.6 1.6 collective-permute-start.12
  214.1 2.6 collective-permute-done.14.refs_1_
  216.7 0.2 collective-permute-done.16.refs_3_
  216.9 0.9 copy-done.6
  217.8 1.8 collective-permute-start.17
  219.6 2.0 all-to-all-done.2.a_ref
  221.7 100.6 %shard_map.79 = bf16[16,32,256]{2,1,0:T(8,128)(2,1)} custom-call(bf16[16,96,256]{2,1,0:T(8,128)(2,1)S(1)} %all-to-all-done.2.a_ref), custom_call_target="tpu_custom_call" | custom-call | flops 34359738368 | bytes 1048576 | tf_op jit(solution)/shard_map/pallas_call | solution.py:282
  322.2 5.0 %all-to-all-start.3 = ((bf16[16,32,256]{2,1,0:T(8,128)(2,1)}), bf16[16,32,256]{2,1,0:T(8,128)(2,1)S(1)}, u32[]{:S(2)}, u32[]{:S(2)}) async-start(bf16[16,32,256]{2,1,0:T(8,128)(2,1)} %shard_map.79), calls=%async_computation.3 | async-start | bytes 524288 | tf_op jit(solution)/shard_map/all_to_all | solution.py:317
  327.3 50.6 %shard_map.81 = (bf16[4,2,32,256]{3,2,1,0:T(8,128)(2,1)S(1)}, bf16[4,2,32,256]{3,2,1,0:T(8,128)(2,1)S(1)}) custom-call(bf16[2,96,256]{2,1,0:T(8,128)(2,1)S(1)} %copy-done.9, bf16[2,96,256]{2,1,0:T(8,128)(2,1)S(1)} %collective-permute-done.11.n1, bf16[2,96,256]{2,1,0:T(8,128)(2,1)S(1)} %collective-permute-done.12.n2, ...), custom_call_target="tpu_custom_call" | custom-call | flops 17179869184 | bytes 1048576 | tf_op jit(solution)/shard_map/pallas_call | solution.py:282
  377.9 2.7 collective-permute-start.18
  380.6 3.9 collective-permute-done.18.far
  384.5 3.3 collective-permute-start.19
  387.7 0.6 collective-permute-start.20
  388.3 0.1 collective-permute-start.21
  388.4 1.2 collective-permute-done.19.refs_4_
  389.6 2.8 collective-permute-done.20.refs_5_
  392.4 0.7 collective-permute-done.21.refs_6_
  393.1 4.2 %shard_map.83 = bf16[32,32,256]{2,1,0:T(8,128)(2,1)} custom-call(s32[2]{0:T(128)S(1)} %pad_add_fusion.pos.refs_0_, bf16[32,32,256]{2,1,0:T(8,128)(2,1)S(1)} %copy-done.7, bf16[16,32,256]{2,1,0:T(8,128)(2,1)S(1)} %all-to-all-done.3.refs_2_, bf16[2,2,32,256]{3,2,1,0:T(8,128)(2,1)S(1)} %get-tuple-element.63.refs_3_, ...), custom_call_target="tpu_custom_call" | custom-call | flops 4294967296 | bytes 1048576 | tf_op jit(solution)/shard_map/pallas_call | solution.py:282
  (36 shorter events, 0.2 us)
Async XLA Ops:
  4.0 20.7 %all-to-all-start = ((bf16[16,96,256]{2,1,0:T(8,128)(2,1)}), bf16[16,96,256]{2,1,0:T(8,128)(2,1)S(1)}, u32[]{:S(2)}, u32[]{:S(2)}) async-start(bf16[16,96,256]{2,1,0:T(8,128)(2,1)} %get-tuple-element.36), calls=%async_computation | async-start | bytes 1572864 | tf_op jit(solution)/shard_map/all_to_all | solution.py:309
  11.8 6.0 %collective-permute-start.3 = (bf16[2,96,256]{2,1,0:T(8,128)(2,1)S(1)}, bf16[2,96,256]{2,1,0:T(8,128)(2,1)S(1)}, u32[]{:S(2)}, u32[]{:S(2)}) collective-permute-start(bf16[2,96,256]{2,1,0:T(8,128)(2,1)S(1)} %get-tuple-element.42), channel_id=1, source_target_pairs={{0,32},{32,64},{64,96},{96,0},{1,33},{33,65},{65,97},{97,1},{2,34}... | collective-permute-start | bytes 294920 | tf_op jit(solution)/shard_map/ppermute | solution.py:301
  13.1 7.3 %collective-permute-start.4 = (bf16[2,96,256]{2,1,0:T(8,128)(2,1)S(1)}, bf16[2,96,256]{2,1,0:T(8,128)(2,1)S(1)}, u32[]{:S(2)}, u32[]{:S(2)}) collective-permute-start(bf16[2,96,256]{2,1,0:T(8,128)(2,1)S(1)} %get-tuple-element.43), channel_id=1, source_target_pairs={{0,64},{32,96},{64,0},{96,32},{1,65},{33,97},{65,1},{97,33},{2,66}... | collective-permute-start | bytes 294920 | tf_op jit(solution)/shard_map/ppermute | solution.py:301
  15.5 4.8 %collective-permute-start.5 = (bf16[2,96,256]{2,1,0:T(8,128)(2,1)S(1)}, bf16[2,96,256]{2,1,0:T(8,128)(2,1)S(1)}, u32[]{:S(2)}, u32[]{:S(2)}) collective-permute-start(bf16[2,96,256]{2,1,0:T(8,128)(2,1)S(1)} %get-tuple-element.44), channel_id=1, source_target_pairs={{0,96},{32,0},{64,32},{96,64},{1,97},{33,1},{65,33},{97,65},{2,98}... | collective-permute-start | bytes 294920 | tf_op jit(solution)/shard_map/ppermute | solution.py:301
  16.7 113.9 %collective-permute-start = (bf16[2,96,256]{2,1,0:T(8,128)(2,1)S(1)}, bf16[2,96,256]{2,1,0:T(8,128)(2,1)S(1)}, u32[]{:S(2)}, u32[]{:S(2)}) collective-permute-start(bf16[2,96,256]{2,1,0:T(8,128)(2,1)S(1)} %get-tuple-element.38), channel_id=1, source_target_pairs={{0,32},{32,64},{64,96},{96,0},{1,33},{33,65},{65,97},{97,1},{2,34}... | collective-permute-start | bytes 294920 | tf_op jit(solution)/shard_map/ppermute | solution.py:301
  17.0 113.5 %collective-permute-start.1 = (bf16[2,96,256]{2,1,0:T(8,128)(2,1)S(1)}, bf16[2,96,256]{2,1,0:T(8,128)(2,1)S(1)}, u32[]{:S(2)}, u32[]{:S(2)}) collective-permute-start(bf16[2,96,256]{2,1,0:T(8,128)(2,1)S(1)} %get-tuple-element.39), channel_id=1, source_target_pairs={{0,64},{32,96},{64,0},{96,32},{1,65},{33,97},{65,1},{97,33},{2,66}... | collective-permute-start | bytes 294920 | tf_op jit(solution)/shard_map/ppermute | solution.py:301
  17.8 112.7 %collective-permute-start.2 = (bf16[2,96,256]{2,1,0:T(8,128)(2,1)S(1)}, bf16[2,96,256]{2,1,0:T(8,128)(2,1)S(1)}, u32[]{:S(2)}, u32[]{:S(2)}) collective-permute-start(bf16[2,96,256]{2,1,0:T(8,128)(2,1)S(1)} %get-tuple-element.40), channel_id=1, source_target_pairs={{0,96},{32,0},{64,32},{96,64},{1,97},{33,1},{65,33},{97,65},{2,98}... | collective-permute-start | bytes 294920 | tf_op jit(solution)/shard_map/ppermute | solution.py:301
  20.4 110.2 %collective-permute-start.6 = (bf16[4,2,96,256]{3,2,1,0:T(8,128)(2,1)S(1)}, bf16[4,2,96,256]{3,2,1,0:T(8,128)(2,1)S(1)}, u32[]{:S(2)}, u32[]{:S(2)}) collective-permute-start(bf16[4,2,96,256]{3,2,1,0:T(8,128)(2,1)S(1)} %shard_map.75), channel_id=1, source_target_pairs={{0,16},{16,0},{1,17},{17,1},{2,18},{18,2},{3,19},{19,3},{4,20},{20... | collective-permute-start | bytes 1179656 | tf_op jit(solution)/shard_map/ppermute | solution.py:301
  125.3 69.8 %all-to-all-start.1 = ((bf16[16,32,256]{2,1,0:T(8,128)(2,1)}), bf16[16,32,256]{2,1,0:T(8,128)(2,1)S(1)}, u32[]{:S(2)}, u32[]{:S(2)}) async-start(bf16[16,32,256]{2,1,0:T(8,128)(2,1)} %shard_map.74), calls=%async_computation.1 | async-start | bytes 524288 | tf_op jit(solution)/shard_map/all_to_all | solution.py:317
  130.5 64.6 %copy-start = (bf16[2,256,1024]{2,1,0:T(8,128)(2,1)S(1)}, bf16[2,256,1024]{2,1,0:T(8,128)(2,1)}, u32[]{:S(2)}) copy-start(bf16[2,256,1024]{2,1,0:T(8,128)(2,1)} %refs_9_.3) | copy-start | bytes 3145732
  181.0 14.1 %copy-start.1 = (bf16[32,32,256]{2,1,0:T(8,128)(2,1)S(1)}, bf16[32,32,256]{2,1,0:T(8,128)(2,1)}, u32[]{:S(2)}) copy-start(bf16[32,32,256]{2,1,0:T(8,128)(2,1)} %refs_1_.1) | copy-start | bytes 1572868
  181.0 6.7 %collective-permute-start.7 = (bf16[4,2,32,256]{3,2,1,0:T(8,128)(2,1)S(1)}, bf16[4,2,32,256]{3,2,1,0:T(8,128)(2,1)S(1)}, u32[]{:S(2)}, u32[]{:S(2)}) collective-permute-start(bf16[4,2,32,256]{3,2,1,0:T(8,128)(2,1)S(1)} %get-tuple-element.46), channel_id=1, source_target_pairs={{0,16},{16,0},{1,17},{17,1},{2,18},{18,2},{3,19},{19,3},{4,20},{20... | collective-permute-start | bytes 393224 | tf_op jit(solution)/shard_map/ppermute | solution.py:301
  187.7 7.4 %copy-start.2 = (bf16[2,256,256]{2,1,0:T(8,128)(2,1)S(1)}, bf16[2,256,256]{2,1,0:T(8,128)(2,1)}, u32[]{:S(2)}) copy-start(bf16[2,256,256]{2,1,0:T(8,128)(2,1)} %refs_7_.3) | copy-start | bytes 786436
  187.7 4.4 %collective-permute-start.10 = (bf16[2,2,32,256]{3,2,1,0:T(8,128)(2,1)S(1)}, bf16[2,2,32,256]{3,2,1,0:T(8,128)(2,1)S(1)}, u32[]{:S(2)}, u32[]{:S(2)}) collective-permute-start(bf16[2,2,32,256]{3,2,1,0:T(8,128)(2,1)S(1)} %get-tuple-element.50), channel_id=1, source_target_pairs={{0,32},{32,64},{64,96},{96,0},{1,33},{33,65},{65,97},{97,1},{2,34}... | collective-permute-start | bytes 196616 | tf_op jit(solution)/shard_map/ppermute | solution.py:301
  188.4 6.7 %copy-start.4 = (f32[2,256]{1,0:T(2,128)S(1)}, f32[2,256]{1,0:T(2,128)}, u32[]{:S(2)}) copy-start(f32[2,256]{1,0:T(2,128)} %refs_8_.3) | copy-start | bytes 6148
  188.4 6.8 %copy-start.3 = (f32[2,256]{1,0:T(2,128)S(1)}, f32[2,256]{1,0:T(2,128)}, u32[]{:S(2)}) copy-start(f32[2,256]{1,0:T(2,128)} %refs_11_.1) | copy-start | bytes 6148
  188.4 3.7 collective-permute-start.8
  190.5 4.6 %collective-permute-start.9 = (bf16[2,2,32,256]{3,2,1,0:T(8,128)(2,1)S(1)}, bf16[2,2,32,256]{3,2,1,0:T(8,128)(2,1)S(1)}, u32[]{:S(2)}, u32[]{:S(2)}) collective-permute-start(bf16[2,2,32,256]{3,2,1,0:T(8,128)(2,1)S(1)} %get-tuple-element.49), channel_id=1, source_target_pairs={{0,64},{32,96},{64,0},{96,32},{1,65},{33,97},{65,1},{97,33},{2,66}... | collective-permute-start | bytes 196616 | tf_op jit(solution)/shard_map/ppermute | solution.py:301
  200.4 0.6 copy-start.5
  200.4 0.7 copy-start.8
  201.1 20.6 %all-to-all-start.2 = ((bf16[16,96,256]{2,1,0:T(8,128)(2,1)}), bf16[16,96,256]{2,1,0:T(8,128)(2,1)S(1)}, u32[]{:S(2)}, u32[]{:S(2)}) async-start(bf16[16,96,256]{2,1,0:T(8,128)(2,1)} %get-tuple-element.52), calls=%async_computation.2 | async-start | bytes 1572864 | tf_op jit(solution)/shard_map/all_to_all | solution.py:309
  209.1 7.6 %collective-permute-start.14 = (bf16[2,96,256]{2,1,0:T(8,128)(2,1)S(1)}, bf16[2,96,256]{2,1,0:T(8,128)(2,1)S(1)}, u32[]{:S(2)}, u32[]{:S(2)}) collective-permute-start(bf16[2,96,256]{2,1,0:T(8,128)(2,1)S(1)} %get-tuple-element.58), channel_id=1, source_target_pairs={{0,32},{32,64},{64,96},{96,0},{1,33},{33,65},{65,97},{97,1},{2,34}... | collective-permute-start | bytes 294920 | tf_op jit(solution)/shard_map/ppermute | solution.py:301
  209.1 7.6 %collective-permute-start.15 = (bf16[2,96,256]{2,1,0:T(8,128)(2,1)S(1)}, bf16[2,96,256]{2,1,0:T(8,128)(2,1)S(1)}, u32[]{:S(2)}, u32[]{:S(2)}) collective-permute-start(bf16[2,96,256]{2,1,0:T(8,128)(2,1)S(1)} %get-tuple-element.59), channel_id=1, source_target_pairs={{0,64},{32,96},{64,0},{96,32},{1,65},{33,97},{65,1},{97,33},{2,66}... | collective-permute-start | bytes 294920 | tf_op jit(solution)/shard_map/ppermute | solution.py:301
  210.7 6.2 %collective-permute-start.16 = (bf16[2,96,256]{2,1,0:T(8,128)(2,1)S(1)}, bf16[2,96,256]{2,1,0:T(8,128)(2,1)S(1)}, u32[]{:S(2)}, u32[]{:S(2)}) collective-permute-start(bf16[2,96,256]{2,1,0:T(8,128)(2,1)S(1)} %get-tuple-element.60), channel_id=1, source_target_pairs={{0,96},{32,0},{64,32},{96,64},{1,97},{33,1},{65,33},{97,65},{2,98}... | collective-permute-start | bytes 294920 | tf_op jit(solution)/shard_map/ppermute | solution.py:301
  212.6 114.7 %collective-permute-start.11 = (bf16[2,96,256]{2,1,0:T(8,128)(2,1)S(1)}, bf16[2,96,256]{2,1,0:T(8,128)(2,1)S(1)}, u32[]{:S(2)}, u32[]{:S(2)}) collective-permute-start(bf16[2,96,256]{2,1,0:T(8,128)(2,1)S(1)} %get-tuple-element.54), channel_id=1, source_target_pairs={{0,32},{32,64},{64,96},{96,0},{1,33},{33,65},{65,97},{97,1},{2,34}... | collective-permute-start | bytes 294920 | tf_op jit(solution)/shard_map/ppermute | solution.py:301
  212.6 114.7 %collective-permute-start.12 = (bf16[2,96,256]{2,1,0:T(8,128)(2,1)S(1)}, bf16[2,96,256]{2,1,0:T(8,128)(2,1)S(1)}, u32[]{:S(2)}, u32[]{:S(2)}) collective-permute-start(bf16[2,96,256]{2,1,0:T(8,128)(2,1)S(1)} %get-tuple-element.55), channel_id=1, source_target_pairs={{0,64},{32,96},{64,0},{96,32},{1,65},{33,97},{65,1},{97,33},{2,66}... | collective-permute-start | bytes 294920 | tf_op jit(solution)/shard_map/ppermute | solution.py:301
  216.7 110.5 %collective-permute-start.13 = (bf16[2,96,256]{2,1,0:T(8,128)(2,1)S(1)}, bf16[2,96,256]{2,1,0:T(8,128)(2,1)S(1)}, u32[]{:S(2)}, u32[]{:S(2)}) collective-permute-start(bf16[2,96,256]{2,1,0:T(8,128)(2,1)S(1)} %get-tuple-element.56), channel_id=1, source_target_pairs={{0,96},{32,0},{64,32},{96,64},{1,97},{33,1},{65,33},{97,65},{2,98}... | collective-permute-start | bytes 294920 | tf_op jit(solution)/shard_map/ppermute | solution.py:301
  216.9 0.9 copy-start.6
  217.8 109.4 %collective-permute-start.17 = (bf16[4,2,96,256]{3,2,1,0:T(8,128)(2,1)S(1)}, bf16[4,2,96,256]{3,2,1,0:T(8,128)(2,1)S(1)}, u32[]{:S(2)}, u32[]{:S(2)}) collective-permute-start(bf16[4,2,96,256]{3,2,1,0:T(8,128)(2,1)S(1)} %shard_map.80), channel_id=1, source_target_pairs={{0,16},{16,0},{1,17},{17,1},{2,18},{18,2},{3,19},{19,3},{4,20},{20... | collective-permute-start | bytes 1179656 | tf_op jit(solution)/shard_map/ppermute | solution.py:301
  322.2 5.1 %copy-start.9 = (bf16[2,96,256]{2,1,0:T(8,128)(2,1)S(1)}, bf16[2,96,256]{2,1,0:T(8,128)(2,1)}, u32[]{:S(2)}) copy-start(bf16[2,96,256]{2,1,0:T(8,128)(2,1)} %copy-done.8) | copy-start | bytes 294916
  322.2 70.8 %all-to-all-start.3 = ((bf16[16,32,256]{2,1,0:T(8,128)(2,1)}), bf16[16,32,256]{2,1,0:T(8,128)(2,1)S(1)}, u32[]{:S(2)}, u32[]{:S(2)}) async-start(bf16[16,32,256]{2,1,0:T(8,128)(2,1)} %shard_map.79), calls=%async_computation.3 | async-start | bytes 524288 | tf_op jit(solution)/shard_map/all_to_all | solution.py:317
  377.9 15.1 %copy-start.7 = (bf16[32,32,256]{2,1,0:T(8,128)(2,1)S(1)}, bf16[32,32,256]{2,1,0:T(8,128)(2,1)}, u32[]{:S(2)}) copy-start(bf16[32,32,256]{2,1,0:T(8,128)(2,1)} %get-tuple-element.51.refs_1_) | copy-start | bytes 1572868
  377.9 6.5 %collective-permute-start.18 = (bf16[4,2,32,256]{3,2,1,0:T(8,128)(2,1)S(1)}, bf16[4,2,32,256]{3,2,1,0:T(8,128)(2,1)S(1)}, u32[]{:S(2)}, u32[]{:S(2)}) collective-permute-start(bf16[4,2,32,256]{3,2,1,0:T(8,128)(2,1)S(1)} %get-tuple-element.62), channel_id=1, source_target_pairs={{0,16},{16,0},{1,17},{17,1},{2,18},{18,2},{3,19},{19,3},{4,20},{20... | collective-permute-start | bytes 393224 | tf_op jit(solution)/shard_map/ppermute | solution.py:301
  384.5 5.2 %collective-permute-start.19 = (bf16[2,2,32,256]{3,2,1,0:T(8,128)(2,1)S(1)}, bf16[2,2,32,256]{3,2,1,0:T(8,128)(2,1)S(1)}, u32[]{:S(2)}, u32[]{:S(2)}) collective-permute-start(bf16[2,2,32,256]{3,2,1,0:T(8,128)(2,1)S(1)} %get-tuple-element.64), channel_id=1, source_target_pairs={{0,96},{32,0},{64,32},{96,64},{1,97},{33,1},{65,33},{97,65},{2,98}... | collective-permute-start | bytes 196616 | tf_op jit(solution)/shard_map/ppermute | solution.py:301
  387.7 4.7 %collective-permute-start.20 = (bf16[2,2,32,256]{3,2,1,0:T(8,128)(2,1)S(1)}, bf16[2,2,32,256]{3,2,1,0:T(8,128)(2,1)S(1)}, u32[]{:S(2)}, u32[]{:S(2)}) collective-permute-start(bf16[2,2,32,256]{3,2,1,0:T(8,128)(2,1)S(1)} %get-tuple-element.65), channel_id=1, source_target_pairs={{0,64},{32,96},{64,0},{96,32},{1,65},{33,97},{65,1},{97,33},{2,66}... | collective-permute-start | bytes 196616 | tf_op jit(solution)/shard_map/ppermute | solution.py:301
  388.3 4.8 %collective-permute-start.21 = (bf16[2,2,32,256]{3,2,1,0:T(8,128)(2,1)S(1)}, bf16[2,2,32,256]{3,2,1,0:T(8,128)(2,1)S(1)}, u32[]{:S(2)}, u32[]{:S(2)}) collective-permute-start(bf16[2,2,32,256]{3,2,1,0:T(8,128)(2,1)S(1)} %get-tuple-element.66), channel_id=1, source_target_pairs={{0,32},{32,64},{64,96},{96,0},{1,33},{33,65},{65,97},{97,1},{2,34}... | collective-permute-start | bytes 196616 | tf_op jit(solution)/shard_map/ppermute | solution.py:301

commit v6 on v5

--- a/solution.py
+++ b/solution.py
@@ -204,7 +204,7 @@
     save.wait()
 
 
-def finish(layer, pos, x_ref, hc_ref, heads, wo_ref, gain_ref, wu_ref, wd, ready, mix, hv, n2, put):
+def finish(layer, pos, x_ref, hc_ref, heads, wo_ref, gain_ref, wu, wd, ready, mix, hv, n2, put):
     cdot = lambda h, w: lax.dot_general(h, w, (((0,), (0,)), ((), ())), preferred_element_type=F32)
     for k in range(4):
         at = 2 * ((pos[0] + k) % 4)
@@ -222,15 +222,15 @@
         n2[256 * b:256 * b + 256, :] = norm(mixed, gain_ref[layer:layer + 1]).astype(BF)
     ready()
     for b in range(4):
-        up = jnp.dot(n2[256 * b:256 * b + 256, :], wu_ref[layer], preferred_element_type=F32)
+        up = jnp.dot(n2[256 * b:256 * b + 256, :], wu[...], preferred_element_type=F32)
         act = 0.5 * up * (1.0 + jnp.tanh(0.7978845608028654 * (up + 0.044715 * (up * up * up))))
         out = jnp.dot(act.astype(BF), wd[...], preferred_element_type=F32)
         put(b, (mix[8 * b:8 * b + 8].reshape(256, D) + out).astype(BF))
 
 
-def mid_kernel(layer, pos, x_ref, hc_ref, h0, h1, h2, h3, wo_ref, gm_ref, wu_ref, wd_hbm, ga_ref, w_hbm, y_hbm, c_hbm, *rest):
-    outs, (mix, sends, wd, hv, n2, sems, y, w, c) = rest[:8], rest[8:]
-    loads = [pltpu.make_async_copy(wd_hbm.at[layer], wd, sems.at[0]), pltpu.make_async_copy(w_hbm.at[layer + 1], w, sems.at[1])]
+def mid_kernel(layer, pos, x_ref, hc_ref, h0, h1, h2, h3, wo_ref, gm_ref, wu_hbm, wd_hbm, ga_ref, w_hbm, y_hbm, c_hbm, *rest):
+    outs, (mix, sends, wd, wu, hv, n2, sems, y, w, c) = rest[:8], rest[8:]
+    loads = [pltpu.make_async_copy(wu_hbm.at[layer], wu, sems.at[4]), pltpu.make_async_copy(wd_hbm.at[layer], wd, sems.at[0]), pltpu.make_async_copy(w_hbm.at[layer + 1], w, sems.at[1])]
     saves = [pltpu.make_async_copy(y, y_hbm, sems.at[2]), pltpu.make_async_copy(c, c_hbm, sems.at[3])]
     for copy in loads:
         copy.start()
@@ -246,7 +246,7 @@
         for copy in saves:
             copy.start()
 
-    finish(layer, pos, x_ref, hc_ref, (h0, h1, h2, h3), wo_ref, gm_ref, wu_ref, wd, ready, mix, hv, n2, put)
+    finish(layer, pos, x_ref, hc_ref, (h0, h1, h2, h3), wo_ref, gm_ref, wu, wd, ready, mix, hv, n2, put)
     project(lambda b: y[8 * b:8 * b + 8].reshape(256, D).astype(F32), pos, ga_ref[layer + 1:layer + 2], w, c, sends, mix, sent)
     for k in range(4):
         for e in range(2):
@@ -255,14 +255,19 @@
         copy.wait()
 
 
-def last_kernel(layer, pos, x_ref, hc_ref, h0, h1, h2, h3, wo_ref, gm_ref, wu_ref, wd_hbm, y_ref, mix, wd, hv, n2, sems):
-    load = pltpu.make_async_copy(wd_hbm.at[layer], wd, sems.at[0])
-    load.start()
+def last_kernel(layer, pos, x_ref, hc_ref, h0, h1, h2, h3, wo_ref, gm_ref, wu_hbm, wd_hbm, y_ref, mix, wd, wu, hv, n2, sems):
+    loads = [pltpu.make_async_copy(wu_hbm.at[layer], wu, sems.at[4]), pltpu.make_async_copy(wd_hbm.at[layer], wd, sems.at[0])]
+    for copy in loads:
+        copy.start()
+
+    def ready():
+        for copy in loads:
+            copy.wait()
 
     def put(b, v):
         y_ref[8 * b:8 * b + 8] = v.reshape(8, 32, D)
 
-    finish(layer, pos, x_ref, hc_ref, (h0, h1, h2, h3), wo_ref, gm_ref, wu_ref, wd, load.wait, mix, hv, n2, put)
+    finish(layer, pos, x_ref, hc_ref, (h0, h1, h2, h3), wo_ref, gm_ref, wu, wd, ready, mix, hv, n2, put)
 
 
 VM = pl.BlockSpec(memory_space=pltpu.VMEM)
@@ -275,7 +280,7 @@
 STATE = jax.ShapeDtypeStruct((32, 32, D), BF)
 HBM_ACROSS = pltpu.HBM((16, 96, 256), BF)
 HBM_STATE = pltpu.HBM((32, 32, D), BF)
-SEMS = pltpu.SemaphoreType.DMA((4,))
+SEMS = pltpu.SemaphoreType.DMA((5,))
 
 
 def call(kernel, specs, outs, out_specs, scratch, flops, limit, *args):
@@ -302,7 +307,7 @@
     state = frame
     sends = vm(4, 2, 2, 96, 256)
     mix = vm(32, 32, D, dtype=F32)
-    mlp = [vm(4 * D, D), vm(8, 2, 32, 256), vm(4 * D, D), SEMS]
+    mlp = [vm(4 * D, D), vm(D, 4 * D), vm(8, 2, 32, 256), vm(4 * D, D), SEMS]
     buffers = [vm(D, 3 * D), vm(16, 96, 256)]
     c, *r = call(first_kernel, [SM] + [HB] * 3, (HBM_ACROSS,) + (BLOCK,) * 8, (HB,) + (VM,) * 8, [mix, sends, vm(32, 32, D), vm(LAYERS, D, dtype=F32), buffers[0], SEMS, buffers[1]], 2 << 30, 12, pos, *map(far_memory, (state, gain_attn, w_qkv)))
     for layer in range(LAYERS):
@@ -317,8 +322,8 @@
         hc = lax.all_to_all(hc, COL, 0, 0, tiled=True)
         o = call(pair_kernel, [VM] * 2, (REPLY,) * 4, (VM,) * 4, [], 1 << 28, 4, near, far)
         o = [o[0]] + [shift(o[k], "x", 4 - k, 4) for k in (1, 2, 3)]
-        rest = (pos, state, hc, *o, w_out, gain_mlp, w_up, far_memory(w_down))
-        specs = [SM] + [VM] * 9 + [HB]
+        rest = (pos, state, hc, *o, w_out, gain_mlp, far_memory(w_up), far_memory(w_down))
+        specs = [SM] + [VM] * 8 + [HB] * 2
         if layer + 1 < LAYERS:
             state, c, *r = call(bind(mid_kernel, layer), specs + [VM, HB], (HBM_STATE, HBM_ACROSS) + (BLOCK,) * 8, (HB, HB) + (VM,) * 8, [mix, sends] + mlp + [vm(32, 32, D)] + buffers, 6 << 30, 24, *rest, gain_attn, far_memory(w_qkv))
         else:

time: 399 us -> 398 us (level)
  no operation moved by 1% of the time
where the time goes in v6:
time: 398 us; the launch traced here: 396 us
  Pallas kernels  316 us (79%)
  starting transfers between devices  54.4 us (14%)
  waiting for transfers between devices  25.3 us (6%)
    pallas_call x11, Pallas kernels, call(): pl.pallas_call(kernel, out_shape=outs, in_specs=specs, out_specs=out_spec...  316 us
    ppermute x22, starting transfers between devices, shards(): lax.ppermute(value, axis, [(i, (i + k) % size) for i in range(size)])  28.7 us
    ppermute x22, waiting for transfers between devices, shards(): lax.ppermute(value, axis, [(i, (i + k) % size) for i in range(size)])  20.7 us
    all_to_all x2, starting transfers between devices, shards(): c = lax.all_to_all(c, COL, 0, 0, tiled=True)  15.9 us
    all_to_all x2, starting transfers between devices, shards(): hc = lax.all_to_all(hc, COL, 0, 0, tiled=True)  9.85 us
  transfers between devices with their start and end apart: 26, of which 12 were waited for; matrix products, arithmetic and copies ran while one was open for 0% of the time, Pallas kernels for 76%

profile of v6, /device:TPU:1, one launch (start us, length us, event | category | flops | bytes accessed | tf_op | source)
XLA Modules:
  0.0 396.1 jit_solution(17626691384840626127)
XLA Ops:
  0.0 0.1 pad_add_fusion.pos.refs_0_
  0.1 3.9 shard_map.73
  4.0 7.8 %all-to-all-start = ((bf16[16,96,256]{2,1,0:T(8,128)(2,1)}), bf16[16,96,256]{2,1,0:T(8,128)(2,1)S(1)}, u32[]{:S(2)}, u32[]{:S(2)}) async-start(bf16[16,96,256]{2,1,0:T(8,128)(2,1)} %get-tuple-element.36), calls=%async_computation | async-start | bytes 1572864 | tf_op jit(solution)/shard_map/all_to_all | solution.py:314
  11.8 1.2 collective-permute-start.3
  13.1 2.5 collective-permute-start.4
  15.5 1.2 collective-permute-start.5
  16.7 0.3 collective-permute-start
  17.0 0.9 collective-permute-start.1
  17.8 0.0 collective-permute-done.3.refs_1_
  17.9 1.5 collective-permute-start.2
  19.4 1.0 collective-permute-done.4.refs_2_
  20.4 2.7 collective-permute-start.6
  23.1 1.6 all-to-all-done.a_ref
  24.7 100.6 %shard_map.74 = bf16[16,32,256]{2,1,0:T(8,128)(2,1)} custom-call(bf16[16,96,256]{2,1,0:T(8,128)(2,1)S(1)} %all-to-all-done.a_ref), custom_call_target="tpu_custom_call" | custom-call | flops 34359738368 | bytes 1048576 | tf_op jit(solution)/shard_map/pallas_call | solution.py:287
  125.3 5.3 %all-to-all-start.1 = ((bf16[16,32,256]{2,1,0:T(8,128)(2,1)}), bf16[16,32,256]{2,1,0:T(8,128)(2,1)S(1)}, u32[]{:S(2)}, u32[]{:S(2)}) async-start(bf16[16,32,256]{2,1,0:T(8,128)(2,1)} %shard_map.74), calls=%async_computation.1 | async-start | bytes 524288 | tf_op jit(solution)/shard_map/all_to_all | solution.py:322
  130.5 0.0 collective-permute-done.n1
  130.5 0.0 collective-permute-done.6.got_far
  130.6 50.4 %shard_map.76 = (bf16[4,2,32,256]{3,2,1,0:T(8,128)(2,1)S(1)}, bf16[4,2,32,256]{3,2,1,0:T(8,128)(2,1)S(1)}) custom-call(bf16[2,96,256]{2,1,0:T(8,128)(2,1)S(1)} %get-tuple-element.37.n0, bf16[2,96,256]{2,1,0:T(8,128)(2,1)S(1)} %collective-permute-done.n1, bf16[2,96,256]{2,1,0:T(8,128)(2,1)S(1)} %collective-permute-done.1.n2, ...), custom_call_target="tpu_custom_call" | custom-call | flops 17179869184 | bytes 1048576 | tf_op jit(solution)/shard_map/pallas_call | solution.py:287
  181.0 0.0 copy-start
  181.0 1.9 collective-permute-start.7
  182.9 4.8 %collective-permute-done.7.far = bf16[4,2,32,256]{3,2,1,0:T(8,128)(2,1)S(1)} collective-permute-done((bf16[4,2,32,256]{3,2,1,0:T(8,128)(2,1)S(1)}, bf16[4,2,32,256]{3,2,1,0:T(8,128)(2,1)S(1)}, u32[]{:S(2)}, u32[]{:S(2)}) %collective-permute-start.7) | collective-permute-done | bytes 131104 | tf_op jit(solution)/shard_map/ppermute | solution.py:306
  187.7 0.6 collective-permute-start.10
  188.4 2.1 collective-permute-start.8
  190.5 1.4 collective-permute-start.9
  191.9 0.2 collective-permute-done.10.refs_6_
  192.1 3.0 collective-permute-done.9.refs_5_
  195.1 5.4 %shard_map.78 = (bf16[32,32,256]{2,1,0:T(8,128)(2,1)}, bf16[16,96,256]{2,1,0:T(8,128)(2,1)}, bf16[2,96,256]{2,1,0:T(8,128)(2,1)S(1)}, bf16[2,96,256]{2,1,0:T(8,1...) custom-call(s32[2]{0:T(128)S(1)} %pad_add_fusion.pos.refs_0_, ...), custom_call_target="tpu_custom_call" | custom-call | flops 6442450944 | bytes 1048576 | tf_op jit(solution)/shard_map/pallas_call | solution.py:287
  200.5 8.0 %all-to-all-start.2 = ((bf16[16,96,256]{2,1,0:T(8,128)(2,1)}), bf16[16,96,256]{2,1,0:T(8,128)(2,1)S(1)}, u32[]{:S(2)}, u32[]{:S(2)}) async-start(bf16[16,96,256]{2,1,0:T(8,128)(2,1)} %get-tuple-element.52), calls=%async_computation.2 | async-start | bytes 1572864 | tf_op jit(solution)/shard_map/all_to_all | solution.py:314
  208.5 1.6 collective-permute-start.15
  210.1 1.9 collective-permute-start.16
  212.0 1.6 collective-permute-start.12
  213.5 2.6 collective-permute-done.14.refs_1_
  216.1 0.2 collective-permute-done.16.refs_3_
  216.3 1.8 collective-permute-start.17
  218.1 2.9 all-to-all-done.2.a_ref
  221.1 100.6 %shard_map.79 = bf16[16,32,256]{2,1,0:T(8,128)(2,1)} custom-call(bf16[16,96,256]{2,1,0:T(8,128)(2,1)S(1)} %all-to-all-done.2.a_ref), custom_call_target="tpu_custom_call" | custom-call | flops 34359738368 | bytes 1048576 | tf_op jit(solution)/shard_map/pallas_call | solution.py:287
  321.6 4.6 %all-to-all-start.3 = ((bf16[16,32,256]{2,1,0:T(8,128)(2,1)}), bf16[16,32,256]{2,1,0:T(8,128)(2,1)S(1)}, u32[]{:S(2)}, u32[]{:S(2)}) async-start(bf16[16,32,256]{2,1,0:T(8,128)(2,1)} %shard_map.79), calls=%async_computation.3 | async-start | bytes 524288 | tf_op jit(solution)/shard_map/all_to_all | solution.py:322
  326.3 50.6 %shard_map.81 = (bf16[4,2,32,256]{3,2,1,0:T(8,128)(2,1)S(1)}, bf16[4,2,32,256]{3,2,1,0:T(8,128)(2,1)S(1)}) custom-call(bf16[2,96,256]{2,1,0:T(8,128)(2,1)S(1)} %get-tuple-element.53.n0, bf16[2,96,256]{2,1,0:T(8,128)(2,1)S(1)} %collective-permute-done.11.n1, bf16[2,96,256]{2,1,0:T(8,128)(2,1)S(1)} %collective-permute-done.12.n2, ...), custom_call_target="tpu_custom_call" | custom-call | flops 17179869184 | bytes 1048576 | tf_op jit(solution)/shard_map/pallas_call | solution.py:287
  376.9 0.0 copy-start.4
  376.9 2.1 collective-permute-start.18
  379.0 4.3 %collective-permute-done.18.far = bf16[4,2,32,256]{3,2,1,0:T(8,128)(2,1)S(1)} collective-permute-done((bf16[4,2,32,256]{3,2,1,0:T(8,128)(2,1)S(1)}, bf16[4,2,32,256]{3,2,1,0:T(8,128)(2,1)S(1)}, u32[]{:S(2)}, u32[]{:S(2)}) %collective-permute-start.18) | collective-permute-done | bytes 131104 | tf_op jit(solution)/shard_map/ppermute | solution.py:306
  383.3 2.8 collective-permute-start.19
  386.1 0.5 collective-permute-start.20
  386.7 0.1 collective-permute-start.21
  386.8 0.7 collective-permute-done.19.refs_4_
  387.5 3.3 collective-permute-done.20.refs_5_
  390.8 0.7 collective-permute-done.21.refs_6_
  391.5 4.5 %shard_map.83 = bf16[32,32,256]{2,1,0:T(8,128)(2,1)} custom-call(s32[2]{0:T(128)S(1)} %pad_add_fusion.pos.refs_0_, bf16[32,32,256]{2,1,0:T(8,128)(2,1)S(1)} %copy-done.4, bf16[16,32,256]{2,1,0:T(8,128)(2,1)S(1)} %all-to-all-done.3.refs_2_, bf16[2,2,32,256]{3,2,1,0:T(8,128)(2,1)S(1)} %get-tuple-element.63.refs_3_, ...), custom_call_target="tpu_custom_call" | custom-call | flops 4294967296 | bytes 1048576 | tf_op jit(solution)/shard_map/pallas_call | solution.py:287
  (26 shorter events, 0.1 us)
Async XLA Ops:
  4.0 20.7 %all-to-all-start = ((bf16[16,96,256]{2,1,0:T(8,128)(2,1)}), bf16[16,96,256]{2,1,0:T(8,128)(2,1)S(1)}, u32[]{:S(2)}, u32[]{:S(2)}) async-start(bf16[16,96,256]{2,1,0:T(8,128)(2,1)} %get-tuple-element.36), calls=%async_computation | async-start | bytes 1572864 | tf_op jit(solution)/shard_map/all_to_all | solution.py:314
  11.8 6.0 %collective-permute-start.3 = (bf16[2,96,256]{2,1,0:T(8,128)(2,1)S(1)}, bf16[2,96,256]{2,1,0:T(8,128)(2,1)S(1)}, u32[]{:S(2)}, u32[]{:S(2)}) collective-permute-start(bf16[2,96,256]{2,1,0:T(8,128)(2,1)S(1)} %get-tuple-element.42), channel_id=1, source_target_pairs={{0,32},{32,64},{64,96},{96,0},{1,33},{33,65},{65,97},{97,1},{2,34}... | collective-permute-start | bytes 294920 | tf_op jit(solution)/shard_map/ppermute | solution.py:306
  13.1 7.3 %collective-permute-start.4 = (bf16[2,96,256]{2,1,0:T(8,128)(2,1)S(1)}, bf16[2,96,256]{2,1,0:T(8,128)(2,1)S(1)}, u32[]{:S(2)}, u32[]{:S(2)}) collective-permute-start(bf16[2,96,256]{2,1,0:T(8,128)(2,1)S(1)} %get-tuple-element.43), channel_id=1, source_target_pairs={{0,64},{32,96},{64,0},{96,32},{1,65},{33,97},{65,1},{97,33},{2,66}... | collective-permute-start | bytes 294920 | tf_op jit(solution)/shard_map/ppermute | solution.py:306
  15.5 4.8 %collective-permute-start.5 = (bf16[2,96,256]{2,1,0:T(8,128)(2,1)S(1)}, bf16[2,96,256]{2,1,0:T(8,128)(2,1)S(1)}, u32[]{:S(2)}, u32[]{:S(2)}) collective-permute-start(bf16[2,96,256]{2,1,0:T(8,128)(2,1)S(1)} %get-tuple-element.44), channel_id=1, source_target_pairs={{0,96},{32,0},{64,32},{96,64},{1,97},{33,1},{65,33},{97,65},{2,98}... | collective-permute-start | bytes 294920 | tf_op jit(solution)/shard_map/ppermute | solution.py:306
  16.7 113.9 %collective-permute-start = (bf16[2,96,256]{2,1,0:T(8,128)(2,1)S(1)}, bf16[2,96,256]{2,1,0:T(8,128)(2,1)S(1)}, u32[]{:S(2)}, u32[]{:S(2)}) collective-permute-start(bf16[2,96,256]{2,1,0:T(8,128)(2,1)S(1)} %get-tuple-element.38), channel_id=1, source_target_pairs={{0,32},{32,64},{64,96},{96,0},{1,33},{33,65},{65,97},{97,1},{2,34}... | collective-permute-start | bytes 294920 | tf_op jit(solution)/shard_map/ppermute | solution.py:306
  17.0 113.6 %collective-permute-start.1 = (bf16[2,96,256]{2,1,0:T(8,128)(2,1)S(1)}, bf16[2,96,256]{2,1,0:T(8,128)(2,1)S(1)}, u32[]{:S(2)}, u32[]{:S(2)}) collective-permute-start(bf16[2,96,256]{2,1,0:T(8,128)(2,1)S(1)} %get-tuple-element.39), channel_id=1, source_target_pairs={{0,64},{32,96},{64,0},{96,32},{1,65},{33,97},{65,1},{97,33},{2,66}... | collective-permute-start | bytes 294920 | tf_op jit(solution)/shard_map/ppermute | solution.py:306
  17.9 112.7 %collective-permute-start.2 = (bf16[2,96,256]{2,1,0:T(8,128)(2,1)S(1)}, bf16[2,96,256]{2,1,0:T(8,128)(2,1)S(1)}, u32[]{:S(2)}, u32[]{:S(2)}) collective-permute-start(bf16[2,96,256]{2,1,0:T(8,128)(2,1)S(1)} %get-tuple-element.40), channel_id=1, source_target_pairs={{0,96},{32,0},{64,32},{96,64},{1,97},{33,1},{65,33},{97,65},{2,98}... | collective-permute-start | bytes 294920 | tf_op jit(solution)/shard_map/ppermute | solution.py:306
  20.4 110.2 %collective-permute-start.6 = (bf16[4,2,96,256]{3,2,1,0:T(8,128)(2,1)S(1)}, bf16[4,2,96,256]{3,2,1,0:T(8,128)(2,1)S(1)}, u32[]{:S(2)}, u32[]{:S(2)}) collective-permute-start(bf16[4,2,96,256]{3,2,1,0:T(8,128)(2,1)S(1)} %shard_map.75), channel_id=1, source_target_pairs={{0,16},{16,0},{1,17},{17,1},{2,18},{18,2},{3,19},{19,3},{4,20},{20... | collective-permute-start | bytes 1179656 | tf_op jit(solution)/shard_map/ppermute | solution.py:306
  125.3 69.8 %all-to-all-start.1 = ((bf16[16,32,256]{2,1,0:T(8,128)(2,1)}), bf16[16,32,256]{2,1,0:T(8,128)(2,1)S(1)}, u32[]{:S(2)}, u32[]{:S(2)}) async-start(bf16[16,32,256]{2,1,0:T(8,128)(2,1)} %shard_map.74), calls=%async_computation.1 | async-start | bytes 524288 | tf_op jit(solution)/shard_map/all_to_all | solution.py:322
  181.0 14.1 %copy-start = (bf16[32,32,256]{2,1,0:T(8,128)(2,1)S(1)}, bf16[32,32,256]{2,1,0:T(8,128)(2,1)}, u32[]{:S(2)}) copy-start(bf16[32,32,256]{2,1,0:T(8,128)(2,1)} %refs_1_.1) | copy-start | bytes 1572868
  181.0 6.7 %collective-permute-start.7 = (bf16[4,2,32,256]{3,2,1,0:T(8,128)(2,1)S(1)}, bf16[4,2,32,256]{3,2,1,0:T(8,128)(2,1)S(1)}, u32[]{:S(2)}, u32[]{:S(2)}) collective-permute-start(bf16[4,2,32,256]{3,2,1,0:T(8,128)(2,1)S(1)} %get-tuple-element.46), channel_id=1, source_target_pairs={{0,16},{16,0},{1,17},{17,1},{2,18},{18,2},{3,19},{19,3},{4,20},{20... | collective-permute-start | bytes 393224 | tf_op jit(solution)/shard_map/ppermute | solution.py:306
  187.7 7.4 %copy-start.1 = (bf16[2,256,256]{2,1,0:T(8,128)(2,1)S(1)}, bf16[2,256,256]{2,1,0:T(8,128)(2,1)}, u32[]{:S(2)}) copy-start(bf16[2,256,256]{2,1,0:T(8,128)(2,1)} %refs_7_.3) | copy-start | bytes 786436
  187.7 4.4 %collective-permute-start.10 = (bf16[2,2,32,256]{3,2,1,0:T(8,128)(2,1)S(1)}, bf16[2,2,32,256]{3,2,1,0:T(8,128)(2,1)S(1)}, u32[]{:S(2)}, u32[]{:S(2)}) collective-permute-start(bf16[2,2,32,256]{3,2,1,0:T(8,128)(2,1)S(1)} %get-tuple-element.50), channel_id=1, source_target_pairs={{0,32},{32,64},{64,96},{96,0},{1,33},{33,65},{65,97},{97,1},{2,34}... | collective-permute-start | bytes 196616 | tf_op jit(solution)/shard_map/ppermute | solution.py:306
  188.4 6.7 %copy-start.3 = (f32[2,256]{1,0:T(2,128)S(1)}, f32[2,256]{1,0:T(2,128)}, u32[]{:S(2)}) copy-start(f32[2,256]{1,0:T(2,128)} %refs_8_.3) | copy-start | bytes 6148
  188.4 6.8 %copy-start.2 = (f32[2,256]{1,0:T(2,128)S(1)}, f32[2,256]{1,0:T(2,128)}, u32[]{:S(2)}) copy-start(f32[2,256]{1,0:T(2,128)} %refs_11_.1) | copy-start | bytes 6148
  188.4 3.8 collective-permute-start.8
  190.5 4.6 %collective-permute-start.9 = (bf16[2,2,32,256]{3,2,1,0:T(8,128)(2,1)S(1)}, bf16[2,2,32,256]{3,2,1,0:T(8,128)(2,1)S(1)}, u32[]{:S(2)}, u32[]{:S(2)}) collective-permute-start(bf16[2,2,32,256]{3,2,1,0:T(8,128)(2,1)S(1)} %get-tuple-element.49), channel_id=1, source_target_pairs={{0,64},{32,96},{64,0},{96,32},{1,65},{33,97},{65,1},{97,33},{2,66}... | collective-permute-start | bytes 196616 | tf_op jit(solution)/shard_map/ppermute | solution.py:306
  200.5 20.6 %all-to-all-start.2 = ((bf16[16,96,256]{2,1,0:T(8,128)(2,1)}), bf16[16,96,256]{2,1,0:T(8,128)(2,1)S(1)}, u32[]{:S(2)}, u32[]{:S(2)}) async-start(bf16[16,96,256]{2,1,0:T(8,128)(2,1)} %get-tuple-element.52), calls=%async_computation.2 | async-start | bytes 1572864 | tf_op jit(solution)/shard_map/all_to_all | solution.py:314
  208.5 7.6 %collective-permute-start.14 = (bf16[2,96,256]{2,1,0:T(8,128)(2,1)S(1)}, bf16[2,96,256]{2,1,0:T(8,128)(2,1)S(1)}, u32[]{:S(2)}, u32[]{:S(2)}) collective-permute-start(bf16[2,96,256]{2,1,0:T(8,128)(2,1)S(1)} %get-tuple-element.58), channel_id=1, source_target_pairs={{0,32},{32,64},{64,96},{96,0},{1,33},{33,65},{65,97},{97,1},{2,34}... | collective-permute-start | bytes 294920 | tf_op jit(solution)/shard_map/ppermute | solution.py:306
  208.5 7.6 %collective-permute-start.15 = (bf16[2,96,256]{2,1,0:T(8,128)(2,1)S(1)}, bf16[2,96,256]{2,1,0:T(8,128)(2,1)S(1)}, u32[]{:S(2)}, u32[]{:S(2)}) collective-permute-start(bf16[2,96,256]{2,1,0:T(8,128)(2,1)S(1)} %get-tuple-element.59), channel_id=1, source_target_pairs={{0,64},{32,96},{64,0},{96,32},{1,65},{33,97},{65,1},{97,33},{2,66}... | collective-permute-start | bytes 294920 | tf_op jit(solution)/shard_map/ppermute | solution.py:306
  210.1 6.2 %collective-permute-start.16 = (bf16[2,96,256]{2,1,0:T(8,128)(2,1)S(1)}, bf16[2,96,256]{2,1,0:T(8,128)(2,1)S(1)}, u32[]{:S(2)}, u32[]{:S(2)}) collective-permute-start(bf16[2,96,256]{2,1,0:T(8,128)(2,1)S(1)} %get-tuple-element.60), channel_id=1, source_target_pairs={{0,96},{32,0},{64,32},{96,64},{1,97},{33,1},{65,33},{97,65},{2,98}... | collective-permute-start | bytes 294920 | tf_op jit(solution)/shard_map/ppermute | solution.py:306
  212.0 114.2 %collective-permute-start.11 = (bf16[2,96,256]{2,1,0:T(8,128)(2,1)S(1)}, bf16[2,96,256]{2,1,0:T(8,128)(2,1)S(1)}, u32[]{:S(2)}, u32[]{:S(2)}) collective-permute-start(bf16[2,96,256]{2,1,0:T(8,128)(2,1)S(1)} %get-tuple-element.54), channel_id=1, source_target_pairs={{0,32},{32,64},{64,96},{96,0},{1,33},{33,65},{65,97},{97,1},{2,34}... | collective-permute-start | bytes 294920 | tf_op jit(solution)/shard_map/ppermute | solution.py:306
  212.0 114.2 %collective-permute-start.12 = (bf16[2,96,256]{2,1,0:T(8,128)(2,1)S(1)}, bf16[2,96,256]{2,1,0:T(8,128)(2,1)S(1)}, u32[]{:S(2)}, u32[]{:S(2)}) collective-permute-start(bf16[2,96,256]{2,1,0:T(8,128)(2,1)S(1)} %get-tuple-element.55), channel_id=1, source_target_pairs={{0,64},{32,96},{64,0},{96,32},{1,65},{33,97},{65,1},{97,33},{2,66}... | collective-permute-start | bytes 294920 | tf_op jit(solution)/shard_map/ppermute | solution.py:306
  216.1 110.1 %collective-permute-start.13 = (bf16[2,96,256]{2,1,0:T(8,128)(2,1)S(1)}, bf16[2,96,256]{2,1,0:T(8,128)(2,1)S(1)}, u32[]{:S(2)}, u32[]{:S(2)}) collective-permute-start(bf16[2,96,256]{2,1,0:T(8,128)(2,1)S(1)} %get-tuple-element.56), channel_id=1, source_target_pairs={{0,96},{32,0},{64,32},{96,64},{1,97},{33,1},{65,33},{97,65},{2,98}... | collective-permute-start | bytes 294920 | tf_op jit(solution)/shard_map/ppermute | solution.py:306
  216.3 109.9 %collective-permute-start.17 = (bf16[4,2,96,256]{3,2,1,0:T(8,128)(2,1)S(1)}, bf16[4,2,96,256]{3,2,1,0:T(8,128)(2,1)S(1)}, u32[]{:S(2)}, u32[]{:S(2)}) collective-permute-start(bf16[4,2,96,256]{3,2,1,0:T(8,128)(2,1)S(1)} %shard_map.80), channel_id=1, source_target_pairs={{0,16},{16,0},{1,17},{17,1},{2,18},{18,2},{3,19},{19,3},{4,20},{20... | collective-permute-start | bytes 1179656 | tf_op jit(solution)/shard_map/ppermute | solution.py:306
  321.6 69.8 %all-to-all-start.3 = ((bf16[16,32,256]{2,1,0:T(8,128)(2,1)}), bf16[16,32,256]{2,1,0:T(8,128)(2,1)S(1)}, u32[]{:S(2)}, u32[]{:S(2)}) async-start(bf16[16,32,256]{2,1,0:T(8,128)(2,1)} %shard_map.79), calls=%async_computation.3 | async-start | bytes 524288 | tf_op jit(solution)/shard_map/all_to_all | solution.py:322
  376.9 14.6 %copy-start.4 = (bf16[32,32,256]{2,1,0:T(8,128)(2,1)S(1)}, bf16[32,32,256]{2,1,0:T(8,128)(2,1)}, u32[]{:S(2)}) copy-start(bf16[32,32,256]{2,1,0:T(8,128)(2,1)} %get-tuple-element.51.refs_1_) | copy-start | bytes 1572868
  376.9 6.4 %collective-permute-start.18 = (bf16[4,2,32,256]{3,2,1,0:T(8,128)(2,1)S(1)}, bf16[4,2,32,256]{3,2,1,0:T(8,128)(2,1)S(1)}, u32[]{:S(2)}, u32[]{:S(2)}) collective-permute-start(bf16[4,2,32,256]{3,2,1,0:T(8,128)(2,1)S(1)} %get-tuple-element.62), channel_id=1, source_target_pairs={{0,16},{16,0},{1,17},{17,1},{2,18},{18,2},{3,19},{19,3},{4,20},{20... | collective-permute-start | bytes 393224 | tf_op jit(solution)/shard_map/ppermute | solution.py:306
  383.3 4.2 %collective-permute-start.19 = (bf16[2,2,32,256]{3,2,1,0:T(8,128)(2,1)S(1)}, bf16[2,2,32,256]{3,2,1,0:T(8,128)(2,1)S(1)}, u32[]{:S(2)}, u32[]{:S(2)}) collective-permute-start(bf16[2,2,32,256]{3,2,1,0:T(8,128)(2,1)S(1)} %get-tuple-element.64), channel_id=1, source_target_pairs={{0,96},{32,0},{64,32},{96,64},{1,97},{33,1},{65,33},{97,65},{2,98}... | collective-permute-start | bytes 196616 | tf_op jit(solution)/shard_map/ppermute | solution.py:306
  386.1 4.7 %collective-permute-start.20 = (bf16[2,2,32,256]{3,2,1,0:T(8,128)(2,1)S(1)}, bf16[2,2,32,256]{3,2,1,0:T(8,128)(2,1)S(1)}, u32[]{:S(2)}, u32[]{:S(2)}) collective-permute-start(bf16[2,2,32,256]{3,2,1,0:T(8,128)(2,1)S(1)} %get-tuple-element.65), channel_id=1, source_target_pairs={{0,64},{32,96},{64,0},{96,32},{1,65},{33,97},{65,1},{97,33},{2,66}... | collective-permute-start | bytes 196616 | tf_op jit(solution)/shard_map/ppermute | solution.py:306
  386.7 4.8 %collective-permute-start.21 = (bf16[2,2,32,256]{3,2,1,0:T(8,128)(2,1)S(1)}, bf16[2,2,32,256]{3,2,1,0:T(8,128)(2,1)S(1)}, u32[]{:S(2)}, u32[]{:S(2)}) collective-permute-start(bf16[2,2,32,256]{3,2,1,0:T(8,128)(2,1)S(1)} %get-tuple-element.66), channel_id=1, source_target_pairs={{0,32},{32,64},{64,96},{96,0},{1,33},{33,65},{65,97},{97,1},{2,34}... | collective-permute-start | bytes 196616 | tf_op jit(solution)/shard_map/ppermute | solution.py:306
